TPU v7x, 8 devices: a whole 2x2x1 slice. The times are simulated.
8 devices in a mesh: rep: 1 (over z), data: 2 (over y), expert: 4 (over x, core).
Axes of the slice: x: 2, y: 2, z: 1, core: 2. Of those that a mesh axis runs over, the one named last changes fastest.
Arguments:
- x: bfloat16 [32768, 2048], P(('rep', 'expert', 'data'))
- expert_idx: int32 [32768, 2], P(('rep', 'expert', 'data'))
- gate: float32 [32768, 2], P(('rep', 'expert', 'data'))
- w_gate: bfloat16 [8, 2048, 5632], P('expert', 'data')
- w_up: bfloat16 [8, 2048, 5632], P('expert', 'data')
- w_down: bfloat16 [8, 5632, 2048], P('expert', None, 'data')
Outputs:
- output: bfloat16 [32768, 2048], P(('rep', 'expert', 'data'))
All inputs are finite; a program needn't handle non-finite values.
Results may differ from a plain program's by a relative error of at most 0.001.
Values are sent between devices in bfloat16 or wider.
A program may use at most 1 GiB of HBM per device.

v0:
```python
import jax
import jax.numpy as jnp
from jax import lax
from jax.sharding import PartitionSpec as P


def capacity_rows(tok_rows, top_k, n_exp):
    return max(8, ((5 * top_k * tok_rows) // (4 * n_exp) + 7) // 8 * 8)


def slot_table(ids_flat, n_exp, n_group, capacity):
    n_local = n_exp // n_group
    one_hot = (ids_flat[:, None] == jnp.arange(n_exp, dtype=jnp.int32)[None, :]).astype(jnp.int32)
    slot_ids = jnp.sum((jnp.cumsum(one_hot, axis=0) - one_hot) * one_hot, axis=1)
    row_base = (ids_flat % n_local) * (n_group * capacity) + (ids_flat // n_local) * capacity
    return jnp.where(slot_ids < capacity, row_base + slot_ids, n_exp * capacity)


def dispatch_rows(x_loc, dest_row, n_slots, top_k):
    tok_rows = x_loc.shape[0]
    pair_token = jnp.arange(dest_row.shape[0], dtype=jnp.int32) // top_k
    src_tok = jnp.full((n_slots,), tok_rows, jnp.int32).at[dest_row].set(pair_token, mode="drop")
    return jnp.take(x_loc, src_tok, axis=0, mode="fill", fill_value=0)


def combine_rows(x_loc, gate_loc, back_rows, dest_row):
    tok_rows, d_model = x_loc.shape
    pair_out = jnp.take(back_rows, dest_row, axis=0, mode="fill", fill_value=0)
    mixed = jnp.sum(pair_out.reshape(tok_rows, gate_loc.shape[1], d_model) * gate_loc[:, :, None], axis=1)
    return (x_loc.astype(jnp.float32) + mixed).astype(jnp.bfloat16)


def expert_ffn(expert_rows, w_gate, w_up, w_down):
    gate_act = jnp.einsum("erd,edf->erf", expert_rows, w_gate, preferred_element_type=jnp.float32)
    up_act = jnp.einsum("erd,edf->erf", expert_rows, w_up, preferred_element_type=jnp.float32)
    hidden = (jax.nn.silu(gate_act) * up_act).astype(jnp.bfloat16)
    return jnp.einsum("erf,efd->erd", hidden, w_down, preferred_element_type=jnp.float32).astype(jnp.bfloat16)


def solution(mesh):
    n_group = mesh.shape["expert"]
    tok_spec = P(("rep", "expert", "data"), None)
    wide_spec = P("expert", "data", None)
    down_spec = P("expert", None, "data")

    def device_step(x_loc, idx_loc, gate_loc, wg_loc, wu_loc, wd_loc):
        tok_rows, d_model = x_loc.shape
        top_k = idx_loc.shape[1]
        n_local = wg_loc.shape[0]
        n_exp = n_local * n_group
        capacity = capacity_rows(tok_rows, top_k, n_exp)
        dest_row = slot_table(idx_loc.reshape(tok_rows * top_k), n_exp, n_group, capacity)
        send_rows = dispatch_rows(x_loc, dest_row, n_exp * capacity, top_k).reshape(n_local, n_group, capacity, d_model)
        recv_rows = lax.all_to_all(send_rows, "expert", 1, 1, tiled=True)
        wg_full = lax.all_gather(wg_loc, "data", axis=1, tiled=True)
        wu_full = lax.all_gather(wu_loc, "data", axis=1, tiled=True)
        wd_full = lax.all_gather(wd_loc, "data", axis=2, tiled=True)
        out_rows = expert_ffn(recv_rows.reshape(n_local, n_group * capacity, d_model), wg_full, wu_full, wd_full)
        back_rows = lax.all_to_all(out_rows.reshape(n_local, n_group, capacity, d_model), "expert", 1, 1, tiled=True)
        return combine_rows(x_loc, gate_loc, back_rows.reshape(n_exp * capacity, d_model), dest_row)

    return jax.shard_map(device_step, mesh=mesh, in_specs=(tok_spec, tok_spec, tok_spec, wide_spec, wide_spec, down_spec), out_specs=tok_spec, check_vma=False)
```

profile of v0, /device:TPU:0, one launch (start us, length us, event | category | flops | bytes accessed | tf_op | source)
XLA Modules:
  0.0 2845.7 jit_solution(11079668015599125400)
XLA Ops:
  6.5 0.0 all-gather.4.cloned.1.call-start
  6.5 0.7 all-gather.4.cloned.1.call-update
  7.3 0.0 all-gather.6.cloned.1.call-start
  7.3 0.7 all-gather.6.cloned.1.call-update
  8.0 0.0 copy-done.5
  8.0 0.6 copy.35
  8.7 1.2 eq.31
  9.9 1.2 eq.27
  11.1 1.4 reshape.183
  12.6 2.4 reduce-window.6
  15.0 0.3 slice_reduce_fusion
  15.3 0.2 reduce-window.9
  15.5 0.1 add_bitcast_fusion
  15.7 0.2 fusion.15
  15.9 0.0 copy-start.3
  15.9 0.3 compare_select_fusion.1
  16.2 0.3 copy-done.3
  16.5 30.5 %scatter_custom_fusion = s32[10240]{0:T(1024)S(1)} fusion(s32[8192]{0:T(1024)S(1)} %bitcast.44, s32[8192]{0:T(1024)S(1)} %add_select_fusion.2, s32[]{:T(128)} %constant.79.clone.1), kind=kCustom, calls=%fused_computation.57 | custom fusion | bytes 40964 | tf_op jit(solution)/shard_map/scatter | solution.py:22
  47.1 85.9 %gather_fusion = bf16[10240,2048]{1,0:T(8,128)(2,1)} fusion(bf16[4096,2048]{1,0:T(8,128)(2,1)} %param.6, s32[10240]{0:T(1024)S(1)} %fusion.17), kind=kCustom, calls=%fused_computation | custom fusion | bytes 83927040 | tf_op jit(solution)/shard_map/jit(_take)/gather | solution.py:23
  133.0 28.2 copy_select_fusion
  161.2 11.2 all-to-all-start
  172.4 0.5 all-gather.8.cloned.1.call-start
  172.9 0.2 all-gather.8.cloned.1.call-update
  173.1 452.8 %all-to-all-done = bf16[2,4,1280,2048]{3,2,0,1:T(8,128)(2,1)} async-done(((bf16[2,4,1280,2048]{3,2,0,1:T(8,128)(2,1)}), bf16[2,4,1280,2048]{3,2,0,1:T(8,128)(2,1)}, u32[]{:S(2)}, u32[]{:S(2)}) %all-to-all-start) | async-done | bytes 41943072 | tf_op jit(solution)/shard_map/all_to_all | solution.py:54
  625.9 28.1 copy.47
  654.0 251.3 %fusion.27 = f32[2,5120,5632]{2,1,0:T(8,128)} fusion(bf16[2,5120,2048]{2,1,0:T(8,128)(2,1)} %bitcast.40, bf16[2,2048,5632]{2,1,0:T(8,128)(2,1)} %all-gather.4.cloned.1.call-done), kind=kOutput, calls=%fused_computation.62 | convolution fusion | flops 236223201280 | bytes 318767104 | tf_op jit(solution)/shard_map/erd,edf->erf/dot_general | solution.py:34
  905.3 164.9 %all-gather.6.cloned.1.call-done = bf16[2,2048,5632]{2,1,0:T(8,128)(2,1)} async-done(((bf16[2,1024,5632]{2,1,0:T(8,128)(2,1)}), bf16[2,2048,5632]{2,1,0:T(8,128)(2,1)}) %all-gather.6.cloned.1.call-update) | async-done | bytes 46137360 | tf_op jit(solution)/shard_map/all_gather | solution.py:56
  1070.1 264.2 %multiply_convert_fusion.6 = bf16[2,5120,5632]{2,1,0:T(8,128)(2,1)} fusion(f32[2,5120,5632]{2,1,0:T(8,128)} %fusion.27, bf16[2,5120,2048]{2,1,0:T(8,128)(2,1)} %bitcast.41, bf16[2,2048,5632]{2,1,0:T(8,128)(2,1)} %all-gather.6.cloned.1.call-done), kind=kOutput, calls=%fused_computation.3.clone.clone.clone.clone.1 | convolution fusion | flops 236569231360 | bytes 434110464 | tf_op jit(solution)/shard_map/erd,edf->erf/dot_general | solution.py:35
  1334.3 266.5 %all-gather.8.cloned.1.call-done = bf16[2,5632,2048]{2,1,0:T(8,128)(2,1)} async-done(((bf16[2,5632,1024]{2,1,0:T(8,128)(2,1)}), bf16[2,5632,2048]{2,1,0:T(8,128)(2,1)}) %all-gather.8.cloned.1.call-update) | async-done | bytes 46137360 | tf_op jit(solution)/shard_map/all_gather | solution.py:57
  1600.8 250.1 %fusion.1 = bf16[2,5120,2048]{2,1,0:T(8,128)(2,1)} fusion(bf16[2,5632,2048]{2,1,0:T(8,128)(2,1)} %all-gather.8.cloned.1.call-done, bf16[2,5120,5632]{2,1,0:T(8,128)(2,1)} %multiply_convert_fusion.6), kind=kOutput, calls=%fused_computation.9 | convolution fusion | flops 236244172800 | bytes 203423744 | tf_op jit(solution)/shard_map/erf,efd->erd/dot_general | solution.py:37
  1850.9 28.1 copy.48
  1879.0 0.0 copy-start.9
  1879.0 0.0 copy-start.8
  1879.0 0.0 copy-start.1
  1879.0 11.6 all-to-all-start.1
  1890.6 3.4 reduce_sum.23
  1894.0 0.0 copy-done.6
  1894.1 0.8 copy.41
  1894.9 2.0 copy.50
  1896.9 0.0 copy-done.1
  1896.9 4.2 compare_and_fusion
  1901.1 442.2 %all-to-all-done.1 = bf16[2,4,1280,2048]{3,2,0,1:T(8,128)(2,1)} async-done(((bf16[2,4,1280,2048]{3,2,0,1:T(8,128)(2,1)}), bf16[2,4,1280,2048]{3,2,0,1:T(8,128)(2,1)}, u32[]{:S(2)}, u32[]{:S(2)}) %all-to-all-start.1) | async-done | bytes 41943072 | tf_op jit(solution)/shard_map/all_to_all | solution.py:59
  2343.3 28.1 copy.49
  2371.3 240.4 %gather_fusion.1 = bf16[8192,2048]{1,0:T(8,128)(2,1)} fusion(bf16[10240,2048]{1,0:T(8,128)(2,1)} %bitcast.38, s32[8192]{0:T(1024)S(1)} %broadcast_clamp_fusion), kind=kCustom, calls=%fused_computation.1 | custom fusion | bytes 67141632 | tf_op jit(solution)/shard_map/jit(_take)/gather | solution.py:28
  2611.7 53.1 %gather.15 = bf16[4096,2,2048]{2,1,0:T(2,128)(2,1)} reshape(bf16[8192,2048]{1,0:T(8,128)(2,1)} %gather_fusion.1) | data formatting | bytes 67108864 | tf_op jit(solution)/shard_map/jit(_take)/gather | solution.py:28
  2664.8 0.0 copy-done.2
  2664.8 151.9 %multiply_reduce_fusion = f32[4096,2048]{1,0:T(8,128)} fusion(bf16[4096,2,2048]{2,1,0:T(2,128)(2,1)} %gather.15, pred[4096,2]{1,0:T(8,128)(4,1)S(1)} %compare_and_fusion, f32[4096,2]{1,0:T(8,128)S(1)} %copy-done.2), kind=kLoop, calls=%fused_computation.5 | loop fusion | flops 58720256 | bytes 67149824 | tf_op jit(solution)/shard_map/reduce_sum | solution.py:29
  2816.7 22.3 add_convert_fusion
  (20 shorter events, 0.1 us)
Async XLA Ops:
  6.5 1.5 copy-start.5
  6.5 647.4 %all-gather.4.cloned.1.call-start = ((), (), s32[]{:S(2)}) async-start(), calls=%async_computation.2 | async-start | bytes 69206016 | tf_op jit(solution)/shard_map/all_gather | solution.py:55
  7.3 1062.9 %all-gather.6.cloned.1.call-start = ((), (), s32[]{:S(2)}) async-start(), calls=%async_computation.3 | async-start | bytes 69206016 | tf_op jit(solution)/shard_map/all_gather | solution.py:56
  8.7 124.3 %copy-start = (s32[4096,2]{1,0:T(8,128)}, s32[4096,2]{1,0:T(8,128)S(1)}, u32[]{:S(2)}) copy-start(s32[4096,2]{1,0:T(8,128)S(1)} %copy.35) | copy-start | bytes 98308
  15.9 0.6 copy-start.3
  16.5 30.5 %copy-start.7 = (s32[8192,1]{0,1:T(1,128)}, s32[8192,1]{0,1:T(1,128)S(1)}, u32[]{:S(2)}) copy-start(s32[8192,1]{0,1:T(1,128)S(1)} %compare_select_fusion.1) | copy-start | bytes 98308
  161.2 464.7 %all-to-all-start = ((bf16[2,4,1280,2048]{3,2,0,1:T(8,128)(2,1)}), bf16[2,4,1280,2048]{3,2,0,1:T(8,128)(2,1)}, u32[]{:S(2)}, u32[]{:S(2)}) async-start(bf16[2,4,1280,2048]{3,2,0,1:T(8,128)(2,1)} %copy_select_fusion), calls=%async_computation | async-start | bytes 83886080 | tf_op jit(solution)/shard_map/all_to_all | solution.py:54
  172.4 1428.4 %all-gather.8.cloned.1.call-start = ((), (), s32[]{:S(2)}) async-start(), calls=%async_computation.4 | async-start | bytes 69206016 | tf_op jit(solution)/shard_map/all_gather | solution.py:57
  1879.0 11.6 copy-start.4
  1879.0 15.0 copy-start.6
  1879.0 15.9 copy-start.9
  1879.0 17.9 copy-start.8
  1879.0 17.9 copy-start.1
  1879.0 464.2 %all-to-all-start.1 = ((bf16[2,4,1280,2048]{3,2,0,1:T(8,128)(2,1)}), bf16[2,4,1280,2048]{3,2,0,1:T(8,128)(2,1)}, u32[]{:S(2)}, u32[]{:S(2)}) async-start(bf16[2,4,1280,2048]{3,2,0,1:T(8,128)(2,1)} %copy.48), calls=%async_computation.1 | async-start | bytes 83886080 | tf_op jit(solution)/shard_map/all_to_all | solution.py:59
  2611.7 53.1 %copy-start.2 = (f32[4096,2]{1,0:T(8,128)S(1)}, f32[4096,2]{1,0:T(8,128)}, u32[]{:S(2)}) copy-start(f32[4096,2]{1,0:T(8,128)} %copy.50) | copy-start | bytes 98308
Sparse Core Ops, SparseCore 0:
  8.9 531.2 all-gather.3
  541.7 528.4 all-gather.5
  1071.7 529.1 all-gather.7
where the time goes:
time: 2860 us; the launch traced here: 2850 us
  waiting for transfers between devices  1330 us (47%)
  matrix products  766 us (27%)
  local copies, waits for them, and re-layouts  505 us (18%)
  other arithmetic  210 us (7%)
    all_to_all x1, waiting for transfers between devices, device_step(): recv_rows = lax.all_to_all(send_rows, 'expert', 1, 1, tiled=True)  453 us
    all_to_all x1, waiting for transfers between devices, device_step(): lax.all_to_all(out_rows.reshape(n_local, n_group, capacity, d_model), 'ex...  442 us
    gather x2, local copies, waits for them, and re-layouts, combine_rows(): pair_out = jnp.take(back_rows, dest_row, axis=0, mode='fill', fill_value=0)  293 us
    all_gather x1, waiting for transfers between devices, device_step(): wd_full = lax.all_gather(wd_loc, 'data', axis=2, tiled=True)  266 us
    dot_general x1, matrix products, expert_ffn(): jnp.einsum('erd,edf->erf', expert_rows, w_up, preferred_element_type=jnp....  264 us
    dot_general x1, matrix products, expert_ffn(): jnp.einsum('erd,edf->erf', expert_rows, w_gate, preferred_element_type=jn...  251 us
    dot_general x1, matrix products, expert_ffn(): jnp.einsum('erf,efd->erd', hidden, w_down, preferred_element_type=jnp.flo...  250 us
    all_gather x1, waiting for transfers between devices, device_step(): wu_full = lax.all_gather(wu_loc, 'data', axis=1, tiled=True)  165 us
  transfers between devices with their start and end apart: 5, of which 4 were waited for; matrix products, arithmetic and copies ran while one was open for 25% of the time, Pallas kernels for 0%

commit v1 on v0

v1 whole, which is shorter than its diff:
```python
import functools

import jax
import jax.numpy as jnp
from jax import lax
from jax.experimental import pallas as pl
from jax.experimental.pallas import tpu as pltpu
from jax.sharding import PartitionSpec as P


BF16 = jnp.bfloat16
F32 = jnp.float32
I32 = jnp.int32
VMEM_LIMIT = 66_000_000

TILE = 256
TOK_BLOCK = 256
MIX_TILE = 128
ALIGN = 16
SLAB = MIX_TILE + ALIGN
SUB = 512
WIDE_CHUNKS = (1024, 1536, 1536, 1536)
DOWN_PIECES = (512, 256, 256)


def capacity_rows(tok_rows, top_k, n_exp):
    return max(8, ((5 * top_k * tok_rows) // (4 * n_exp) + 7) // 8 * 8)


def after(value, *earlier):
    return lax.optimization_barrier((value, earlier))[0]


def any_spec():
    return pl.BlockSpec(memory_space=pl.ANY)


def pack_body(n_local, local, n_blk, n_group, first_ref, slot_ref, x_ref, *refs):
    out_refs, acc_ref = refs[:n_group], refs[n_group]
    e, s = pl.program_id(0) * n_local + local, pl.program_id(1)
    count = first_ref[e * (n_blk + 1) + n_blk]
    base = s * TILE

    @pl.when(base < count)
    def _():
        end = jnp.minimum(base + TILE, count)
        lo = jnp.int32(0)
        hi = jnp.int32(0)
        for i in range(n_blk):
            lo += (first_ref[e * (n_blk + 1) + i + 1] <= base).astype(I32)
            hi += (first_ref[e * (n_blk + 1) + i] < end).astype(I32)
        acc_ref[...] = jnp.zeros_like(acc_ref)
        slots = base + lax.broadcasted_iota(I32, (TILE, TOK_BLOCK), 0)

        def visit(i, carry):
            off = pl.multiple_of(i * TOK_BLOCK, TOK_BLOCK)
            pick = (slots == slot_ref[pl.ds(e, 1), pl.ds(off, TOK_BLOCK)]).astype(F32).astype(BF16)
            acc_ref[...] += jnp.dot(pick, x_ref[pl.ds(off, TOK_BLOCK), :], preferred_element_type=F32)
            return carry

        lax.fori_loop(lo, hi, visit, 0)
        for d in range(n_group):

            @pl.when(pl.program_id(0) == d)
            def _():
                out_refs[d][...] = acc_ref[...].astype(BF16)


def pack_rows(first_blk, x_loc, slot_te, n_exp, n_local, local, capacity):
    tok_rows, d_model = x_loc.shape
    n_blk = tok_rows // TOK_BLOCK
    n_group = n_exp // n_local

    def out_spec(d):
        def index(p, s, first):
            used = (first[(d * n_local + local) * (n_blk + 1) + n_blk] + TILE - 1) // TILE
            last = jnp.maximum(used - 1, 0)
            return jnp.where(p < d, 0, jnp.where(p > d, last, jnp.minimum(s, last))), 0

        return pl.BlockSpec((TILE, d_model), index)

    return pl.pallas_call(
        functools.partial(pack_body, n_local, local, n_blk, n_group),
        grid_spec=pltpu.PrefetchScalarGridSpec(
            num_scalar_prefetch=1,
            grid=(n_group, capacity // TILE),
            in_specs=[
                pl.BlockSpec((n_exp, tok_rows), lambda p, s, f: (0, 0)),
                pl.BlockSpec((tok_rows, d_model), lambda p, s, f: (0, 0)),
            ],
            out_specs=[out_spec(d) for d in range(n_group)],
            scratch_shapes=[pltpu.VMEM((TILE, d_model), F32)],
        ),
        out_shape=[jax.ShapeDtypeStruct((capacity, d_model), BF16)] * n_group,
        compiler_params=pltpu.CompilerParams(vmem_limit_bytes=VMEM_LIMIT),
        cost_estimate=pl.CostEstimate(flops=20_000_000_000, bytes_accessed=60_000_000, transcendentals=0),
        name="pack_rows",
    )(first_blk, slot_te, x_loc)


def wide_body(n_group, local, lo_col, cols, meta_ref, *refs):
    x_refs = refs[:n_group]
    wg_ref, wu_ref, far_ref, h_ref, rows_buf, gate_w, up_w, row_sems, sems = refs[n_group:]
    side = meta_ref[0]
    half = wg_ref.shape[1]
    i = pl.program_id(0)
    n_live = meta_ref[1 + n_group]

    def fetch(step):
        for d in range(n_group):

            @pl.when((step >= meta_ref[1 + d]) & (step < meta_ref[2 + d]))
            def _():
                at = pl.multiple_of((step - meta_ref[1 + d]) * TILE, TILE)
                pltpu.make_async_copy(x_refs[d].at[pl.ds(at, TILE), :], rows_buf.at[step % 2], row_sems.at[step % 2]).start()

    @pl.when(i == 0)
    def _():
        fetch(i)
        near = pl.ds(pl.multiple_of(side * half, half), half)
        far = pl.ds(pl.multiple_of((1 - side) * half, half), half)
        copies = [
            pltpu.make_async_copy(wg_ref.at[local, :, pl.ds(lo_col, cols)], gate_w.at[near, :], sems.at[0]),
            pltpu.make_async_copy(wu_ref.at[local, :, pl.ds(lo_col, cols)], up_w.at[near, :], sems.at[1]),
            pltpu.make_async_copy(far_ref.at[0], gate_w.at[far, :], sems.at[2]),
            pltpu.make_async_copy(far_ref.at[1], up_w.at[far, :], sems.at[3]),
        ]
        for copy in copies:
            copy.start()
        for copy in copies:
            copy.wait()

    @pl.when(i < n_live)
    def _():
        fetch(i + 1)
        pltpu.make_async_copy(x_refs[0].at[pl.ds(0, TILE), :], rows_buf.at[i % 2], row_sems.at[i % 2]).wait()
        rows = rows_buf[i % 2]
        for j in range(0, cols, SUB):
            g = jnp.dot(rows, gate_w[:, j : j + SUB], preferred_element_type=F32)
            u = jnp.dot(rows, up_w[:, j : j + SUB], preferred_element_type=F32)
            h_ref[:, j : j + SUB] = (jax.nn.silu(g) * u).astype(BF16)


def wide_part(meta, rows, w_gate, w_up, far, local, lo_col, cols):
    n_group = len(rows)
    capacity, d_model = rows[0].shape
    n_rows = n_group * capacity
    return pl.pallas_call(
        functools.partial(wide_body, n_group, local, lo_col, cols),
        grid_spec=pltpu.PrefetchScalarGridSpec(
            num_scalar_prefetch=1,
            grid=(n_rows // TILE,),
            in_specs=[any_spec()] * (n_group + 3),
            out_specs=pl.BlockSpec((TILE, cols), lambda i, m: (jnp.clip(i, 0, jnp.maximum(m[1 + n_group] - 1, 0)), 0)),
            scratch_shapes=[
                pltpu.VMEM((2, TILE, d_model), BF16),
                pltpu.VMEM((d_model, cols), BF16),
                pltpu.VMEM((d_model, cols), BF16),
                pltpu.SemaphoreType.DMA((2,)),
                pltpu.SemaphoreType.DMA((4,)),
            ],
        ),
        out_shape=jax.ShapeDtypeStruct((n_rows, cols), BF16),
        compiler_params=pltpu.CompilerParams(vmem_limit_bytes=VMEM_LIMIT),
        cost_estimate=pl.CostEstimate(flops=4 * n_rows * d_model * cols, bytes_accessed=n_rows * d_model * 2, transcendentals=0),
        name="wide_part",
    )(meta, *rows, w_gate, w_up, far)


def down_body(n_group, splits, local, meta_ref, *refs):
    h_refs = refs[: len(splits)]
    w_ref = refs[len(splits)]
    out_refs = refs[len(splits) + 1 : len(splits) + 1 + n_group]
    w_buf, sem = refs[-2:]
    i = pl.program_id(0)

    @pl.when(i == 0)
    def _():
        copy = pltpu.make_async_copy(w_ref if local is None else w_ref.at[local], w_buf, sem)
        copy.start()
        copy.wait()

    @pl.when(i < meta_ref[1 + n_group])
    def _():
        total = None
        lo = 0
        for h_ref, cols in zip(h_refs, splits):
            part = jnp.dot(h_ref[...], w_buf[lo : lo + cols, :], preferred_element_type=F32)
            total = part if total is None else total + part
            lo += cols
        total = total.astype(BF16)
        for d in range(n_group):

            @pl.when((i >= meta_ref[1 + d]) & (i < meta_ref[2 + d]))
            def _():
                out_refs[d][...] = total


def down_part(meta, hidden, weight, n_group, local=None):
    n_rows = hidden[0].shape[0]
    splits = tuple(h.shape[1] for h in hidden)
    ffn, width = weight.shape[-2:]

    def h_spec(w):
        return pl.BlockSpec((TILE, w), lambda i, m: (jnp.clip(i, 0, jnp.maximum(m[1 + n_group] - 1, 0)), 0))

    def out_spec(d):
        def index(i, m):
            return jnp.clip(i - m[1 + d], 0, jnp.maximum(m[2 + d] - m[1 + d] - 1, 0)), 0

        return pl.BlockSpec((TILE, width), index)

    return pl.pallas_call(
        functools.partial(down_body, n_group, splits, local),
        grid_spec=pltpu.PrefetchScalarGridSpec(
            num_scalar_prefetch=1,
            grid=(n_rows // TILE,),
            in_specs=[h_spec(cols) for cols in splits] + [any_spec()],
            out_specs=[out_spec(d) for d in range(n_group)],
            scratch_shapes=[pltpu.VMEM((ffn, width), BF16), pltpu.SemaphoreType.DMA],
        ),
        out_shape=[jax.ShapeDtypeStruct((n_rows // n_group, width), BF16)] * n_group,
        compiler_params=pltpu.CompilerParams(vmem_limit_bytes=VMEM_LIMIT),
        cost_estimate=pl.CostEstimate(flops=2 * n_rows * ffn * width, bytes_accessed=n_rows * ffn * 2, transcendentals=0),
        name="down_part",
    )(meta, *hidden, weight)


def slab_start(first, e, n_tile, i, capacity):
    return jnp.minimum(first[e * n_tile + i] // ALIGN * ALIGN, capacity - SLAB)


def mix_body(n_exp, n_tile, capacity, with_pick, col_ref, first_ref, count_ref, pos_ref, gate_ref, x_ref, *refs):
    back_refs, refs = refs[:n_exp], refs[n_exp:]
    pick_ref = refs[0] if with_pick else refs[-1]
    y_ref, mark_ref = refs[-2:] if with_pick else refs[-3:-1]
    i = pl.program_id(0)
    reach = n_exp * SLAB
    if not with_pick:
        col = lax.broadcasted_iota(I32, (MIX_TILE, reach), 1)
        for j in range(2):
            pick_ref[:, j * reach : (j + 1) * reach] = (col == pos_ref[:, j : j + 1]).astype(F32).astype(BF16)
    row = lax.broadcasted_iota(I32, (SLAB, 1), 0)
    parts = []
    for e in range(n_exp):
        start = slab_start(first_ref, e, n_tile, i, capacity)
        slab = back_refs[e][pl.ds(pl.multiple_of(start, ALIGN), SLAB), :]
        parts.append(jnp.where(row + start < count_ref[e], slab, jnp.zeros_like(slab)))
    rows = jnp.concatenate(parts, axis=0)
    o0 = jnp.dot(pick_ref[:, :reach], rows, preferred_element_type=F32)
    o1 = jnp.dot(pick_ref[:, reach:], rows, preferred_element_type=F32)
    mixed = gate_ref[:, 0:1] * o0 + gate_ref[:, 1:2] * o1
    y_ref[...] = (x_ref[...].astype(F32) + mixed).astype(BF16)
    mark_ref[...] = jnp.zeros_like(mark_ref)


def mix_cols(col_block, y_loc, pick, x_loc, pos, gate_loc, first_mix, counts, back):
    tok_rows, d_model = x_loc.shape
    n_tile = tok_rows // MIX_TILE
    n_exp = len(back)
    capacity, width = back[0].shape
    reach = n_exp * SLAB
    tile = lambda w: pl.BlockSpec((MIX_TILE, w), lambda i, c, f, n: (i, 0))
    cols = pl.BlockSpec((MIX_TILE, width), lambda i, c, f, n: (i, c[0]))
    mark = pl.BlockSpec((8, 128), lambda i, c, f, n: (0, 0))
    whole = pl.BlockSpec((capacity, width), lambda i, c, f, n: (0, 0))
    args = [col_block, first_mix, counts, pos, gate_loc, x_loc, *back]
    specs = [tile(2), tile(2), cols] + [whole] * n_exp
    outs = [jax.ShapeDtypeStruct((tok_rows, d_model), BF16), jax.ShapeDtypeStruct((8, 128), I32)]
    out_specs = [cols, mark]
    alias = {}
    if pick is None:
        outs.append(jax.ShapeDtypeStruct((tok_rows, 2 * reach), BF16))
        out_specs.append(tile(2 * reach))
    else:
        args += [pick, y_loc]
        specs += [tile(2 * reach), any_spec()]
        alias = {len(args) - 1: 0}
    return pl.pallas_call(
        functools.partial(mix_body, n_exp, n_tile, capacity, pick is not None),
        grid_spec=pltpu.PrefetchScalarGridSpec(num_scalar_prefetch=3, grid=(n_tile,), in_specs=specs, out_specs=out_specs),
        out_shape=outs,
        input_output_aliases=alias,
        compiler_params=pltpu.CompilerParams(vmem_limit_bytes=VMEM_LIMIT),
        cost_estimate=pl.CostEstimate(flops=20_000_000 * width, bytes_accessed=20_000 * width, transcendentals=0),
        name="mix_cols",
    )(*args)


def spans(sizes):
    lo = 0
    for size in sizes:
        yield lo, size
        lo += size


def solution(mesh):
    n_group, n_side = mesh.shape["expert"], mesh.shape["data"]
    tok_spec = P(("rep", "expert", "data"), None)
    wide_spec = P("expert", "data", None)
    down_spec = P("expert", None, "data")
    swap = [(s, 1 - s) for s in range(n_side)]

    def whole_step(x_loc, idx_loc, gate_loc, wg_loc, wu_loc, wd_loc):
        tok_rows, _ = x_loc.shape
        top_k = idx_loc.shape[1]
        n_local, half, _ = wg_loc.shape
        n_exp = n_local * n_group
        capacity = capacity_rows(tok_rows, top_k, n_exp)
        side = lax.axis_index("data")
        place = lax.axis_index("expert")
        locals_ = range(n_local)
        groups = jnp.arange(n_group, dtype=I32)

        ids = ((idx_loc // n_local + n_group - place) % n_group * n_local + idx_loc % n_local).T
        experts = jnp.arange(n_exp, dtype=I32)[:, None]
        chosen = functools.reduce(jnp.logical_or, [ids[j][None, :] == experts for j in range(top_k)])
        chosen_i = chosen.astype(I32)
        running = jnp.cumsum(chosen_i, axis=1)
        before = running - chosen_i
        slot_te = jnp.where(chosen & (before < capacity), before, -1)
        counts = jnp.minimum(running[:, -1], capacity)
        first = jnp.minimum(before, capacity)
        first_blk = jnp.concatenate([first[:, ::TOK_BLOCK], counts[:, None]], axis=1).reshape(-1)
        first_mix = first[:, ::MIX_TILE]

        table = lax.all_gather(counts, "expert")
        meta = []
        for l in locals_:
            mine = jnp.sum(jnp.where(((place - groups) % n_group)[:, None, None] == groups[None, :, None], table.reshape(n_group, n_group, n_local)[None, :, :, l] * (groups[:, None, None] == groups[None, None, :]), 0), axis=(1, 2))
            ends = jnp.cumsum((mine + TILE - 1) // TILE)
            meta.append(jnp.concatenate([side[None], jnp.zeros((1,), I32), ends]).astype(I32))

        starts = jnp.minimum(first_mix // ALIGN * ALIGN, capacity - SLAB)
        at = jnp.where(slot_te < 0, -n_exp * SLAB, slot_te - jnp.repeat(starts, MIX_TILE, axis=1) + experts * SLAB)
        pos = jnp.stack([jnp.sum(jnp.where(ids[j][None, :] == experts, at, 0), axis=0) for j in range(top_k)], axis=1)
        first_mix = first_mix.reshape(-1)

        done = []

        def in_turn(kernel, small, *args):
            if done:
                small = after(small, done[-1]) if done[-1].ndim else small + done[-1]
            out = kernel(small, *args)
            done.append(out[0] if isinstance(out, (list, tuple)) else out)
            return out

        wide_spans = list(spans(WIDE_CHUNKS))
        down_spans = list(spans(DOWN_PIECES))
        parts = [jnp.stack([w[l, :, lo : lo + n] for w in (wg_loc, wu_loc)]) for l in locals_ for lo, n in wide_spans]
        parts += [wd_loc[l, :, lo : lo + n] for lo, n in down_spans for l in locals_]
        far = []

        def cross():
            if len(far) == len(parts):
                return
            piece = parts[len(far)]
            if len(far) >= 2:
                piece = after(piece, far[-2])
            far.append(lax.ppermute(piece, "data", swap))

        def exchange(blocks, step):
            out = [blocks[0]]
            for d in range(1, n_group):
                out.append(lax.ppermute(blocks[d], "expert", [(s, (s + step * d) % n_group) for s in range(n_group)]))
            return out

        def mix(y_loc, pick, col_block, back):
            back = [back[l][d] for d in range(n_group) for l in locals_]
            out = in_turn(mix_cols, col_block.astype(I32)[None], y_loc, pick, x_loc, pos, gate_loc, first_mix, counts, back)
            done[-1] = out[1][0, 0]
            return out[0], out[2] if pick is None else pick

        cross()
        cross()
        first_blk = after(first_blk, meta)
        rows = [exchange(in_turn(pack_rows, first_blk, x_loc, slot_te, n_exp, n_local, 0, capacity), 1)]
        cross()
        packed = in_turn(pack_rows, first_blk, x_loc, slot_te, n_exp, n_local, 1, capacity)
        cross()
        rows.append(exchange([after(block, rows[0]) for block in packed], 1))

        n_wide = len(wide_spans)
        hidden, own = [], []
        for l in locals_:
            hidden.append([])
            for k, (lo, n) in enumerate(wide_spans):
                if l or k >= 2:
                    cross()
                hidden[l].append(in_turn(wide_part, meta[l], rows[l], wg_loc, wu_loc, far[l * n_wide + k], l, lo, n))
            own.append(exchange(in_turn(down_part, meta[l], hidden[l], wd_loc, n_group, l), -1))

        def far_piece(c, l):
            cross()
            return exchange(in_turn(down_part, meta[l], hidden[l], far[n_local * (n_wide + c) + l], n_group), -1)

        def col_block(c):
            return ((1 - side) * half + down_spans[c][0]) // down_spans[c][1]

        piece = [far_piece(0, l) for l in locals_]
        y_loc, pick = mix(None, None, side, own)
        for c in range(1, len(down_spans) - 1):
            piece, ready = [far_piece(c, l) for l in locals_], piece
            y_loc, pick = mix(y_loc, pick, col_block(c - 1), ready)
        c = len(down_spans) - 1
        last = [far_piece(c, 0)]
        y_loc, pick = mix(y_loc, pick, col_block(c - 1), piece)
        last.append(far_piece(c, 1))
        return mix(y_loc, pick, col_block(c), last)[0]

    in_specs = (tok_spec, tok_spec, tok_spec, wide_spec, wide_spec, down_spec)
    return jax.shard_map(whole_step, mesh=mesh, in_specs=in_specs, out_specs=tok_spec, check_vma=False)
```

time: 2860 us -> 1800 us (0.63)
  Pallas kernels: 0 us -> 914 us
  matrix products: 766 us -> 0 us
  waiting for transfers between devices: 1330 us -> 643 us
  local copies, waits for them, and re-layouts: 505 us -> 61.4 us
  other arithmetic: 210 us -> 41.5 us
  starting transfers between devices: 23.3 us -> 114 us
    pallas_call x0 -> x22, Pallas kernels: none -> 914 us  [the longest x8 411 us: wide_part(): pl.pallas_call(functools.partial(wide_body, n_group, local, lo_col, cols)...]
    all_to_all x2 -> x0, waiting for transfers between devices: 895 us -> none  [the longest x1 453 us: device_step(): recv_rows = lax.all_to_all(send_rows, 'expert', 1, 1, tiled=True)]
    dot_general x3 -> x0, matrix products: 766 us -> none  [the longest x1 264 us: expert_ffn(): jnp.einsum('erd,edf->erf', expert_rows, w_up, preferred_element_type=jnp....]
    ppermute x0 -> x44, waiting for transfers between devices: none -> 643 us  [the longest x14 427 us: cross(): far.append(lax.ppermute(piece, 'data', swap))]
    all_gather x3 -> x0, waiting for transfers between devices: 431 us -> none  [the longest x1 266 us: device_step(): wd_full = lax.all_gather(wd_loc, 'data', axis=2, tiled=True)]
    gather x3 -> x0, local copies, waits for them, and re-layouts: 379 us -> none  [the longest x2 293 us: combine_rows(): pair_out = jnp.take(back_rows, dest_row, axis=0, mode='fill', fill_value=0)]
    reduce_sum x2, other arithmetic: 152 us -> 0.46 us  [the longest x1 0.31 us: whole_step(): jnp.sum(jnp.where(((place - groups) % n_group)[:, None, None] == groups[N...]
    ppermute x0 -> x44, starting transfers between devices: none -> 114 us  [the longest x30 94.7 us: exchange(): lax.ppermute(blocks[d], 'expert', [(s, (s + step * d) % n_group) for s in...]
  transfers between devices with their start and end apart: 5 -> 44, of which waited for: 4 -> 14; matrix products, arithmetic and copies ran while one was open for 25% -> 5% of each run, Pallas kernels for 0% -> 50%
where the time goes in v1:
time: 1800 us; the launch traced here: 1780 us
  Pallas kernels  914 us (51%)
  waiting for transfers between devices  643 us (36%)
  starting transfers between devices  114 us (6%)
  local copies, waits for them, and re-layouts  61.4 us (3%)
  other arithmetic  41.5 us (2%)
    ppermute x14, waiting for transfers between devices, cross(): far.append(lax.ppermute(piece, 'data', swap))  427 us
    pallas_call x8, Pallas kernels, wide_part(): pl.pallas_call(functools.partial(wide_body, n_group, local, lo_col, cols)...  411 us
    pallas_call x8, Pallas kernels, down_part(): pl.pallas_call(functools.partial(down_body, n_group, splits, local), grid...  282 us
    ppermute x30, waiting for transfers between devices, exchange(): lax.ppermute(blocks[d], 'expert', [(s, (s + step * d) % n_group) for s in...  216 us
    pallas_call x4, Pallas kernels, mix_cols(): pl.pallas_call(functools.partial(mix_body, n_exp, n_tile, capacity, pick...  136 us
    ppermute x30, starting transfers between devices, exchange(): lax.ppermute(blocks[d], 'expert', [(s, (s + step * d) % n_group) for s in...  94.7 us
    pallas_call x2, Pallas kernels, pack_rows(): pl.pallas_call(functools.partial(pack_body, n_local, local, n_blk, n_grou...  85.5 us
  transfers between devices with their start and end apart: 44, of which 14 were waited for; matrix products, arithmetic and copies ran while one was open for 5% of the time, Pallas kernels for 50%

profile of v1, /device:TPU:0, one launch (start us, length us, event | category | flops | bytes accessed | tf_op | source)
XLA Modules:
  0.0 1780.4 jit_solution(12258428253957959306)
XLA Ops:
  0.0 5.2 fusion.17
  16.0 4.9 all-reduce
  24.7 40.3 %pack_rows.2 = (bf16[1280,2048]{1,0:T(8,128)(2,1)}, bf16[1280,2048]{1,0:T(8,128)(2,1)}, bf16[1280,2048]{1,0:T(8,128)(2,1)}, bf16[1280,2048]{1,0:T(8,128)(2,1)}) custom-call(s32[136]{0:T(256)} %reshape.319.first_ref, s32[8,4096]{1,0:T(8,128)} %get-tuple-element.199.slot_ref, bf16[4096,2048]{1,0:T(8,128)(2,1)} %x_ref.11), custom_call_target="tpu_custom_call" | custom-call | flops 20000000000 | bytes 60000000 | tf_op jit(solution)/shard_map/pack_rows/pallas_call | solution.py:82
  68.6 24.4 %fusion.15 = (bf16[1,1024,1536]{2,1,0:T(8,128)(2,1)}, bf16[1,1024,1536]{2,1,0:T(8,128)(2,1)}, bf16[1,1024,1536]{2,1,0:T(8,128)(2,1)}, bf16[1,1024,1536]{2,1,0:T(...) fusion(bf16[2,1024,5632]{2,1,0:T(8,128)(2,1)} %refs_4_.18, ...), kind=kLoop, calls=%fused_computation.83 | loop fusion | bytes 75497472 | tf_op jit(solution)/shard_map/slice | solution.py:350
  93.0 5.2 pad_maximum_fusion
  98.3 45.2 %pack_rows.3 = (bf16[1280,2048]{1,0:T(8,128)(2,1)}, bf16[1280,2048]{1,0:T(8,128)(2,1)}, bf16[1280,2048]{1,0:T(8,128)(2,1)}, bf16[1280,2048]{1,0:T(8,128)(2,1)}) custom-call(s32[136]{0:T(256)} %reshape.319.first_ref, s32[8,4096]{1,0:T(8,128)} %get-tuple-element.199.slot_ref, bf16[4096,2048]{1,0:T(8,128)(2,1)} %x_ref.11), custom_call_target="tpu_custom_call" | custom-call | flops 20000000000 | bytes 60000000 | tf_op jit(solution)/shard_map/pack_rows/pallas_call | solution.py:82
  143.5 6.2 pad_maximum_fusion.5
  163.2 8.9 slice_bitcast_fusion.2
  179.1 5.2 pad_maximum_fusion.1
  184.3 9.5 slice_bitcast_fusion
  195.8 96.8 %collective-permute-done.2.refs_3_ = bf16[1280,2048]{1,0:T(8,128)(2,1)} collective-permute-done((bf16[1280,2048]{1,0:T(8,128)(2,1)}, bf16[1280,2048]{1,0:T(8,128)(2,1)}, u32[]{:S(2)}, u32[]{:S(2)}) %collective-permute-start.2) | collective-permute-done | bytes 5242912 | tf_op jit(solution)/shard_map/ppermute | solution.py:365
  295.0 39.0 %wide_part.8.refs_0_ = bf16[5120,1024]{1,0:T(8,128)(2,1)} custom-call(s32[6]{0:T(128)} %pad_add_fusion.4.meta_ref, bf16[1280,2048]{1,0:T(8,128)(2,1)} %get-tuple-element.89.refs_0_, bf16[1280,2048]{1,0:T(8,128)(2,1)} %collective-permute-done.refs_1_, bf16[1280,2048]{1,0:T(8,128)(2,1)} %collective-permute-done.1.refs_2_, ...), custom_call_target="tpu_custom_call" | custom-call | flops 42949672960 | bytes 20971520 | tf_op jit(solution)/shard_map/wide_part/pallas_call | solution.py:148
  334.0 55.5 %wide_part.9.refs_1_ = bf16[5120,1536]{1,0:T(8,128)(2,1)} custom-call(s32[6]{0:T(128)} %pad_add_fusion.4.meta_ref, bf16[1280,2048]{1,0:T(8,128)(2,1)} %get-tuple-element.89.refs_0_, bf16[1280,2048]{1,0:T(8,128)(2,1)} %collective-permute-done.refs_1_, bf16[1280,2048]{1,0:T(8,128)(2,1)} %collective-permute-done.1.refs_2_, ...), custom_call_target="tpu_custom_call" | custom-call | flops 64424509440 | bytes 20971520 | tf_op jit(solution)/shard_map/wide_part/pallas_call | solution.py:148
  389.6 55.4 %wide_part.10.refs_2_ = bf16[5120,1536]{1,0:T(8,128)(2,1)} custom-call(s32[6]{0:T(128)} %pad_add_fusion.4.meta_ref, bf16[1280,2048]{1,0:T(8,128)(2,1)} %get-tuple-element.89.refs_0_, bf16[1280,2048]{1,0:T(8,128)(2,1)} %collective-permute-done.refs_1_, bf16[1280,2048]{1,0:T(8,128)(2,1)} %collective-permute-done.1.refs_2_, ...), custom_call_target="tpu_custom_call" | custom-call | flops 64424509440 | bytes 20971520 | tf_op jit(solution)/shard_map/wide_part/pallas_call | solution.py:148
  445.0 62.2 %collective-permute-done.6.refs_6_ = bf16[2,1024,1536]{2,1,0:T(8,128)(2,1)} collective-permute-done((bf16[2,1024,1536]{2,1,0:T(8,128)(2,1)}, bf16[2,1024,1536]{2,1,0:T(8,128)(2,1)}, u32[]{:S(2)}, u32[]{:S(2)}) %collective-permute-start.6) | collective-permute-done | bytes 6291488 | tf_op jit(solution)/shard_map/ppermute | solution.py:360
  509.2 55.4 %wide_part.11.refs_3_ = bf16[5120,1536]{1,0:T(8,128)(2,1)} custom-call(s32[6]{0:T(128)} %pad_add_fusion.4.meta_ref, bf16[1280,2048]{1,0:T(8,128)(2,1)} %get-tuple-element.89.refs_0_, bf16[1280,2048]{1,0:T(8,128)(2,1)} %collective-permute-done.refs_1_, bf16[1280,2048]{1,0:T(8,128)(2,1)} %collective-permute-done.1.refs_2_, ...), custom_call_target="tpu_custom_call" | custom-call | flops 64424509440 | bytes 20971520 | tf_op jit(solution)/shard_map/wide_part/pallas_call | solution.py:148
  564.6 56.1 %down_part.8 = (bf16[1280,1024]{1,0:T(8,128)(2,1)}, bf16[1280,1024]{1,0:T(8,128)(2,1)}, bf16[1280,1024]{1,0:T(8,128)(2,1)}, bf16[1280,1024]{1,0:T(8,128)(2,1)}) custom-call(s32[6]{0:T(128)} %pad_add_fusion.4.meta_ref, bf16[5120,1024]{1,0:T(8,128)(2,1)} %wide_part.8.refs_0_, bf16[5120,1536]{1,0:T(8,128)(2,1)} %wide_part.9.refs_1_, ...), custom_call_target="tpu_custom_call" | custom-call | flops 59055800320 | bytes 57671680 | tf_op jit(solution)/shard_map/down_part/pallas_call | solution.py:213
  620.7 38.4 %collective-permute-start.16 = (bf16[1280,1024]{1,0:T(8,128)(2,1)}, bf16[1280,1024]{1,0:T(8,128)(2,1)}, u32[]{:S(2)}, u32[]{:S(2)}) collective-permute-start(bf16[1280,1024]{1,0:T(8,128)(2,1)} %get-tuple-element.127), channel_id=1, source_target_pairs={{0,3},{1,0},{2,1},{3,2},{4,7},{5,4},{6,5},{7,6}} | collective-permute-start | bytes 7864328 | tf_op jit(solution)/shard_map/ppermute | solution.py:365
  662.7 39.1 %wide_part.12.refs_0_ = bf16[5120,1024]{1,0:T(8,128)(2,1)} custom-call(s32[6]{0:T(128)} %pad_add_fusion.2.meta_ref, bf16[1280,2048]{1,0:T(8,128)(2,1)} %get-tuple-element.104.refs_0_, bf16[1280,2048]{1,0:T(8,128)(2,1)} %collective-permute-done.7.refs_1_, bf16[1280,2048]{1,0:T(8,128)(2,1)} %collective-permute-done.8.refs_2_, ...), custom_call_target="tpu_custom_call" | custom-call | flops 42949672960 | bytes 20971520 | tf_op jit(solution)/shard_map/wide_part/pallas_call | solution.py:148
  701.8 30.1 %collective-permute-done.11.refs_6_ = bf16[2,1024,1536]{2,1,0:T(8,128)(2,1)} collective-permute-done((bf16[2,1024,1536]{2,1,0:T(8,128)(2,1)}, bf16[2,1024,1536]{2,1,0:T(8,128)(2,1)}, u32[]{:S(2)}, u32[]{:S(2)}) %collective-permute-start.11) | collective-permute-done | bytes 6291488 | tf_op jit(solution)/shard_map/ppermute | solution.py:360
  733.9 55.6 %wide_part.13.refs_1_ = bf16[5120,1536]{1,0:T(8,128)(2,1)} custom-call(s32[6]{0:T(128)} %pad_add_fusion.2.meta_ref, bf16[1280,2048]{1,0:T(8,128)(2,1)} %get-tuple-element.104.refs_0_, bf16[1280,2048]{1,0:T(8,128)(2,1)} %collective-permute-done.7.refs_1_, bf16[1280,2048]{1,0:T(8,128)(2,1)} %collective-permute-done.8.refs_2_, ...), custom_call_target="tpu_custom_call" | custom-call | flops 64424509440 | bytes 20971520 | tf_op jit(solution)/shard_map/wide_part/pallas_call | solution.py:148
  789.5 77.2 %collective-permute-done.12.refs_6_ = bf16[2,1024,1536]{2,1,0:T(8,128)(2,1)} collective-permute-done((bf16[2,1024,1536]{2,1,0:T(8,128)(2,1)}, bf16[2,1024,1536]{2,1,0:T(8,128)(2,1)}, u32[]{:S(2)}, u32[]{:S(2)}) %collective-permute-start.12) | collective-permute-done | bytes 6291488 | tf_op jit(solution)/shard_map/ppermute | solution.py:360
  868.7 55.4 %wide_part.14.refs_2_ = bf16[5120,1536]{1,0:T(8,128)(2,1)} custom-call(s32[6]{0:T(128)} %pad_add_fusion.2.meta_ref, bf16[1280,2048]{1,0:T(8,128)(2,1)} %get-tuple-element.104.refs_0_, bf16[1280,2048]{1,0:T(8,128)(2,1)} %collective-permute-done.7.refs_1_, bf16[1280,2048]{1,0:T(8,128)(2,1)} %collective-permute-done.8.refs_2_, ...), custom_call_target="tpu_custom_call" | custom-call | flops 64424509440 | bytes 20971520 | tf_op jit(solution)/shard_map/wide_part/pallas_call | solution.py:148
  924.1 77.4 %collective-permute-done.13.refs_6_ = bf16[2,1024,1536]{2,1,0:T(8,128)(2,1)} collective-permute-done((bf16[2,1024,1536]{2,1,0:T(8,128)(2,1)}, bf16[2,1024,1536]{2,1,0:T(8,128)(2,1)}, u32[]{:S(2)}, u32[]{:S(2)}) %collective-permute-start.13) | collective-permute-done | bytes 6291488 | tf_op jit(solution)/shard_map/ppermute | solution.py:360
  1003.6 55.4 %wide_part.15.refs_3_ = bf16[5120,1536]{1,0:T(8,128)(2,1)} custom-call(s32[6]{0:T(128)} %pad_add_fusion.2.meta_ref, bf16[1280,2048]{1,0:T(8,128)(2,1)} %get-tuple-element.104.refs_0_, bf16[1280,2048]{1,0:T(8,128)(2,1)} %collective-permute-done.7.refs_1_, bf16[1280,2048]{1,0:T(8,128)(2,1)} %collective-permute-done.8.refs_2_, ...), custom_call_target="tpu_custom_call" | custom-call | flops 64424509440 | bytes 20971520 | tf_op jit(solution)/shard_map/wide_part/pallas_call | solution.py:148
  1058.9 66.2 %collective-permute-done.14.refs_4_ = bf16[5632,512]{1,0:T(8,128)(2,1)} collective-permute-done((bf16[5632,512]{1,0:T(8,128)(2,1)}, bf16[5632,512]{1,0:T(8,128)(2,1)}, u32[]{:S(2)}, u32[]{:S(2)}) %collective-permute-start.14) | collective-permute-done | bytes 5767200 | tf_op jit(solution)/shard_map/ppermute | solution.py:360
  1127.1 56.1 %down_part.9 = (bf16[1280,1024]{1,0:T(8,128)(2,1)}, bf16[1280,1024]{1,0:T(8,128)(2,1)}, bf16[1280,1024]{1,0:T(8,128)(2,1)}, bf16[1280,1024]{1,0:T(8,128)(2,1)}) custom-call(s32[6]{0:T(128)} %pad_add_fusion.2.meta_ref, bf16[5120,1024]{1,0:T(8,128)(2,1)} %wide_part.12.refs_0_, bf16[5120,1536]{1,0:T(8,128)(2,1)} %wide_part.13.refs_1_, ...), custom_call_target="tpu_custom_call" | custom-call | flops 59055800320 | bytes 57671680 | tf_op jit(solution)/shard_map/down_part/pallas_call | solution.py:213
  1183.2 32.9 %down_part.10 = (bf16[1280,512]{1,0:T(8,128)(2,1)}, bf16[1280,512]{1,0:T(8,128)(2,1)}, bf16[1280,512]{1,0:T(8,128)(2,1)}, bf16[1280,512]{1,0:T(8,128)(2,1)}) custom-call(s32[6]{0:T(128)} %pad_add_fusion.4.meta_ref, bf16[5120,1024]{1,0:T(8,128)(2,1)} %wide_part.8.refs_0_, bf16[5120,1536]{1,0:T(8,128)(2,1)} %wide_part.9.refs_1_, ...), custom_call_target="tpu_custom_call" | custom-call | flops 29527900160 | bytes 57671680 | tf_op jit(solution)/shard_map/down_part/pallas_call | solution.py:213
  1216.1 93.6 %collective-permute-done.22.refs_4_ = bf16[5632,256]{1,0:T(8,128)(2,1)} collective-permute-done((bf16[5632,256]{1,0:T(8,128)(2,1)}, bf16[5632,256]{1,0:T(8,128)(2,1)}, u32[]{:S(2)}, u32[]{:S(2)}) %collective-permute-start.22) | collective-permute-done | bytes 2883616 | tf_op jit(solution)/shard_map/ppermute | solution.py:360
  1311.6 32.9 %down_part.11 = (bf16[1280,512]{1,0:T(8,128)(2,1)}, bf16[1280,512]{1,0:T(8,128)(2,1)}, bf16[1280,512]{1,0:T(8,128)(2,1)}, bf16[1280,512]{1,0:T(8,128)(2,1)}) custom-call(s32[6]{0:T(128)} %pad_add_fusion.2.meta_ref, bf16[5120,1024]{1,0:T(8,128)(2,1)} %wide_part.12.refs_0_, bf16[5120,1536]{1,0:T(8,128)(2,1)} %wide_part.13.refs_1_, ...), custom_call_target="tpu_custom_call" | custom-call | flops 29527900160 | bytes 57671680 | tf_op jit(solution)/shard_map/down_part/pallas_call | solution.py:213
  1344.6 11.7 collective-permute-start.24
  1356.2 10.4 collective-permute-done.17.refs_3_
  1369.5 56.1 %collective-permute-done.19.refs_5_ = bf16[1280,1024]{1,0:T(8,128)(2,1)} collective-permute-done((bf16[1280,1024]{1,0:T(8,128)(2,1)}, bf16[1280,1024]{1,0:T(8,128)(2,1)}, u32[]{:S(2)}, u32[]{:S(2)}) %collective-permute-start.19) | collective-permute-done | bytes 2621472 | tf_op jit(solution)/shard_map/ppermute | solution.py:365
  1427.6 43.7 %mix_cols.4 = (bf16[4096,2048]{1,0:T(8,128)(2,1)}, s32[8,128]{1,0:T(8,128)}, bf16[4096,2304]{1,0:T(8,128)(2,1)}) custom-call(s32[1]{0:T(128)} %bitcast.1.col_ref, s32[256]{0:T(256)} %reshape.320.first_ref, s32[8]{0:T(128)} %copy-done.13, s32[4096,2]{1,0:T(8,128)} %copy.28.pos_ref, f32[4096,2]{1,0:T(8,128)} %copy.29.gate_ref, bf16[4096,2048]{1,0:T(8,128)(2,1)} %x_ref.11, ...), custom_call_target="tpu_custom_call" | custom-call | flops 20480000000 | bytes 20480000 | tf_op jit(solution)/shard_map/mix_cols/pallas_call | solution.py:279
  1473.8 25.9 %down_part.12 = (bf16[1280,256]{1,0:T(8,128)(2,1)}, bf16[1280,256]{1,0:T(8,128)(2,1)}, bf16[1280,256]{1,0:T(8,128)(2,1)}, bf16[1280,256]{1,0:T(8,128)(2,1)}) custom-call(s32[6]{0:T(128)} %broadcast_add_fusion.2.meta_ref, bf16[5120,1024]{1,0:T(8,128)(2,1)} %wide_part.8.refs_0_, bf16[5120,1536]{1,0:T(8,128)(2,1)} %wide_part.9.refs_1_, ...), custom_call_target="tpu_custom_call" | custom-call | flops 14763950080 | bytes 57671680 | tf_op jit(solution)/shard_map/down_part/pallas_call | solution.py:213
  1499.7 20.7 %collective-permute-done.23.refs_4_ = bf16[5632,256]{1,0:T(8,128)(2,1)} collective-permute-done((bf16[5632,256]{1,0:T(8,128)(2,1)}, bf16[5632,256]{1,0:T(8,128)(2,1)}, u32[]{:S(2)}, u32[]{:S(2)}) %collective-permute-start.23) | collective-permute-done | bytes 2883616 | tf_op jit(solution)/shard_map/ppermute | solution.py:360
  1520.9 25.9 %down_part.13 = (bf16[1280,256]{1,0:T(8,128)(2,1)}, bf16[1280,256]{1,0:T(8,128)(2,1)}, bf16[1280,256]{1,0:T(8,128)(2,1)}, bf16[1280,256]{1,0:T(8,128)(2,1)}) custom-call(s32[6]{0:T(128)} %pad_add_fusion.2.meta_ref, bf16[5120,1024]{1,0:T(8,128)(2,1)} %wide_part.12.refs_0_, bf16[5120,1536]{1,0:T(8,128)(2,1)} %wide_part.13.refs_1_, ...), custom_call_target="tpu_custom_call" | custom-call | flops 14763950080 | bytes 57671680 | tf_op jit(solution)/shard_map/down_part/pallas_call | solution.py:213
  1546.8 9.3 collective-permute-start.31
  1556.1 21.8 %collective-permute-done.27.refs_5_ = bf16[1280,512]{1,0:T(8,128)(2,1)} collective-permute-done((bf16[1280,512]{1,0:T(8,128)(2,1)}, bf16[1280,512]{1,0:T(8,128)(2,1)}, u32[]{:S(2)}, u32[]{:S(2)}) %collective-permute-start.27) | collective-permute-done | bytes 1310752 | tf_op jit(solution)/shard_map/ppermute | solution.py:365
  1581.5 34.0 %mix_cols.5 = (bf16[4096,2048]{1,0:T(8,128)(2,1)}, s32[8,128]{1,0:T(8,128)}) custom-call(s32[1]{0:T(128)} %bitcast.11.col_ref, s32[256]{0:T(256)} %reshape.320.first_ref, s32[8]{0:T(128)} %copy-done.13, s32[4096,2]{1,0:T(8,128)} %copy.28.pos_ref, f32[4096,2]{1,0:T(8,128)} %copy.29.gate_ref, ...), custom_call_target="tpu_custom_call", output_to_operand_aliasing={{0}: (15, {})} | custom-call | flops 10240000000 | bytes 10240000 | tf_op jit(solution)/shard_map/mix_cols/pallas_call | solution.py:279
  1619.8 25.9 %down_part.14 = (bf16[1280,256]{1,0:T(8,128)(2,1)}, bf16[1280,256]{1,0:T(8,128)(2,1)}, bf16[1280,256]{1,0:T(8,128)(2,1)}, bf16[1280,256]{1,0:T(8,128)(2,1)}) custom-call(s32[6]{0:T(128)} %broadcast_add_fusion.1.meta_ref, bf16[5120,1024]{1,0:T(8,128)(2,1)} %wide_part.8.refs_0_, bf16[5120,1536]{1,0:T(8,128)(2,1)} %wide_part.9.refs_1_, ...), custom_call_target="tpu_custom_call" | custom-call | flops 14763950080 | bytes 57671680 | tf_op jit(solution)/shard_map/down_part/pallas_call | solution.py:213
  1645.8 9.5 collective-permute-start.38
  1655.5 29.0 %mix_cols.6 = (bf16[4096,2048]{1,0:T(8,128)(2,1)}, s32[8,128]{1,0:T(8,128)}) custom-call(s32[1]{0:T(128)} %bitcast.8.col_ref, s32[256]{0:T(256)} %reshape.320.first_ref, s32[8]{0:T(128)} %copy-done.13, s32[4096,2]{1,0:T(8,128)} %copy.28.pos_ref, f32[4096,2]{1,0:T(8,128)} %copy.29.gate_ref, ...), custom_call_target="tpu_custom_call", output_to_operand_aliasing={{0}: (15, {})} | custom-call | flops 5120000000 | bytes 5120000 | tf_op jit(solution)/shard_map/mix_cols/pallas_call | solution.py:279
  1686.8 25.9 %down_part.15 = (bf16[1280,256]{1,0:T(8,128)(2,1)}, bf16[1280,256]{1,0:T(8,128)(2,1)}, bf16[1280,256]{1,0:T(8,128)(2,1)}, bf16[1280,256]{1,0:T(8,128)(2,1)}) custom-call(s32[6]{0:T(128)} %broadcast_add_fusion.meta_ref, bf16[5120,1024]{1,0:T(8,128)(2,1)} %wide_part.12.refs_0_, bf16[5120,1536]{1,0:T(8,128)(2,1)} %wide_part.13.refs_1_, ...), custom_call_target="tpu_custom_call" | custom-call | flops 14763950080 | bytes 57671680 | tf_op jit(solution)/shard_map/down_part/pallas_call | solution.py:213
  1712.7 9.4 collective-permute-start.39
  1722.3 15.3 collective-permute-done.39.refs_3_
  1737.5 13.5 collective-permute-done.41.refs_5_
  1751.0 28.9 %mix_cols.7 = (bf16[4096,2048]{1,0:T(8,128)(2,1)}, s32[8,128]{1,0:T(8,128)}) custom-call(s32[1]{0:T(128)} %bitcast.col_ref, s32[256]{0:T(256)} %reshape.320.first_ref, s32[8]{0:T(128)} %copy-done.13, s32[4096,2]{1,0:T(8,128)} %copy.28.pos_ref, f32[4096,2]{1,0:T(8,128)} %copy.29.gate_ref, ...), custom_call_target="tpu_custom_call", output_to_operand_aliasing={{0}: (15, {})} | custom-call | flops 5120000000 | bytes 5120000 | tf_op jit(solution)/shard_map/mix_cols/pallas_call | solution.py:279
  (154 shorter events, 76.5 us)
Async XLA Ops:
  7.6 186.2 %collective-permute-start.3 = (bf16[2,1024,1024]{2,1,0:T(8,128)(2,1)}, bf16[2,1024,1024]{2,1,0:T(8,128)(2,1)}, u32[]{:S(2)}, u32[]{:S(2)}) collective-permute-start(bf16[2,1024,1024]{2,1,0:T(8,128)(2,1)} %pad_maximum_fusion.6), channel_id=1, source_target_pairs={{0,4},{4,0},{1,5},{5,1},{2,6},{6,2},{3,7},{7,3}} | collective-permute-start | bytes 12582920 | tf_op jit(solution)/shard_map/ppermute | solution.py:360
  65.0 130.8 %collective-permute-start = (bf16[1280,2048]{1,0:T(8,128)(2,1)}, bf16[1280,2048]{1,0:T(8,128)(2,1)}, u32[]{:S(2)}, u32[]{:S(2)}) collective-permute-start(bf16[1280,2048]{1,0:T(8,128)(2,1)} %get-tuple-element.93), channel_id=1, source_target_pairs={{0,1},{1,2},{2,3},{3,0},{4,5},{5,6},{6,7},{7,4}} | collective-permute-start | bytes 15728648 | tf_op jit(solution)/shard_map/ppermute | solution.py:365
  65.1 130.7 %collective-permute-start.1 = (bf16[1280,2048]{1,0:T(8,128)(2,1)}, bf16[1280,2048]{1,0:T(8,128)(2,1)}, u32[]{:S(2)}, u32[]{:S(2)}) collective-permute-start(bf16[1280,2048]{1,0:T(8,128)(2,1)} %get-tuple-element.94), channel_id=1, source_target_pairs={{0,2},{1,3},{2,0},{3,1},{4,6},{5,7},{6,4},{7,5}} | collective-permute-start | bytes 15728648 | tf_op jit(solution)/shard_map/ppermute | solution.py:365
  67.1 225.5 %collective-permute-start.2 = (bf16[1280,2048]{1,0:T(8,128)(2,1)}, bf16[1280,2048]{1,0:T(8,128)(2,1)}, u32[]{:S(2)}, u32[]{:S(2)}) collective-permute-start(bf16[1280,2048]{1,0:T(8,128)(2,1)} %get-tuple-element.95), channel_id=1, source_target_pairs={{0,3},{1,0},{2,1},{3,2},{4,7},{5,4},{6,5},{7,6}} | collective-permute-start | bytes 15728648 | tf_op jit(solution)/shard_map/ppermute | solution.py:365
  98.2 235.8 %collective-permute-start.4 = (bf16[2,1024,1536]{2,1,0:T(8,128)(2,1)}, bf16[2,1024,1536]{2,1,0:T(8,128)(2,1)}, u32[]{:S(2)}, u32[]{:S(2)}) collective-permute-start(bf16[2,1024,1536]{2,1,0:T(8,128)(2,1)} %pad_maximum_fusion), channel_id=1, source_target_pairs={{0,4},{4,0},{1,5},{5,1},{2,6},{6,2},{3,7},{7,3}} | collective-permute-start | bytes 18874376 | tf_op jit(solution)/shard_map/ppermute | solution.py:360
  193.8 195.8 %collective-permute-start.5 = (bf16[2,1024,1536]{2,1,0:T(8,128)(2,1)}, bf16[2,1024,1536]{2,1,0:T(8,128)(2,1)}, u32[]{:S(2)}, u32[]{:S(2)}) collective-permute-start(bf16[2,1024,1536]{2,1,0:T(8,128)(2,1)} %pad_maximum_fusion.1), channel_id=1, source_target_pairs={{0,4},{4,0},{1,5},{5,1},{2,6},{6,2},{3,7},{7,3}} | collective-permute-start | bytes 18874376 | tf_op jit(solution)/shard_map/ppermute | solution.py:360
  292.7 366.4 %collective-permute-start.9 = (bf16[1280,2048]{1,0:T(8,128)(2,1)}, bf16[1280,2048]{1,0:T(8,128)(2,1)}, u32[]{:S(2)}, u32[]{:S(2)}) collective-permute-start(bf16[1280,2048]{1,0:T(8,128)(2,1)} %get-tuple-element.110), channel_id=1, source_target_pairs={{0,3},{1,0},{2,1},{3,2},{4,7},{5,4},{6,5},{7,6}} | collective-permute-start | bytes 15728648 | tf_op jit(solution)/shard_map/ppermute | solution.py:365
  294.9 367.1 %collective-permute-start.8 = (bf16[1280,2048]{1,0:T(8,128)(2,1)}, bf16[1280,2048]{1,0:T(8,128)(2,1)}, u32[]{:S(2)}, u32[]{:S(2)}) collective-permute-start(bf16[1280,2048]{1,0:T(8,128)(2,1)} %get-tuple-element.108), channel_id=1, source_target_pairs={{0,2},{1,3},{2,0},{3,1},{4,6},{5,7},{6,4},{7,5}} | collective-permute-start | bytes 15728648 | tf_op jit(solution)/shard_map/ppermute | solution.py:365
  294.9 367.3 %collective-permute-start.7 = (bf16[1280,2048]{1,0:T(8,128)(2,1)}, bf16[1280,2048]{1,0:T(8,128)(2,1)}, u32[]{:S(2)}, u32[]{:S(2)}) collective-permute-start(bf16[1280,2048]{1,0:T(8,128)(2,1)} %get-tuple-element.106), channel_id=1, source_target_pairs={{0,1},{1,2},{2,3},{3,0},{4,5},{5,6},{6,7},{7,4}} | collective-permute-start | bytes 15728648 | tf_op jit(solution)/shard_map/ppermute | solution.py:365
  334.0 173.2 %collective-permute-start.6 = (bf16[2,1024,1536]{2,1,0:T(8,128)(2,1)}, bf16[2,1024,1536]{2,1,0:T(8,128)(2,1)}, u32[]{:S(2)}, u32[]{:S(2)}) collective-permute-start(bf16[2,1024,1536]{2,1,0:T(8,128)(2,1)} %pad_maximum_fusion.2), channel_id=1, source_target_pairs={{0,4},{4,0},{1,5},{5,1},{2,6},{6,2},{3,7},{7,3}} | collective-permute-start | bytes 18874376 | tf_op jit(solution)/shard_map/ppermute | solution.py:360
  389.6 231.1 %collective-permute-start.10 = (bf16[2,1024,1024]{2,1,0:T(8,128)(2,1)}, bf16[2,1024,1024]{2,1,0:T(8,128)(2,1)}, u32[]{:S(2)}, u32[]{:S(2)}) collective-permute-start(bf16[2,1024,1024]{2,1,0:T(8,128)(2,1)} %pad_maximum_fusion.7), channel_id=1, source_target_pairs={{0,4},{4,0},{1,5},{5,1},{2,6},{6,2},{3,7},{7,3}} | collective-permute-start | bytes 12582920 | tf_op jit(solution)/shard_map/ppermute | solution.py:360
  507.2 224.7 %collective-permute-start.11 = (bf16[2,1024,1536]{2,1,0:T(8,128)(2,1)}, bf16[2,1024,1536]{2,1,0:T(8,128)(2,1)}, u32[]{:S(2)}, u32[]{:S(2)}) collective-permute-start(bf16[2,1024,1536]{2,1,0:T(8,128)(2,1)} %pad_maximum_fusion.3), channel_id=1, source_target_pairs={{0,4},{4,0},{1,5},{5,1},{2,6},{6,2},{3,7},{7,3}} | collective-permute-start | bytes 18874376 | tf_op jit(solution)/shard_map/ppermute | solution.py:360
  620.7 690.7 %collective-permute-start.16 = (bf16[1280,1024]{1,0:T(8,128)(2,1)}, bf16[1280,1024]{1,0:T(8,128)(2,1)}, u32[]{:S(2)}, u32[]{:S(2)}) collective-permute-start(bf16[1280,1024]{1,0:T(8,128)(2,1)} %get-tuple-element.127), channel_id=1, source_target_pairs={{0,3},{1,0},{2,1},{3,2},{4,7},{5,4},{6,5},{7,6}} | collective-permute-start | bytes 7864328 | tf_op jit(solution)/shard_map/ppermute | solution.py:365
  659.1 685.5 %collective-permute-start.18 = (bf16[1280,1024]{1,0:T(8,128)(2,1)}, bf16[1280,1024]{1,0:T(8,128)(2,1)}, u32[]{:S(2)}, u32[]{:S(2)}) collective-permute-start(bf16[1280,1024]{1,0:T(8,128)(2,1)} %get-tuple-element.129), channel_id=1, source_target_pairs={{0,2},{1,3},{2,0},{3,1},{4,6},{5,7},{6,4},{7,5}} | collective-permute-start | bytes 7864328 | tf_op jit(solution)/shard_map/ppermute | solution.py:365
  662.0 694.3 %collective-permute-start.20 = (bf16[1280,1024]{1,0:T(8,128)(2,1)}, bf16[1280,1024]{1,0:T(8,128)(2,1)}, u32[]{:S(2)}, u32[]{:S(2)}) collective-permute-start(bf16[1280,1024]{1,0:T(8,128)(2,1)} %get-tuple-element.131), channel_id=1, source_target_pairs={{0,1},{1,2},{2,3},{3,0},{4,5},{5,6},{6,7},{7,4}} | collective-permute-start | bytes 7864328 | tf_op jit(solution)/shard_map/ppermute | solution.py:365
  662.1 204.6 %collective-permute-start.12 = (bf16[2,1024,1536]{2,1,0:T(8,128)(2,1)}, bf16[2,1024,1536]{2,1,0:T(8,128)(2,1)}, u32[]{:S(2)}, u32[]{:S(2)}) collective-permute-start(bf16[2,1024,1536]{2,1,0:T(8,128)(2,1)} %pad_maximum_fusion.4), channel_id=1, source_target_pairs={{0,4},{4,0},{1,5},{5,1},{2,6},{6,2},{3,7},{7,3}} | collective-permute-start | bytes 18874376 | tf_op jit(solution)/shard_map/ppermute | solution.py:360
  731.9 269.6 %collective-permute-start.13 = (bf16[2,1024,1536]{2,1,0:T(8,128)(2,1)}, bf16[2,1024,1536]{2,1,0:T(8,128)(2,1)}, u32[]{:S(2)}, u32[]{:S(2)}) collective-permute-start(bf16[2,1024,1536]{2,1,0:T(8,128)(2,1)} %pad_maximum_fusion.5), channel_id=1, source_target_pairs={{0,4},{4,0},{1,5},{5,1},{2,6},{6,2},{3,7},{7,3}} | collective-permute-start | bytes 18874376 | tf_op jit(solution)/shard_map/ppermute | solution.py:360
  866.7 258.4 %collective-permute-start.14 = (bf16[5632,512]{1,0:T(8,128)(2,1)}, bf16[5632,512]{1,0:T(8,128)(2,1)}, u32[]{:S(2)}, u32[]{:S(2)}) collective-permute-start(bf16[5632,512]{1,0:T(8,128)(2,1)} %get-tuple-element.121), channel_id=1, source_target_pairs={{0,4},{4,0},{1,5},{5,1},{2,6},{6,2},{3,7},{7,3}} | collective-permute-start | bytes 17301512 | tf_op jit(solution)/shard_map/ppermute | solution.py:360
  1001.5 308.4 %collective-permute-start.15 = (bf16[5632,512]{1,0:T(8,128)(2,1)}, bf16[5632,512]{1,0:T(8,128)(2,1)}, u32[]{:S(2)}, u32[]{:S(2)}) collective-permute-start(bf16[5632,512]{1,0:T(8,128)(2,1)} %get-tuple-element.124), channel_id=1, source_target_pairs={{0,4},{4,0},{1,5},{5,1},{2,6},{6,2},{3,7},{7,3}} | collective-permute-start | bytes 17301512 | tf_op jit(solution)/shard_map/ppermute | solution.py:360
  1125.1 184.5 %collective-permute-start.22 = (bf16[5632,256]{1,0:T(8,128)(2,1)}, bf16[5632,256]{1,0:T(8,128)(2,1)}, u32[]{:S(2)}, u32[]{:S(2)}) collective-permute-start(bf16[5632,256]{1,0:T(8,128)(2,1)} %get-tuple-element.134), channel_id=1, source_target_pairs={{0,4},{4,0},{1,5},{5,1},{2,6},{6,2},{3,7},{7,3}} | collective-permute-start | bytes 8650760 | tf_op jit(solution)/shard_map/ppermute | solution.py:360
  1309.7 56.9 %collective-permute-start.17 = (bf16[1280,1024]{1,0:T(8,128)(2,1)}, bf16[1280,1024]{1,0:T(8,128)(2,1)}, u32[]{:S(2)}, u32[]{:S(2)}) collective-permute-start(bf16[1280,1024]{1,0:T(8,128)(2,1)} %get-tuple-element.128), channel_id=1, source_target_pairs={{0,3},{1,0},{2,1},{3,2},{4,7},{5,4},{6,5},{7,6}} | collective-permute-start | bytes 7864328 | tf_op jit(solution)/shard_map/ppermute | solution.py:365
  1310.0 115.6 %collective-permute-start.19 = (bf16[1280,1024]{1,0:T(8,128)(2,1)}, bf16[1280,1024]{1,0:T(8,128)(2,1)}, u32[]{:S(2)}, u32[]{:S(2)}) collective-permute-start(bf16[1280,1024]{1,0:T(8,128)(2,1)} %get-tuple-element.130), channel_id=1, source_target_pairs={{0,2},{1,3},{2,0},{3,1},{4,6},{5,7},{6,4},{7,5}} | collective-permute-start | bytes 7864328 | tf_op jit(solution)/shard_map/ppermute | solution.py:365
  1311.4 115.6 %collective-permute-start.21 = (bf16[1280,1024]{1,0:T(8,128)(2,1)}, bf16[1280,1024]{1,0:T(8,128)(2,1)}, u32[]{:S(2)}, u32[]{:S(2)}) collective-permute-start(bf16[1280,1024]{1,0:T(8,128)(2,1)} %get-tuple-element.132), channel_id=1, source_target_pairs={{0,1},{1,2},{2,3},{3,0},{4,5},{5,6},{6,7},{7,4}} | collective-permute-start | bytes 7864328 | tf_op jit(solution)/shard_map/ppermute | solution.py:365
  1344.6 175.8 %collective-permute-start.24 = (bf16[1280,512]{1,0:T(8,128)(2,1)}, bf16[1280,512]{1,0:T(8,128)(2,1)}, u32[]{:S(2)}, u32[]{:S(2)}) collective-permute-start(bf16[1280,512]{1,0:T(8,128)(2,1)} %get-tuple-element.140), channel_id=1, source_target_pairs={{0,3},{1,0},{2,1},{3,2},{4,7},{5,4},{6,5},{7,6}} | collective-permute-start | bytes 3932168 | tf_op jit(solution)/shard_map/ppermute | solution.py:365
  1356.2 164.5 %collective-permute-start.26 = (bf16[1280,512]{1,0:T(8,128)(2,1)}, bf16[1280,512]{1,0:T(8,128)(2,1)}, u32[]{:S(2)}, u32[]{:S(2)}) collective-permute-start(bf16[1280,512]{1,0:T(8,128)(2,1)} %get-tuple-element.142), channel_id=1, source_target_pairs={{0,2},{1,3},{2,0},{3,1},{4,6},{5,7},{6,4},{7,5}} | collective-permute-start | bytes 3932168 | tf_op jit(solution)/shard_map/ppermute | solution.py:365
  1366.6 106.0 %copy-start.15 = (s32[4,1]{0,1:T(1,128)S(1)}, s32[4,1]{0,1:T(1,128)}, u32[]{:S(2)}) copy-start(s32[4,1]{0,1:T(1,128)} %copy-done.14) | copy-start | bytes 52
  1366.6 180.2 %collective-permute-start.28 = (bf16[1280,512]{1,0:T(8,128)(2,1)}, bf16[1280,512]{1,0:T(8,128)(2,1)}, u32[]{:S(2)}, u32[]{:S(2)}) collective-permute-start(bf16[1280,512]{1,0:T(8,128)(2,1)} %get-tuple-element.144), channel_id=1, source_target_pairs={{0,1},{1,2},{2,3},{3,0},{4,5},{5,6},{6,7},{7,4}} | collective-permute-start | bytes 3932168 | tf_op jit(solution)/shard_map/ppermute | solution.py:365
  1425.6 194.3 %collective-permute-start.30 = (bf16[5632,256]{1,0:T(8,128)(2,1)}, bf16[5632,256]{1,0:T(8,128)(2,1)}, u32[]{:S(2)}, u32[]{:S(2)}) collective-permute-start(bf16[5632,256]{1,0:T(8,128)(2,1)} %get-tuple-element.149), channel_id=1, source_target_pairs={{0,4},{4,0},{1,5},{5,1},{2,6},{6,2},{3,7},{7,3}} | collective-permute-start | bytes 8650760 | tf_op jit(solution)/shard_map/ppermute | solution.py:360
  1427.0 93.4 %collective-permute-start.23 = (bf16[5632,256]{1,0:T(8,128)(2,1)}, bf16[5632,256]{1,0:T(8,128)(2,1)}, u32[]{:S(2)}, u32[]{:S(2)}) collective-permute-start(bf16[5632,256]{1,0:T(8,128)(2,1)} %get-tuple-element.137), channel_id=1, source_target_pairs={{0,4},{4,0},{1,5},{5,1},{2,6},{6,2},{3,7},{7,3}} | collective-permute-start | bytes 8650760 | tf_op jit(solution)/shard_map/ppermute | solution.py:360
  1520.4 35.7 %collective-permute-start.25 = (bf16[1280,512]{1,0:T(8,128)(2,1)}, bf16[1280,512]{1,0:T(8,128)(2,1)}, u32[]{:S(2)}, u32[]{:S(2)}) collective-permute-start(bf16[1280,512]{1,0:T(8,128)(2,1)} %get-tuple-element.141), channel_id=1, source_target_pairs={{0,3},{1,0},{2,1},{3,2},{4,7},{5,4},{6,5},{7,6}} | collective-permute-start | bytes 3932168 | tf_op jit(solution)/shard_map/ppermute | solution.py:365
  1520.4 57.6 %collective-permute-start.27 = (bf16[1280,512]{1,0:T(8,128)(2,1)}, bf16[1280,512]{1,0:T(8,128)(2,1)}, u32[]{:S(2)}, u32[]{:S(2)}) collective-permute-start(bf16[1280,512]{1,0:T(8,128)(2,1)} %get-tuple-element.143), channel_id=1, source_target_pairs={{0,2},{1,3},{2,0},{3,1},{4,6},{5,7},{6,4},{7,5}} | collective-permute-start | bytes 3932168 | tf_op jit(solution)/shard_map/ppermute | solution.py:365
  1520.7 59.3 %collective-permute-start.29 = (bf16[1280,512]{1,0:T(8,128)(2,1)}, bf16[1280,512]{1,0:T(8,128)(2,1)}, u32[]{:S(2)}, u32[]{:S(2)}) collective-permute-start(bf16[1280,512]{1,0:T(8,128)(2,1)} %get-tuple-element.145), channel_id=1, source_target_pairs={{0,1},{1,2},{2,3},{3,0},{4,5},{5,6},{6,7},{7,4}} | collective-permute-start | bytes 3932168 | tf_op jit(solution)/shard_map/ppermute | solution.py:365
  1546.8 71.1 %collective-permute-start.31 = (bf16[1280,256]{1,0:T(8,128)(2,1)}, bf16[1280,256]{1,0:T(8,128)(2,1)S(1)}, u32[]{:S(2)}, u32[]{:S(2)}) collective-permute-start(bf16[1280,256]{1,0:T(8,128)(2,1)} %get-tuple-element.152), channel_id=1, source_target_pairs={{0,3},{1,0},{2,1},{3,2},{4,7},{5,4},{6,5},{7,6}} | collective-permute-start | bytes 1966088 | tf_op jit(solution)/shard_map/ppermute | solution.py:365
  1556.1 61.9 %collective-permute-start.33 = (bf16[1280,256]{1,0:T(8,128)(2,1)}, bf16[1280,256]{1,0:T(8,128)(2,1)}, u32[]{:S(2)}, u32[]{:S(2)}) collective-permute-start(bf16[1280,256]{1,0:T(8,128)(2,1)} %get-tuple-element.154), channel_id=1, source_target_pairs={{0,2},{1,3},{2,0},{3,1},{4,6},{5,7},{6,4},{7,5}} | collective-permute-start | bytes 1966088 | tf_op jit(solution)/shard_map/ppermute | solution.py:365
  1578.0 67.8 %collective-permute-start.35 = (bf16[1280,256]{1,0:T(8,128)(2,1)}, bf16[1280,256]{1,0:T(8,128)(2,1)}, u32[]{:S(2)}, u32[]{:S(2)}) collective-permute-start(bf16[1280,256]{1,0:T(8,128)(2,1)} %get-tuple-element.156), channel_id=1, source_target_pairs={{0,1},{1,2},{2,3},{3,0},{4,5},{5,6},{6,7},{7,4}} | collective-permute-start | bytes 1966088 | tf_op jit(solution)/shard_map/ppermute | solution.py:365
  1580.0 106.8 %collective-permute-start.37 = (bf16[5632,256]{1,0:T(8,128)(2,1)}, bf16[5632,256]{1,0:T(8,128)(2,1)}, u32[]{:S(2)}, u32[]{:S(2)}) collective-permute-start(bf16[5632,256]{1,0:T(8,128)(2,1)} %get-tuple-element.160), channel_id=1, source_target_pairs={{0,4},{4,0},{1,5},{5,1},{2,6},{6,2},{3,7},{7,3}} | collective-permute-start | bytes 8650760 | tf_op jit(solution)/shard_map/ppermute | solution.py:360
  1618.0 27.8 %copy-start.10 = (bf16[1280,256]{1,0:T(8,128)(2,1)}, bf16[1280,256]{1,0:T(8,128)(2,1)S(1)}, u32[]{:S(2)}) copy-start(bf16[1280,256]{1,0:T(8,128)(2,1)S(1)} %collective-permute-done.31.refs_2_) | copy-start | bytes 1966084
  1618.0 37.3 %collective-permute-start.32 = (bf16[1280,256]{1,0:T(8,128)(2,1)}, bf16[1280,256]{1,0:T(8,128)(2,1)}, u32[]{:S(2)}, u32[]{:S(2)}) collective-permute-start(bf16[1280,256]{1,0:T(8,128)(2,1)} %get-tuple-element.153), channel_id=1, source_target_pairs={{0,3},{1,0},{2,1},{3,2},{4,7},{5,4},{6,5},{7,6}} | collective-permute-start | bytes 1966088 | tf_op jit(solution)/shard_map/ppermute | solution.py:365
  1618.0 37.3 %collective-permute-start.34 = (bf16[1280,256]{1,0:T(8,128)(2,1)}, bf16[1280,256]{1,0:T(8,128)(2,1)}, u32[]{:S(2)}, u32[]{:S(2)}) collective-permute-start(bf16[1280,256]{1,0:T(8,128)(2,1)} %get-tuple-element.155), channel_id=1, source_target_pairs={{0,2},{1,3},{2,0},{3,1},{4,6},{5,7},{6,4},{7,5}} | collective-permute-start | bytes 1966088 | tf_op jit(solution)/shard_map/ppermute | solution.py:365
  1619.8 35.6 %collective-permute-start.36 = (bf16[1280,256]{1,0:T(8,128)(2,1)}, bf16[1280,256]{1,0:T(8,128)(2,1)}, u32[]{:S(2)}, u32[]{:S(2)}) collective-permute-start(bf16[1280,256]{1,0:T(8,128)(2,1)} %get-tuple-element.157), channel_id=1, source_target_pairs={{0,1},{1,2},{2,3},{3,0},{4,5},{5,6},{6,7},{7,4}} | collective-permute-start | bytes 1966088 | tf_op jit(solution)/shard_map/ppermute | solution.py:365
  1645.8 76.3 %collective-permute-start.38 = (bf16[1280,256]{1,0:T(8,128)(2,1)}, bf16[1280,256]{1,0:T(8,128)(2,1)S(1)}, u32[]{:S(2)}, u32[]{:S(2)}) collective-permute-start(bf16[1280,256]{1,0:T(8,128)(2,1)} %get-tuple-element.163), channel_id=1, source_target_pairs={{0,3},{1,0},{2,1},{3,2},{4,7},{5,4},{6,5},{7,6}} | collective-permute-start | bytes 1966088 | tf_op jit(solution)/shard_map/ppermute | solution.py:365
  1655.3 67.0 %collective-permute-start.40 = (bf16[1280,256]{1,0:T(8,128)(2,1)}, bf16[1280,256]{1,0:T(8,128)(2,1)}, u32[]{:S(2)}, u32[]{:S(2)}) collective-permute-start(bf16[1280,256]{1,0:T(8,128)(2,1)} %get-tuple-element.165), channel_id=1, source_target_pairs={{0,2},{1,3},{2,0},{3,1},{4,6},{5,7},{6,4},{7,5}} | collective-permute-start | bytes 1966088 | tf_op jit(solution)/shard_map/ppermute | solution.py:365
  1655.3 66.9 %collective-permute-start.42 = (bf16[1280,256]{1,0:T(8,128)(2,1)}, bf16[1280,256]{1,0:T(8,128)(2,1)}, u32[]{:S(2)}, u32[]{:S(2)}) collective-permute-start(bf16[1280,256]{1,0:T(8,128)(2,1)} %get-tuple-element.167), channel_id=1, source_target_pairs={{0,1},{1,2},{2,3},{3,0},{4,5},{5,6},{6,7},{7,4}} | collective-permute-start | bytes 1966088 | tf_op jit(solution)/shard_map/ppermute | solution.py:365
  1655.5 30.2 %copy-start.17 = (s32[4,1]{0,1:T(1,128)S(1)}, s32[4,1]{0,1:T(1,128)}, u32[]{:S(2)}) copy-start(s32[4,1]{0,1:T(1,128)} %copy-done.16) | copy-start | bytes 52
  1712.7 24.8 %collective-permute-start.39 = (bf16[1280,256]{1,0:T(8,128)(2,1)}, bf16[1280,256]{1,0:T(8,128)(2,1)}, u32[]{:S(2)}, u32[]{:S(2)}) collective-permute-start(bf16[1280,256]{1,0:T(8,128)(2,1)} %get-tuple-element.164), channel_id=1, source_target_pairs={{0,3},{1,0},{2,1},{3,2},{4,7},{5,4},{6,5},{7,6}} | collective-permute-start | bytes 1966088 | tf_op jit(solution)/shard_map/ppermute | solution.py:365
  1722.1 28.9 %collective-permute-start.41 = (bf16[1280,256]{1,0:T(8,128)(2,1)}, bf16[1280,256]{1,0:T(8,128)(2,1)}, u32[]{:S(2)}, u32[]{:S(2)}) collective-permute-start(bf16[1280,256]{1,0:T(8,128)(2,1)} %get-tuple-element.166), channel_id=1, source_target_pairs={{0,2},{1,3},{2,0},{3,1},{4,6},{5,7},{6,4},{7,5}} | collective-permute-start | bytes 1966088 | tf_op jit(solution)/shard_map/ppermute | solution.py:365
  1722.1 28.9 %copy-start.9 = (bf16[1280,256]{1,0:T(8,128)(2,1)}, bf16[1280,256]{1,0:T(8,128)(2,1)S(1)}, u32[]{:S(2)}) copy-start(bf16[1280,256]{1,0:T(8,128)(2,1)S(1)} %collective-permute-done.38.refs_2_) | copy-start | bytes 1966084
  1722.1 28.9 %collective-permute-start.43 = (bf16[1280,256]{1,0:T(8,128)(2,1)}, bf16[1280,256]{1,0:T(8,128)(2,1)}, u32[]{:S(2)}, u32[]{:S(2)}) collective-permute-start(bf16[1280,256]{1,0:T(8,128)(2,1)} %get-tuple-element.168), channel_id=1, source_target_pairs={{0,1},{1,2},{2,3},{3,0},{4,5},{5,6},{6,7},{7,4}} | collective-permute-start | bytes 1966088 | tf_op jit(solution)/shard_map/ppermute | solution.py:365
  (15 other events, 84.2 us)

commit v2 on v1

v2 whole, which is shorter than its diff:
```python
import functools

import jax
import jax.numpy as jnp
from jax import lax
from jax.experimental import pallas as pl
from jax.experimental.pallas import tpu as pltpu
from jax.sharding import PartitionSpec as P


BF16 = jnp.bfloat16
F32 = jnp.float32
I32 = jnp.int32
VMEM_LIMIT = 66_000_000

TILE = 256
TOK_BLOCK = 256
MIX_TILE = 128
MIX_UNROLL = 4
ALIGN = 16
REACH = 512
DEEP = 4
SUB = 512
WIDE_CHUNKS = (512, 1536, 1536, 2048)
DOWN_PIECES = ((0, 0, 512), (1, 0, 512), (0, 512, 256), (1, 512, 256), (0, 768, 256), (1, 768, 128), (1, 896, 128))


def capacity_rows(tok_rows, top_k, n_exp):
    return max(8, ((5 * top_k * tok_rows) // (4 * n_exp) + 7) // 8 * 8)


def after(value, *earlier):
    return lax.optimization_barrier((value, earlier))[0]


def any_spec():
    return pl.BlockSpec(memory_space=pl.ANY)


def pack_body(n_local, local, n_blk, n_group, first_ref, slot_ref, x_ref, *refs):
    out_refs, acc_ref = refs[:n_group], refs[n_group]
    e, s = pl.program_id(0) * n_local + local, pl.program_id(1)
    count = first_ref[e * (n_blk + 1) + n_blk]
    base = s * TILE

    @pl.when(base < count)
    def _():
        end = jnp.minimum(base + TILE, count)
        lo = jnp.int32(0)
        hi = jnp.int32(0)
        for i in range(n_blk):
            lo += (first_ref[e * (n_blk + 1) + i + 1] <= base).astype(I32)
            hi += (first_ref[e * (n_blk + 1) + i] < end).astype(I32)
        acc_ref[...] = jnp.zeros_like(acc_ref)
        slots = base + lax.broadcasted_iota(I32, (TILE, TOK_BLOCK), 0)

        def visit(i, carry):
            off = pl.multiple_of(i * TOK_BLOCK, TOK_BLOCK)
            pick = (slots == slot_ref[pl.ds(e, 1), pl.ds(off, TOK_BLOCK)]).astype(F32).astype(BF16)
            acc_ref[...] += jnp.dot(pick, x_ref[pl.ds(off, TOK_BLOCK), :], preferred_element_type=F32)
            return carry

        lax.fori_loop(lo, hi, visit, 0)
        for d in range(n_group):

            @pl.when(pl.program_id(0) == d)
            def _():
                out_refs[d][...] = acc_ref[...].astype(BF16)


def pack_rows(first_blk, x_loc, slot_te, n_exp, n_local, local, capacity):
    tok_rows, d_model = x_loc.shape
    n_blk = tok_rows // TOK_BLOCK
    n_group = n_exp // n_local

    def out_spec(d):
        def index(p, s, first):
            used = (first[(d * n_local + local) * (n_blk + 1) + n_blk] + TILE - 1) // TILE
            last = jnp.maximum(used - 1, 0)
            return jnp.where(p < d, 0, jnp.where(p > d, last, jnp.minimum(s, last))), 0

        return pl.BlockSpec((TILE, d_model), index)

    return pl.pallas_call(
        functools.partial(pack_body, n_local, local, n_blk, n_group),
        grid_spec=pltpu.PrefetchScalarGridSpec(
            num_scalar_prefetch=1,
            grid=(n_group, capacity // TILE),
            in_specs=[
                pl.BlockSpec((n_exp, tok_rows), lambda p, s, f: (0, 0)),
                pl.BlockSpec((tok_rows, d_model), lambda p, s, f: (0, 0)),
            ],
            out_specs=[out_spec(d) for d in range(n_group)],
            scratch_shapes=[pltpu.VMEM((TILE, d_model), F32)],
        ),
        out_shape=[jax.ShapeDtypeStruct((capacity, d_model), BF16)] * n_group,
        compiler_params=pltpu.CompilerParams(vmem_limit_bytes=VMEM_LIMIT),
        cost_estimate=pl.CostEstimate(flops=20_000_000_000, bytes_accessed=60_000_000, transcendentals=0),
        name="pack_rows",
    )(first_blk, slot_te, x_loc)


def smem():
    return pl.BlockSpec(memory_space=pltpu.SMEM)


def tile_at(i):
    return pl.ds(pl.multiple_of(i * TILE, TILE), TILE)


def wide_body(n_group, local, lo_col, cols, meta_ref, *refs):
    x_refs = refs[:n_group]
    wg_ref, wu_ref, far_ref = refs[n_group : n_group + 3]
    h_ref, rows_buf, h_buf, gate_w, up_w, row_sems, h_sems, sems = refs[-8:]
    side = meta_ref[0]
    half = wg_ref.shape[1]
    n_live = meta_ref[1 + n_group]

    def fetch(i):
        for d in range(n_group):

            @pl.when((i >= meta_ref[1 + d]) & (i < meta_ref[2 + d]))
            def _():
                pltpu.make_async_copy(x_refs[d].at[tile_at(i - meta_ref[1 + d]), :], rows_buf.at[i % 2], row_sems.at[i % 2]).start()

    def send(i):
        return pltpu.make_async_copy(h_buf.at[i % 2], h_ref.at[tile_at(i), pl.ds(lo_col, cols)], h_sems.at[i % 2])

    fetch(0)
    near = pl.ds(pl.multiple_of(side * half, half), half)
    far = pl.ds(pl.multiple_of((1 - side) * half, half), half)
    copies = [
        pltpu.make_async_copy(wg_ref.at[local, :, pl.ds(lo_col, cols)], gate_w.at[near, :], sems.at[0]),
        pltpu.make_async_copy(wu_ref.at[local, :, pl.ds(lo_col, cols)], up_w.at[near, :], sems.at[1]),
        pltpu.make_async_copy(far_ref.at[0], gate_w.at[far, :], sems.at[2]),
        pltpu.make_async_copy(far_ref.at[1], up_w.at[far, :], sems.at[3]),
    ]
    for copy in copies:
        copy.start()
    for copy in copies:
        copy.wait()

    def step(i, carry):
        fetch(i + 1)
        pltpu.make_async_copy(x_refs[0].at[tile_at(0), :], rows_buf.at[i % 2], row_sems.at[i % 2]).wait()

        @pl.when(i >= 2)
        def _():
            send(i - 2).wait()

        rows = rows_buf[i % 2]
        for j in range(0, cols, SUB):
            g = jnp.dot(rows, gate_w[:, j : j + SUB], preferred_element_type=F32)
            u = jnp.dot(rows, up_w[:, j : j + SUB], preferred_element_type=F32)
            h_buf[i % 2, :, j : j + SUB] = (jax.nn.silu(g) * u).astype(BF16)
        send(i).start()
        return carry

    lax.fori_loop(0, n_live, step, 0)
    for back in (2, 1):

        @pl.when(n_live >= back)
        def _():
            send(n_live - back).wait()


def wide_part(meta, hidden, rows, w_gate, w_up, far, local, lo_col, cols):
    n_group = len(rows)
    capacity, d_model = rows[0].shape
    n_rows = n_group * capacity
    ffn = w_gate.shape[2]
    args = [meta, *rows, w_gate, w_up, far]
    alias = {}
    if hidden is not None:
        alias = {len(args): 0}
        args.append(hidden)
    return pl.pallas_call(
        functools.partial(wide_body, n_group, local, lo_col, cols),
        in_specs=[smem()] + [any_spec()] * (len(args) - 1),
        out_specs=any_spec(),
        scratch_shapes=[
            pltpu.VMEM((2, TILE, d_model), BF16),
            pltpu.VMEM((2, TILE, cols), BF16),
            pltpu.VMEM((d_model, cols), BF16),
            pltpu.VMEM((d_model, cols), BF16),
            pltpu.SemaphoreType.DMA((2,)),
            pltpu.SemaphoreType.DMA((2,)),
            pltpu.SemaphoreType.DMA((4,)),
        ],
        out_shape=jax.ShapeDtypeStruct((n_rows, ffn), BF16),
        input_output_aliases=alias,
        compiler_params=pltpu.CompilerParams(vmem_limit_bytes=VMEM_LIMIT),
        cost_estimate=pl.CostEstimate(flops=4 * n_rows * d_model * cols, bytes_accessed=n_rows * d_model * 2, transcendentals=0),
        name="wide_part",
    )(*args)


def down_body(n_group, local, meta_ref, h_ref, w_ref, *refs):
    out_refs = refs[:n_group]
    h_buf, out_buf, w_buf, h_sems, out_sems, sem = refs[n_group:]
    n_live = meta_ref[1 + n_group]

    def fetch(i):
        return pltpu.make_async_copy(h_ref.at[tile_at(i), :], h_buf.at[i % DEEP], h_sems.at[i % DEEP])

    def sent(i):
        pltpu.make_async_copy(out_buf.at[i % 2], out_refs[0].at[tile_at(0), :], out_sems.at[i % 2]).wait()

    for i in range(DEEP - 1):

        @pl.when(i < n_live)
        def _():
            fetch(i).start()

    copy = pltpu.make_async_copy(w_ref if local is None else w_ref.at[local], w_buf, sem)
    copy.start()
    copy.wait()

    def step(i, carry):
        @pl.when(i + DEEP - 1 < n_live)
        def _():
            fetch(i + DEEP - 1).start()

        fetch(i).wait()

        @pl.when(i >= 2)
        def _():
            sent(i)

        out_buf[i % 2] = jnp.dot(h_buf[i % DEEP], w_buf[...], preferred_element_type=F32).astype(BF16)
        for d in range(n_group):

            @pl.when((i >= meta_ref[1 + d]) & (i < meta_ref[2 + d]))
            def _():
                pltpu.make_async_copy(out_buf.at[i % 2], out_refs[d].at[tile_at(i - meta_ref[1 + d]), :], out_sems.at[i % 2]).start()

        return carry

    lax.fori_loop(0, n_live, step, 0)
    for back in (2, 1):

        @pl.when(n_live >= back)
        def _():
            sent(n_live - back)

    for d in range(n_group):
        @pl.when(meta_ref[1 + d] == meta_ref[2 + d])
        def _():
            out_buf[0] = jnp.zeros_like(out_buf[0])
            blank = pltpu.make_async_copy(out_buf.at[0], out_refs[d].at[tile_at(0), :], out_sems.at[0])
            blank.start()
            blank.wait()


def down_part(meta, hidden, weight, n_group, local=None):
    n_rows = hidden.shape[0]
    ffn, width = weight.shape[-2:]
    return pl.pallas_call(
        functools.partial(down_body, n_group, local),
        in_specs=[smem(), any_spec(), any_spec()],
        out_specs=[any_spec()] * n_group,
        scratch_shapes=[
            pltpu.VMEM((DEEP, TILE, ffn), BF16),
            pltpu.VMEM((2, TILE, width), BF16),
            pltpu.VMEM((ffn, width), BF16),
            pltpu.SemaphoreType.DMA((DEEP,)),
            pltpu.SemaphoreType.DMA((2,)),
            pltpu.SemaphoreType.DMA,
        ],
        out_shape=[jax.ShapeDtypeStruct((n_rows // n_group, width), BF16)] * n_group,
        compiler_params=pltpu.CompilerParams(vmem_limit_bytes=VMEM_LIMIT),
        cost_estimate=pl.CostEstimate(flops=2 * n_rows * ffn * width, bytes_accessed=n_rows * ffn * 2, transcendentals=0),
        name="down_part",
    )(meta, hidden, weight)


def mix_body(n_exp, n_tile, subs, col_ref, chunk_ref, pos_ref, gate_ref, x_ref, *refs):
    back_refs = refs[:n_exp]
    y_ref, mark_ref, back_buf, near_buf, x_buf, y_buf, sems = refs[-7:]
    width = x_buf.shape[1]
    capacity = back_refs[0].shape[0]
    cols = pl.ds(pl.multiple_of(col_ref[0], 128), width)
    copies = [
        pltpu.make_async_copy(ref.at[:, pl.ds(sub * width, width)], back_buf.at[pl.ds(e * capacity, capacity), :], sems.at[e])
        for e, (ref, sub) in enumerate(zip(back_refs, subs))
    ]
    copies.append(pltpu.make_async_copy(x_ref.at[:, cols], x_buf, sems.at[n_exp]))
    for copy in copies:
        copy.start()
    for copy in copies:
        copy.wait()

    def step(block, carry):
        for k in range(MIX_UNROLL):
            i = block * MIX_UNROLL + k
            tokens = pl.ds(pl.multiple_of(i * MIX_TILE, MIX_TILE), MIX_TILE)
            for c in range(REACH // ALIGN):
                chunk = pl.multiple_of(chunk_ref[i * (REACH // ALIGN) + c], ALIGN)
                near_buf[k, c * ALIGN : (c + 1) * ALIGN, :] = back_buf[pl.ds(chunk, ALIGN), :]
            seat = lax.broadcasted_iota(I32, (MIX_TILE, REACH), 1)
            pick = jnp.concatenate([(seat == pos_ref[tokens, j : j + 1]).astype(F32).astype(BF16) for j in range(2)], axis=0)
            found = jnp.dot(pick, near_buf[k], preferred_element_type=F32)
            mixed = gate_ref[tokens, 0:1] * found[:MIX_TILE] + gate_ref[tokens, 1:2] * found[MIX_TILE:]
            y_buf[tokens, :] = (x_buf[tokens, :].astype(F32) + mixed).astype(BF16)
        return carry

    lax.fori_loop(0, n_tile // MIX_UNROLL, step, 0)
    out = pltpu.make_async_copy(y_buf, y_ref.at[:, cols], sems.at[0])
    out.start()
    out.wait()
    mark_ref[0] = 0


def mix_cols(col, y_loc, x_loc, pos, gate_loc, chunks, width, back):
    tok_rows, d_model = x_loc.shape
    n_exp = len(back)
    capacity = back[0][0].shape[0]
    vmem = pl.BlockSpec(memory_space=pltpu.VMEM)
    args = [col, chunks, pos, gate_loc, x_loc, *[array for array, _ in back]]
    specs = [smem(), smem(), vmem, vmem, any_spec()] + [any_spec()] * n_exp
    alias = {}
    if y_loc is not None:
        alias = {len(args): 0}
        args.append(y_loc)
        specs.append(any_spec())
    return pl.pallas_call(
        functools.partial(mix_body, n_exp, tok_rows // MIX_TILE, tuple(sub for _, sub in back)),
        in_specs=specs,
        out_specs=[any_spec(), smem()],
        scratch_shapes=[
            pltpu.VMEM((n_exp * capacity, width), BF16),
            pltpu.VMEM((MIX_UNROLL, REACH, width), BF16),
            pltpu.VMEM((tok_rows, width), BF16),
            pltpu.VMEM((tok_rows, width), BF16),
            pltpu.SemaphoreType.DMA((n_exp + 1,)),
        ],
        out_shape=[jax.ShapeDtypeStruct((tok_rows, d_model), BF16), jax.ShapeDtypeStruct((1,), I32)],
        input_output_aliases=alias,
        compiler_params=pltpu.CompilerParams(vmem_limit_bytes=VMEM_LIMIT),
        cost_estimate=pl.CostEstimate(flops=20_000_000 * width, bytes_accessed=20_000 * width, transcendentals=0),
        name="mix_cols",
    )(*args)


def spans(sizes):
    lo = 0
    for size in sizes:
        yield lo, size
        lo += size


def solution(mesh):
    n_group, n_side = mesh.shape["expert"], mesh.shape["data"]
    tok_spec = P(("rep", "expert", "data"), None)
    wide_spec = P("expert", "data", None)
    down_spec = P("expert", None, "data")
    swap = [(s, 1 - s) for s in range(n_side)]

    def whole_step(x_loc, idx_loc, gate_loc, wg_loc, wu_loc, wd_loc):
        tok_rows, _ = x_loc.shape
        top_k = idx_loc.shape[1]
        n_local, half, _ = wg_loc.shape
        n_exp = n_local * n_group
        capacity = capacity_rows(tok_rows, top_k, n_exp)
        side = lax.axis_index("data")
        place = lax.axis_index("expert")
        locals_ = range(n_local)
        groups = jnp.arange(n_group, dtype=I32)

        ids = ((idx_loc // n_local + n_group - place) % n_group * n_local + idx_loc % n_local).T
        experts = jnp.arange(n_exp, dtype=I32)[:, None]
        chosen = functools.reduce(jnp.logical_or, [ids[j][None, :] == experts for j in range(top_k)])
        chosen_i = chosen.astype(I32)
        running = jnp.cumsum(chosen_i, axis=1)
        before = running - chosen_i
        slot_te = jnp.where(chosen & (before < capacity), before, -1)
        counts = jnp.minimum(running[:, -1], capacity)
        first = jnp.minimum(before, capacity)
        first_blk = jnp.concatenate([first[:, ::TOK_BLOCK], counts[:, None]], axis=1).reshape(-1)
        first_mix = first[:, ::MIX_TILE]

        table = lax.all_gather(counts, "expert")
        meta = []
        for l in locals_:
            mine = jnp.sum(jnp.where(((place - groups) % n_group)[:, None, None] == groups[None, :, None], table.reshape(n_group, n_group, n_local)[None, :, :, l] * (groups[:, None, None] == groups[None, None, :]), 0), axis=(1, 2))
            ends = jnp.cumsum((mine + TILE - 1) // TILE)
            meta.append(jnp.concatenate([side[None], jnp.zeros((1,), I32), ends]).astype(I32))

        reach = REACH // ALIGN
        start = first_mix // ALIGN
        stop = jnp.concatenate([first_mix[:, 1:], counts[:, None]], axis=1)
        size = jnp.where(stop > first_mix, (stop + ALIGN - 1) // ALIGN - start, 0)
        lead = jnp.cumsum(size, axis=0) - size
        at = slot_te + jnp.repeat((lead - start) * ALIGN, MIX_TILE, axis=1)
        at = jnp.where(slot_te < 0, -1, at)
        pos = jnp.stack([jnp.sum(jnp.where(ids[j][None, :] == experts, at, 0), axis=0) for j in range(top_k)], axis=1)
        seat = jnp.arange(reach, dtype=I32)[None, None, :]
        taken = (seat >= lead[:, :, None]) & (seat < (lead + size)[:, :, None])
        source = experts[:, :, None] * (capacity // ALIGN) + (start - lead)[:, :, None] + seat
        chunks = (jnp.sum(jnp.where(taken, source, 0), axis=0) * ALIGN).reshape(-1)

        done = []

        def in_turn(kernel, small, *args, follows=True):
            if done and follows:
                small = after(small, done[-1]) if done[-1].ndim else small + done[-1]
            out = kernel(small, *args)
            done.append(out[0] if isinstance(out, (list, tuple)) else out)
            return out

        wide_spans = list(spans(WIDE_CHUNKS))
        parts = [jnp.stack([w[0, :, : wide_spans[0][1]] for w in (wg_loc, wu_loc)])]
        later = after((wg_loc, wu_loc), parts[0])
        parts += [jnp.stack([w[l, :, lo : lo + n] for w in later]) for l in locals_ for lo, n in wide_spans if l or lo]
        parts += [wd_loc[l, :, lo : lo + n] for l, lo, n in DOWN_PIECES]
        far = []

        def cross():
            if len(far) == len(parts):
                return
            piece = parts[len(far)]
            if len(far) >= 2:
                piece = after(piece, far[-2])
            far.append(lax.ppermute(piece, "data", swap))

        def exchange(blocks, step):
            out = [blocks[0]]
            for d in range(1, n_group):
                out.append(lax.ppermute(blocks[d], "expert", [(s, (s + step * d) % n_group) for s in range(n_group)]))
            return out

        def mix(y_loc, col, width, back):
            col = col.astype(I32)[None]
            back = [(back[l][0][d], back[l][1]) for d in range(n_group) for l in locals_]
            out = in_turn(mix_cols, col, y_loc, x_loc, pos, gate_loc, chunks, width, back)
            done[-1] = out[1][0]
            return out[0]

        cross()
        cross()
        first_blk = after(first_blk, meta)
        rows = [exchange(in_turn(pack_rows, first_blk, x_loc, slot_te, n_exp, n_local, 0, capacity), 1)]
        cross()
        packed = in_turn(pack_rows, first_blk, x_loc, slot_te, n_exp, n_local, 1, capacity)
        cross()
        rows.append(exchange([after(block, rows[0]) for block in packed], 1))

        n_wide = len(wide_spans)
        hidden, own = [], []
        for l in locals_:
            hidden.append(None)
            for k, (lo, n) in enumerate(wide_spans):
                if l or k >= 2:
                    cross()
                hidden[l] = in_turn(wide_part, meta[l], hidden[l], rows[l], wg_loc, wu_loc, far[l * n_wide + k], l, lo, n, follows=k == 0)
            own.append(exchange(in_turn(down_part, meta[l], hidden[l], wd_loc, n_group, l, follows=False), -1))

        def far_piece(i):
            cross()
            l = DOWN_PIECES[i][0]
            return exchange(in_turn(down_part, meta[l], hidden[l], far[n_local * n_wide + i], n_group), -1)

        far_col = (1 - side) * half
        ret = [far_piece(0), far_piece(1)]
        y_loc = mix(None, side * half, half, [(own[l], 0) for l in locals_])
        ret += [far_piece(2), far_piece(3)]
        y_loc = mix(y_loc, far_col, 512, [(ret[0], 0), (ret[1], 0)])
        ret += [far_piece(4), far_piece(5), far_piece(6)]
        y_loc = mix(y_loc, far_col + 512, 256, [(ret[2], 0), (ret[3], 0)])
        y_loc = mix(y_loc, far_col + 768, 128, [(ret[4], 0), (ret[5], 0)])
        return mix(y_loc, far_col + 896, 128, [(ret[4], 1), (ret[6], 0)])

    in_specs = (tok_spec, tok_spec, tok_spec, wide_spec, wide_spec, down_spec)
    return jax.shard_map(whole_step, mesh=mesh, in_specs=in_specs, out_specs=tok_spec, check_vma=False)
```

time: 1800 us -> 1910 us (1.061)
  waiting for transfers between devices: 643 us -> 803 us
  Pallas kernels: 914 us -> 824 us
  starting transfers between devices: 114 us -> 160 us
    ppermute x14 -> x15, waiting for transfers between devices: 427 us -> 603 us  [cross(): far.append(lax.ppermute(piece, 'data', swap))]
    pallas_call x12 -> x14, Pallas kernels: 417 us -> 333 us  [the longest x9 257 us: down_part(): pl.pallas_call(functools.partial(down_body, n_group, local), in_specs=[sm...]
    ppermute x30 -> x33, starting transfers between devices: 94.7 us -> 146 us  [exchange(): lax.ppermute(blocks[d], 'expert', [(s, (s + step * d) % n_group) for s in...]
    ppermute x30 -> x33, waiting for transfers between devices: 216 us -> 200 us  [exchange(): lax.ppermute(blocks[d], 'expert', [(s, (s + step * d) % n_group) for s in...]
    another operation x12 -> x13, other arithmetic: 34.8 us -> 38.7 us  [the longest x7 34.2 us: whole_step(): jnp.stack([w[l, :, lo:lo + n] for w in later])]
  transfers between devices with their start and end apart: 44 -> 48, of which waited for: 14 -> 15; matrix products, arithmetic and copies ran while one was open for 5% -> 5% of each run, Pallas kernels for 50% -> 41%
where the time goes in v2:
time: 1910 us; the launch traced here: 1900 us
  Pallas kernels  824 us (43%)
  waiting for transfers between devices  803 us (42%)
  starting transfers between devices  160 us (8%)
  local copies, waits for them, and re-layouts  61.7 us (3%)
  other arithmetic  45.4 us (2%)
    ppermute x15, waiting for transfers between devices, cross(): far.append(lax.ppermute(piece, 'data', swap))  603 us
    pallas_call x8, Pallas kernels, wide_part(): pl.pallas_call(functools.partial(wide_body, n_group, local, lo_col, cols)...  406 us
    pallas_call x9, Pallas kernels, down_part(): pl.pallas_call(functools.partial(down_body, n_group, local), in_specs=[sm...  257 us
    ppermute x33, waiting for transfers between devices, exchange(): lax.ppermute(blocks[d], 'expert', [(s, (s + step * d) % n_group) for s in...  200 us
    ppermute x33, starting transfers between devices, exchange(): lax.ppermute(blocks[d], 'expert', [(s, (s + step * d) % n_group) for s in...  146 us
    pallas_call x2, Pallas kernels, pack_rows(): pl.pallas_call(functools.partial(pack_body, n_local, local, n_blk, n_grou...  85.6 us
    pallas_call x5, Pallas kernels, mix_cols(): pl.pallas_call(functools.partial(mix_body, n_exp, tok_rows // MIX_TILE, t...  76.3 us
  transfers between devices with their start and end apart: 48, of which 15 were waited for; matrix products, arithmetic and copies ran while one was open for 5% of the time, Pallas kernels for 41%

profile of v2, /device:TPU:0, one launch (start us, length us, event | category | flops | bytes accessed | tf_op | source)
XLA Modules:
  0.0 1904.1 jit_solution(18410876382874558275)
XLA Ops:
  6.4 6.7 all-reduce
  17.1 40.3 %pack_rows.2 = (bf16[1280,2048]{1,0:T(8,128)(2,1)}, bf16[1280,2048]{1,0:T(8,128)(2,1)}, bf16[1280,2048]{1,0:T(8,128)(2,1)}, bf16[1280,2048]{1,0:T(8,128)(2,1)}) custom-call(s32[136]{0:T(256)} %reshape.314.first_ref, s32[8,4096]{1,0:T(8,128)} %get-tuple-element.200.slot_ref, bf16[4096,2048]{1,0:T(8,128)(2,1)} %x_ref.13), custom_call_target="tpu_custom_call" | custom-call | flops 20000000000 | bytes 60000000 | tf_op jit(solution)/shard_map/pack_rows/pallas_call | solution.py:84
  65.8 15.6 fusion.18
  85.9 12.6 fusion.20
  98.5 6.5 slice_bitcast_fusion.2
  109.0 7.4 pad_maximum_fusion
  138.7 45.3 %pack_rows.3 = (bf16[1280,2048]{1,0:T(8,128)(2,1)}, bf16[1280,2048]{1,0:T(8,128)(2,1)}, bf16[1280,2048]{1,0:T(8,128)(2,1)}, bf16[1280,2048]{1,0:T(8,128)(2,1)}) custom-call(s32[136]{0:T(256)} %reshape.314.first_ref, s32[8,4096]{1,0:T(8,128)} %get-tuple-element.200.slot_ref, bf16[4096,2048]{1,0:T(8,128)(2,1)} %x_ref.13), custom_call_target="tpu_custom_call" | custom-call | flops 20000000000 | bytes 60000000 | tf_op jit(solution)/shard_map/pack_rows/pallas_call | solution.py:84
  192.8 9.6 slice_bitcast_fusion
  203.2 81.7 %collective-permute-done.2.refs_3_ = bf16[1280,2048]{1,0:T(8,128)(2,1)} collective-permute-done((bf16[1280,2048]{1,0:T(8,128)(2,1)}, bf16[1280,2048]{1,0:T(8,128)(2,1)}, u32[]{:S(2)}, u32[]{:S(2)}) %collective-permute-start.2) | collective-permute-done | bytes 5242912 | tf_op jit(solution)/shard_map/ppermute | solution.py:429
  287.5 22.2 %wide_part.8.refs_7_ = bf16[5120,5632]{1,0:T(8,128)(2,1)} custom-call(s32[6]{0:T(128)} %pad_add_fusion.5.meta_ref, bf16[1280,2048]{1,0:T(8,128)(2,1)} %get-tuple-element.90.refs_0_, bf16[1280,2048]{1,0:T(8,128)(2,1)} %collective-permute-done.refs_1_, bf16[1280,2048]{1,0:T(8,128)(2,1)} %collective-permute-done.1.refs_2_, ...), custom_call_target="tpu_custom_call" | custom-call | flops 21474836480 | bytes 20971520 | tf_op jit(solution)/shard_map/wide_part/pallas_call | solution.py:177
  309.8 54.8 %wide_part.9.refs_7_ = bf16[5120,5632]{1,0:T(8,128)(2,1)} custom-call(s32[6]{0:T(128)} %pad_add_fusion.5.meta_ref, bf16[1280,2048]{1,0:T(8,128)(2,1)} %get-tuple-element.90.refs_0_, bf16[1280,2048]{1,0:T(8,128)(2,1)} %collective-permute-done.refs_1_, bf16[1280,2048]{1,0:T(8,128)(2,1)} %collective-permute-done.1.refs_2_, ...), custom_call_target="tpu_custom_call", output_to_operand_aliasing={{}: (8, {})} | custom-call | flops 64424509440 | bytes 20971520 | tf_op jit(solution)/shard_map/wide_part/pallas_call | solution.py:177
  364.6 18.9 collective-permute-done.11.refs_6_
  384.3 54.7 %wide_part.10.refs_7_ = bf16[5120,5632]{1,0:T(8,128)(2,1)} custom-call(s32[6]{0:T(128)} %pad_add_fusion.5.meta_ref, bf16[1280,2048]{1,0:T(8,128)(2,1)} %get-tuple-element.90.refs_0_, bf16[1280,2048]{1,0:T(8,128)(2,1)} %collective-permute-done.refs_1_, bf16[1280,2048]{1,0:T(8,128)(2,1)} %collective-permute-done.1.refs_2_, ...), custom_call_target="tpu_custom_call", output_to_operand_aliasing={{}: (8, {})} | custom-call | flops 64424509440 | bytes 20971520 | tf_op jit(solution)/shard_map/wide_part/pallas_call | solution.py:177
  439.0 167.2 %collective-permute-done.12.refs_6_ = bf16[2,1024,512]{2,1,0:T(8,128)(2,1)} collective-permute-done((bf16[2,1024,512]{2,1,0:T(8,128)(2,1)}, bf16[2,1024,512]{2,1,0:T(8,128)(2,1)}, u32[]{:S(2)}, u32[]{:S(2)}) %collective-permute-start.12) | collective-permute-done | bytes 2097184 | tf_op jit(solution)/shard_map/ppermute | solution.py:424
  608.3 71.3 %wide_part.11.h_ref = bf16[5120,5632]{1,0:T(8,128)(2,1)} custom-call(s32[6]{0:T(128)} %pad_add_fusion.5.meta_ref, bf16[1280,2048]{1,0:T(8,128)(2,1)} %get-tuple-element.90.refs_0_, bf16[1280,2048]{1,0:T(8,128)(2,1)} %collective-permute-done.refs_1_, bf16[1280,2048]{1,0:T(8,128)(2,1)} %collective-permute-done.1.refs_2_, ...), custom_call_target="tpu_custom_call", output_to_operand_aliasing={{}: (8, {})} | custom-call | flops 85899345920 | bytes 20971520 | tf_op jit(solution)/shard_map/wide_part/pallas_call | solution.py:177
  679.6 65.4 %collective-permute-done.13.refs_6_ = bf16[2,1024,1536]{2,1,0:T(8,128)(2,1)} collective-permute-done((bf16[2,1024,1536]{2,1,0:T(8,128)(2,1)}, bf16[2,1024,1536]{2,1,0:T(8,128)(2,1)}, u32[]{:S(2)}, u32[]{:S(2)}) %collective-permute-start.13) | collective-permute-done | bytes 6291488 | tf_op jit(solution)/shard_map/ppermute | solution.py:424
  745.8 52.4 %down_part.9 = (bf16[1280,1024]{1,0:T(8,128)(2,1)}, bf16[1280,1024]{1,0:T(8,128)(2,1)}, bf16[1280,1024]{1,0:T(8,128)(2,1)}, bf16[1280,1024]{1,0:T(8,128)(2,1)}) custom-call(s32[6]{0:T(128)} %pad_add_fusion.5.meta_ref, bf16[5120,5632]{1,0:T(8,128)(2,1)} %wide_part.11.h_ref, bf16[2,5632,1024]{2,1,0:T(8,128)(2,1)} %w_ref.3), custom_call_target="tpu_custom_call" | custom-call | flops 59055800320 | bytes 57671680 | tf_op jit(solution)/shard_map/down_part/pallas_call | solution.py:258
  798.2 15.7 collective-permute-start.16
  818.7 22.0 %wide_part.12.refs_7_ = bf16[5120,5632]{1,0:T(8,128)(2,1)} custom-call(s32[6]{0:T(128)} %pad_add_fusion.3.meta_ref, bf16[1280,2048]{1,0:T(8,128)(2,1)} %get-tuple-element.96.refs_0_, bf16[1280,2048]{1,0:T(8,128)(2,1)} %collective-permute-done.3.refs_1_, bf16[1280,2048]{1,0:T(8,128)(2,1)} %collective-permute-done.4.refs_2_, ...), custom_call_target="tpu_custom_call" | custom-call | flops 21474836480 | bytes 20971520 | tf_op jit(solution)/shard_map/wide_part/pallas_call | solution.py:177
  840.7 39.1 %collective-permute-done.8.refs_6_ = bf16[2,1024,1536]{2,1,0:T(8,128)(2,1)} collective-permute-done((bf16[2,1024,1536]{2,1,0:T(8,128)(2,1)}, bf16[2,1024,1536]{2,1,0:T(8,128)(2,1)}, u32[]{:S(2)}, u32[]{:S(2)}) %collective-permute-start.8) | collective-permute-done | bytes 6291488 | tf_op jit(solution)/shard_map/ppermute | solution.py:424
  880.6 122.7 %collective-permute-done.14.w_ref = bf16[5632,512]{1,0:T(8,128)(2,1)} collective-permute-done((bf16[5632,512]{1,0:T(8,128)(2,1)}, bf16[5632,512]{1,0:T(8,128)(2,1)}, u32[]{:S(2)}, u32[]{:S(2)}) %collective-permute-start.14) | collective-permute-done | bytes 5767200 | tf_op jit(solution)/shard_map/ppermute | solution.py:424
  1004.2 54.8 %wide_part.13.refs_7_ = bf16[5120,5632]{1,0:T(8,128)(2,1)} custom-call(s32[6]{0:T(128)} %pad_add_fusion.3.meta_ref, bf16[1280,2048]{1,0:T(8,128)(2,1)} %get-tuple-element.96.refs_0_, bf16[1280,2048]{1,0:T(8,128)(2,1)} %collective-permute-done.3.refs_1_, bf16[1280,2048]{1,0:T(8,128)(2,1)} %collective-permute-done.4.refs_2_, ...), custom_call_target="tpu_custom_call", output_to_operand_aliasing={{}: (8, {})} | custom-call | flops 64424509440 | bytes 20971520 | tf_op jit(solution)/shard_map/wide_part/pallas_call | solution.py:177
  1059.0 183.2 %collective-permute-done.22.w_ref = bf16[5632,256]{1,0:T(8,128)(2,1)} collective-permute-done((bf16[5632,256]{1,0:T(8,128)(2,1)}, bf16[5632,256]{1,0:T(8,128)(2,1)}, u32[]{:S(2)}, u32[]{:S(2)}) %collective-permute-start.22) | collective-permute-done | bytes 2883616 | tf_op jit(solution)/shard_map/ppermute | solution.py:424
  1243.1 54.8 %wide_part.14.refs_7_ = bf16[5120,5632]{1,0:T(8,128)(2,1)} custom-call(s32[6]{0:T(128)} %pad_add_fusion.3.meta_ref, bf16[1280,2048]{1,0:T(8,128)(2,1)} %get-tuple-element.96.refs_0_, bf16[1280,2048]{1,0:T(8,128)(2,1)} %collective-permute-done.3.refs_1_, bf16[1280,2048]{1,0:T(8,128)(2,1)} %collective-permute-done.4.refs_2_, ...), custom_call_target="tpu_custom_call", output_to_operand_aliasing={{}: (8, {})} | custom-call | flops 64424509440 | bytes 20971520 | tf_op jit(solution)/shard_map/wide_part/pallas_call | solution.py:177
  1297.9 6.9 collective-permute-done.30.w_ref
  1305.7 71.3 %wide_part.15.h_ref = bf16[5120,5632]{1,0:T(8,128)(2,1)} custom-call(s32[6]{0:T(128)} %pad_add_fusion.3.meta_ref, bf16[1280,2048]{1,0:T(8,128)(2,1)} %get-tuple-element.96.refs_0_, bf16[1280,2048]{1,0:T(8,128)(2,1)} %collective-permute-done.3.refs_1_, bf16[1280,2048]{1,0:T(8,128)(2,1)} %collective-permute-done.4.refs_2_, ...), custom_call_target="tpu_custom_call", output_to_operand_aliasing={{}: (8, {})} | custom-call | flops 85899345920 | bytes 20971520 | tf_op jit(solution)/shard_map/wide_part/pallas_call | solution.py:177
  1377.0 52.4 %down_part.10 = (bf16[1280,1024]{1,0:T(8,128)(2,1)}, bf16[1280,1024]{1,0:T(8,128)(2,1)}, bf16[1280,1024]{1,0:T(8,128)(2,1)}, bf16[1280,1024]{1,0:T(8,128)(2,1)}) custom-call(s32[6]{0:T(128)} %pad_add_fusion.3.meta_ref, bf16[5120,5632]{1,0:T(8,128)(2,1)} %wide_part.15.h_ref, bf16[2,5632,1024]{2,1,0:T(8,128)(2,1)} %w_ref.3), custom_call_target="tpu_custom_call" | custom-call | flops 59055800320 | bytes 57671680 | tf_op jit(solution)/shard_map/down_part/pallas_call | solution.py:258
  1429.4 29.8 %down_part.11 = (bf16[1280,512]{1,0:T(8,128)(2,1)}, bf16[1280,512]{1,0:T(8,128)(2,1)}, bf16[1280,512]{1,0:T(8,128)(2,1)}, bf16[1280,512]{1,0:T(8,128)(2,1)}) custom-call(s32[6]{0:T(128)} %pad_add_fusion.5.meta_ref, bf16[5120,5632]{1,0:T(8,128)(2,1)} %wide_part.11.h_ref, bf16[5632,512]{1,0:T(8,128)(2,1)} %collective-permute-done.14.w_ref), custom_call_target="tpu_custom_call" | custom-call | flops 29527900160 | bytes 57671680 | tf_op jit(solution)/shard_map/down_part/pallas_call | solution.py:258
  1459.3 69.8 %collective-permute-start.17 = (bf16[1280,1024]{1,0:T(8,128)(2,1)}, bf16[1280,1024]{1,0:T(8,128)(2,1)}, u32[]{:S(2)}, u32[]{:S(2)}) collective-permute-start(bf16[1280,1024]{1,0:T(8,128)(2,1)} %get-tuple-element.123), channel_id=1, source_target_pairs={{0,3},{1,0},{2,1},{3,2},{4,7},{5,4},{6,5},{7,6}} | collective-permute-start | bytes 7864328 | tf_op jit(solution)/shard_map/ppermute | solution.py:429
  1529.2 30.1 %down_part.12 = (bf16[1280,512]{1,0:T(8,128)(2,1)}, bf16[1280,512]{1,0:T(8,128)(2,1)}, bf16[1280,512]{1,0:T(8,128)(2,1)}, bf16[1280,512]{1,0:T(8,128)(2,1)}) custom-call(s32[6]{0:T(128)} %pad_add_fusion.3.meta_ref, bf16[5120,5632]{1,0:T(8,128)(2,1)} %wide_part.15.h_ref, bf16[5632,512]{1,0:T(8,128)(2,1)} %collective-permute-done.15.w_ref), custom_call_target="tpu_custom_call" | custom-call | flops 29527900160 | bytes 57671680 | tf_op jit(solution)/shard_map/down_part/pallas_call | solution.py:258
  1559.3 11.6 collective-permute-start.24
  1570.9 15.7 collective-permute-done.17.refs_3_
  1586.6 56.2 %collective-permute-done.19.refs_5_ = bf16[1280,1024]{1,0:T(8,128)(2,1)} collective-permute-done((bf16[1280,1024]{1,0:T(8,128)(2,1)}, bf16[1280,1024]{1,0:T(8,128)(2,1)}, u32[]{:S(2)}, u32[]{:S(2)}) %collective-permute-start.19) | collective-permute-done | bytes 2621472 | tf_op jit(solution)/shard_map/ppermute | solution.py:429
  1643.1 27.4 %mix_cols.5 = (bf16[4096,2048]{1,0:T(8,128)(2,1)}, s32[1]{0:T(128)}) custom-call(s32[1]{0:T(128)} %bitcast.13.col_ref, s32[1024]{0:T(1024)} %mul.74.chunk_ref, s32[4096,2]{1,0:T(8,128)} %copy.39.pos_ref, f32[4096,2]{1,0:T(8,128)} %copy.40.gate_ref, bf16[4096,2048]{1,0:T(8,128)(2,1)} %x_ref.13, bf16[1280,1024]{1,0:T(8,128)(2,1)} %get-tuple-element.112.refs_0_, ...), custom_call_target="tpu_custom_call" | custom-call | flops 20480000000 | bytes 20480000 | tf_op jit(solution)/shard_map/mix_cols/pallas_call | solution.py:326
  1671.8 18.6 down_part.13
  1698.7 18.6 down_part.14
  1719.1 6.8 collective-permute-start.33
  1728.0 28.5 %collective-permute-done.27.refs_5_ = bf16[1280,512]{1,0:T(8,128)(2,1)} collective-permute-done((bf16[1280,512]{1,0:T(8,128)(2,1)}, bf16[1280,512]{1,0:T(8,128)(2,1)}, u32[]{:S(2)}, u32[]{:S(2)}) %collective-permute-start.27) | collective-permute-done | bytes 1310752 | tf_op jit(solution)/shard_map/ppermute | solution.py:429
  1758.3 16.8 mix_cols.6
  1776.2 18.6 down_part.15
  1794.9 7.0 collective-permute-start.34
  1802.0 18.0 down_part.16
  1828.3 18.0 down_part.17
  1846.5 6.7 collective-permute-start.44
  1856.0 12.7 collective-permute-done.43.refs_6_
  1868.7 11.8 mix_cols.7
  1882.7 10.1 mix_cols.8
  1893.5 10.1 mix_cols.9
  (151 shorter events, 102.6 us)
Async XLA Ops:
  57.4 145.8 %collective-permute-start = (bf16[1280,2048]{1,0:T(8,128)(2,1)}, bf16[1280,2048]{1,0:T(8,128)(2,1)}, u32[]{:S(2)}, u32[]{:S(2)}) collective-permute-start(bf16[1280,2048]{1,0:T(8,128)(2,1)} %get-tuple-element.93), channel_id=1, source_target_pairs={{0,1},{1,2},{2,3},{3,0},{4,5},{5,6},{6,7},{7,4}} | collective-permute-start | bytes 15728648 | tf_op jit(solution)/shard_map/ppermute | solution.py:429
  57.4 145.8 %collective-permute-start.1 = (bf16[1280,2048]{1,0:T(8,128)(2,1)}, bf16[1280,2048]{1,0:T(8,128)(2,1)}, u32[]{:S(2)}, u32[]{:S(2)}) collective-permute-start(bf16[1280,2048]{1,0:T(8,128)(2,1)} %get-tuple-element.94), channel_id=1, source_target_pairs={{0,2},{1,3},{2,0},{3,1},{4,6},{5,7},{6,4},{7,5}} | collective-permute-start | bytes 15728648 | tf_op jit(solution)/shard_map/ppermute | solution.py:429
  59.4 225.5 %collective-permute-start.2 = (bf16[1280,2048]{1,0:T(8,128)(2,1)}, bf16[1280,2048]{1,0:T(8,128)(2,1)}, u32[]{:S(2)}, u32[]{:S(2)}) collective-permute-start(bf16[1280,2048]{1,0:T(8,128)(2,1)} %get-tuple-element.95), channel_id=1, source_target_pairs={{0,3},{1,0},{2,1},{3,2},{4,7},{5,4},{6,5},{7,6}} | collective-permute-start | bytes 15728648 | tf_op jit(solution)/shard_map/ppermute | solution.py:429
  65.0 137.4 %collective-permute-start.10 = (bf16[2,1024,512]{2,1,0:T(8,128)(2,1)}, bf16[2,1024,512]{2,1,0:T(8,128)(2,1)}, u32[]{:S(2)}, u32[]{:S(2)}) collective-permute-start(bf16[2,1024,512]{2,1,0:T(8,128)(2,1)} %pad_maximum_fusion.6), channel_id=1, source_target_pairs={{0,4},{4,0},{1,5},{5,1},{2,6},{6,2},{3,7},{7,3}} | collective-permute-start | bytes 6291464 | tf_op jit(solution)/shard_map/ppermute | solution.py:424
  84.6 225.1 %collective-permute-start.6 = (bf16[2,1024,1536]{2,1,0:T(8,128)(2,1)}, bf16[2,1024,1536]{2,1,0:T(8,128)(2,1)}, u32[]{:S(2)}, u32[]{:S(2)}) collective-permute-start(bf16[2,1024,1536]{2,1,0:T(8,128)(2,1)} %pad_maximum_fusion.3), channel_id=1, source_target_pairs={{0,4},{4,0},{1,5},{5,1},{2,6},{6,2},{3,7},{7,3}} | collective-permute-start | bytes 18874376 | tf_op jit(solution)/shard_map/ppermute | solution.py:424
  202.4 181.0 %collective-permute-start.11 = (bf16[2,1024,1536]{2,1,0:T(8,128)(2,1)}, bf16[2,1024,1536]{2,1,0:T(8,128)(2,1)}, u32[]{:S(2)}, u32[]{:S(2)}) collective-permute-start(bf16[2,1024,1536]{2,1,0:T(8,128)(2,1)} %pad_maximum_fusion.5), channel_id=1, source_target_pairs={{0,4},{4,0},{1,5},{5,1},{2,6},{6,2},{3,7},{7,3}} | collective-permute-start | bytes 18874376 | tf_op jit(solution)/shard_map/ppermute | solution.py:424
  284.9 513.3 %collective-permute-start.3 = (bf16[1280,2048]{1,0:T(8,128)(2,1)}, bf16[1280,2048]{1,0:T(8,128)(2,1)}, u32[]{:S(2)}, u32[]{:S(2)}) collective-permute-start(bf16[1280,2048]{1,0:T(8,128)(2,1)} %get-tuple-element.98), channel_id=1, source_target_pairs={{0,1},{1,2},{2,3},{3,0},{4,5},{5,6},{6,7},{7,4}} | collective-permute-start | bytes 15728648 | tf_op jit(solution)/shard_map/ppermute | solution.py:429
  285.5 528.4 %collective-permute-start.4 = (bf16[1280,2048]{1,0:T(8,128)(2,1)}, bf16[1280,2048]{1,0:T(8,128)(2,1)}, u32[]{:S(2)}, u32[]{:S(2)}) collective-permute-start(bf16[1280,2048]{1,0:T(8,128)(2,1)} %get-tuple-element.100), channel_id=1, source_target_pairs={{0,2},{1,3},{2,0},{3,1},{4,6},{5,7},{6,4},{7,5}} | collective-permute-start | bytes 15728648 | tf_op jit(solution)/shard_map/ppermute | solution.py:429
  287.5 530.9 %collective-permute-start.5 = (bf16[1280,2048]{1,0:T(8,128)(2,1)}, bf16[1280,2048]{1,0:T(8,128)(2,1)}, u32[]{:S(2)}, u32[]{:S(2)}) collective-permute-start(bf16[1280,2048]{1,0:T(8,128)(2,1)} %get-tuple-element.102), channel_id=1, source_target_pairs={{0,3},{1,0},{2,1},{3,2},{4,7},{5,4},{6,5},{7,6}} | collective-permute-start | bytes 15728648 | tf_op jit(solution)/shard_map/ppermute | solution.py:429
  309.8 297.4 %collective-permute-start.7 = (bf16[2,1024,2048]{2,1,0:T(8,128)(2,1)}, bf16[2,1024,2048]{2,1,0:T(8,128)(2,1)}, u32[]{:S(2)}, u32[]{:S(2)}) collective-permute-start(bf16[2,1024,2048]{2,1,0:T(8,128)(2,1)} %pad_maximum_fusion.1), channel_id=1, source_target_pairs={{0,4},{4,0},{1,5},{5,1},{2,6},{6,2},{3,7},{7,3}} | collective-permute-start | bytes 25165832 | tf_op jit(solution)/shard_map/ppermute | solution.py:424
  383.5 222.8 %collective-permute-start.12 = (bf16[2,1024,512]{2,1,0:T(8,128)(2,1)}, bf16[2,1024,512]{2,1,0:T(8,128)(2,1)}, u32[]{:S(2)}, u32[]{:S(2)}) collective-permute-start(bf16[2,1024,512]{2,1,0:T(8,128)(2,1)} %pad_maximum_fusion.7), channel_id=1, source_target_pairs={{0,4},{4,0},{1,5},{5,1},{2,6},{6,2},{3,7},{7,3}} | collective-permute-start | bytes 6291464 | tf_op jit(solution)/shard_map/ppermute | solution.py:424
  606.3 138.7 %collective-permute-start.13 = (bf16[2,1024,1536]{2,1,0:T(8,128)(2,1)}, bf16[2,1024,1536]{2,1,0:T(8,128)(2,1)}, u32[]{:S(2)}, u32[]{:S(2)}) collective-permute-start(bf16[2,1024,1536]{2,1,0:T(8,128)(2,1)} %pad_maximum_fusion.4), channel_id=1, source_target_pairs={{0,4},{4,0},{1,5},{5,1},{2,6},{6,2},{3,7},{7,3}} | collective-permute-start | bytes 18874376 | tf_op jit(solution)/shard_map/ppermute | solution.py:424
  607.1 272.7 %collective-permute-start.8 = (bf16[2,1024,1536]{2,1,0:T(8,128)(2,1)}, bf16[2,1024,1536]{2,1,0:T(8,128)(2,1)}, u32[]{:S(2)}, u32[]{:S(2)}) collective-permute-start(bf16[2,1024,1536]{2,1,0:T(8,128)(2,1)} %pad_maximum_fusion.2), channel_id=1, source_target_pairs={{0,4},{4,0},{1,5},{5,1},{2,6},{6,2},{3,7},{7,3}} | collective-permute-start | bytes 18874376 | tf_op jit(solution)/shard_map/ppermute | solution.py:424
  745.0 258.4 %collective-permute-start.14 = (bf16[5632,512]{1,0:T(8,128)(2,1)}, bf16[5632,512]{1,0:T(8,128)(2,1)}, u32[]{:S(2)}, u32[]{:S(2)}) collective-permute-start(bf16[5632,512]{1,0:T(8,128)(2,1)} %get-tuple-element.116), channel_id=1, source_target_pairs={{0,4},{4,0},{1,5},{5,1},{2,6},{6,2},{3,7},{7,3}} | collective-permute-start | bytes 17301512 | tf_op jit(solution)/shard_map/ppermute | solution.py:424
  798.2 730.8 %collective-permute-start.16 = (bf16[1280,1024]{1,0:T(8,128)(2,1)}, bf16[1280,1024]{1,0:T(8,128)(2,1)}, u32[]{:S(2)}, u32[]{:S(2)}) collective-permute-start(bf16[1280,1024]{1,0:T(8,128)(2,1)} %get-tuple-element.122), channel_id=1, source_target_pairs={{0,3},{1,0},{2,1},{3,2},{4,7},{5,4},{6,5},{7,6}} | collective-permute-start | bytes 7864328 | tf_op jit(solution)/shard_map/ppermute | solution.py:429
  813.9 745.4 %collective-permute-start.18 = (bf16[1280,1024]{1,0:T(8,128)(2,1)}, bf16[1280,1024]{1,0:T(8,128)(2,1)}, u32[]{:S(2)}, u32[]{:S(2)}) collective-permute-start(bf16[1280,1024]{1,0:T(8,128)(2,1)} %get-tuple-element.124), channel_id=1, source_target_pairs={{0,2},{1,3},{2,0},{3,1},{4,6},{5,7},{6,4},{7,5}} | collective-permute-start | bytes 7864328 | tf_op jit(solution)/shard_map/ppermute | solution.py:429
  818.5 752.5 %collective-permute-start.20 = (bf16[1280,1024]{1,0:T(8,128)(2,1)}, bf16[1280,1024]{1,0:T(8,128)(2,1)}, u32[]{:S(2)}, u32[]{:S(2)}) collective-permute-start(bf16[1280,1024]{1,0:T(8,128)(2,1)} %get-tuple-element.126), channel_id=1, source_target_pairs={{0,1},{1,2},{2,3},{3,0},{4,5},{5,6},{6,7},{7,4}} | collective-permute-start | bytes 7864328 | tf_op jit(solution)/shard_map/ppermute | solution.py:429
  879.8 425.0 %collective-permute-start.9 = (bf16[2,1024,2048]{2,1,0:T(8,128)(2,1)}, bf16[2,1024,2048]{2,1,0:T(8,128)(2,1)}, u32[]{:S(2)}, u32[]{:S(2)}) collective-permute-start(bf16[2,1024,2048]{2,1,0:T(8,128)(2,1)} %pad_maximum_fusion), channel_id=1, source_target_pairs={{0,4},{4,0},{1,5},{5,1},{2,6},{6,2},{3,7},{7,3}} | collective-permute-start | bytes 25165832 | tf_op jit(solution)/shard_map/ppermute | solution.py:424
  1003.4 238.8 %collective-permute-start.22 = (bf16[5632,256]{1,0:T(8,128)(2,1)}, bf16[5632,256]{1,0:T(8,128)(2,1)}, u32[]{:S(2)}, u32[]{:S(2)}) collective-permute-start(bf16[5632,256]{1,0:T(8,128)(2,1)} %get-tuple-element.129), channel_id=1, source_target_pairs={{0,4},{4,0},{1,5},{5,1},{2,6},{6,2},{3,7},{7,3}} | collective-permute-start | bytes 8650760 | tf_op jit(solution)/shard_map/ppermute | solution.py:424
  1242.2 62.6 %collective-permute-start.30 = (bf16[5632,256]{1,0:T(8,128)(2,1)}, bf16[5632,256]{1,0:T(8,128)(2,1)}, u32[]{:S(2)}, u32[]{:S(2)}) collective-permute-start(bf16[5632,256]{1,0:T(8,128)(2,1)} %get-tuple-element.143), channel_id=1, source_target_pairs={{0,4},{4,0},{1,5},{5,1},{2,6},{6,2},{3,7},{7,3}} | collective-permute-start | bytes 8650760 | tf_op jit(solution)/shard_map/ppermute | solution.py:424
  1304.8 224.3 %collective-permute-start.15 = (bf16[5632,512]{1,0:T(8,128)(2,1)}, bf16[5632,512]{1,0:T(8,128)(2,1)}, u32[]{:S(2)}, u32[]{:S(2)}) collective-permute-start(bf16[5632,512]{1,0:T(8,128)(2,1)} %get-tuple-element.119), channel_id=1, source_target_pairs={{0,4},{4,0},{1,5},{5,1},{2,6},{6,2},{3,7},{7,3}} | collective-permute-start | bytes 17301512 | tf_op jit(solution)/shard_map/ppermute | solution.py:424
  1459.3 127.4 %collective-permute-start.17 = (bf16[1280,1024]{1,0:T(8,128)(2,1)}, bf16[1280,1024]{1,0:T(8,128)(2,1)}, u32[]{:S(2)}, u32[]{:S(2)}) collective-permute-start(bf16[1280,1024]{1,0:T(8,128)(2,1)} %get-tuple-element.123), channel_id=1, source_target_pairs={{0,3},{1,0},{2,1},{3,2},{4,7},{5,4},{6,5},{7,6}} | collective-permute-start | bytes 7864328 | tf_op jit(solution)/shard_map/ppermute | solution.py:429
  1529.1 113.7 %collective-permute-start.19 = (bf16[1280,1024]{1,0:T(8,128)(2,1)}, bf16[1280,1024]{1,0:T(8,128)(2,1)}, u32[]{:S(2)}, u32[]{:S(2)}) collective-permute-start(bf16[1280,1024]{1,0:T(8,128)(2,1)} %get-tuple-element.125), channel_id=1, source_target_pairs={{0,2},{1,3},{2,0},{3,1},{4,6},{5,7},{6,4},{7,5}} | collective-permute-start | bytes 7864328 | tf_op jit(solution)/shard_map/ppermute | solution.py:429
  1529.1 114.0 %collective-permute-start.21 = (bf16[1280,1024]{1,0:T(8,128)(2,1)}, bf16[1280,1024]{1,0:T(8,128)(2,1)}, u32[]{:S(2)}, u32[]{:S(2)}) collective-permute-start(bf16[1280,1024]{1,0:T(8,128)(2,1)} %get-tuple-element.127), channel_id=1, source_target_pairs={{0,1},{1,2},{2,3},{3,0},{4,5},{5,6},{6,7},{7,4}} | collective-permute-start | bytes 7864328 | tf_op jit(solution)/shard_map/ppermute | solution.py:429
  1559.3 133.6 %collective-permute-start.24 = (bf16[1280,512]{1,0:T(8,128)(2,1)}, bf16[1280,512]{1,0:T(8,128)(2,1)}, u32[]{:S(2)}, u32[]{:S(2)}) collective-permute-start(bf16[1280,512]{1,0:T(8,128)(2,1)} %get-tuple-element.135), channel_id=1, source_target_pairs={{0,3},{1,0},{2,1},{3,2},{4,7},{5,4},{6,5},{7,6}} | collective-permute-start | bytes 3932168 | tf_op jit(solution)/shard_map/ppermute | solution.py:429
  1570.9 146.4 %collective-permute-start.26 = (bf16[1280,512]{1,0:T(8,128)(2,1)}, bf16[1280,512]{1,0:T(8,128)(2,1)}, u32[]{:S(2)}, u32[]{:S(2)}) collective-permute-start(bf16[1280,512]{1,0:T(8,128)(2,1)} %get-tuple-element.137), channel_id=1, source_target_pairs={{0,2},{1,3},{2,0},{3,1},{4,6},{5,7},{6,4},{7,5}} | collective-permute-start | bytes 3932168 | tf_op jit(solution)/shard_map/ppermute | solution.py:429
  1586.6 132.5 %collective-permute-start.28 = (bf16[1280,512]{1,0:T(8,128)(2,1)}, bf16[1280,512]{1,0:T(8,128)(2,1)}, u32[]{:S(2)}, u32[]{:S(2)}) collective-permute-start(bf16[1280,512]{1,0:T(8,128)(2,1)} %get-tuple-element.139), channel_id=1, source_target_pairs={{0,1},{1,2},{2,3},{3,0},{4,5},{5,6},{6,7},{7,4}} | collective-permute-start | bytes 3932168 | tf_op jit(solution)/shard_map/ppermute | solution.py:429
  1642.8 55.7 %collective-permute-start.23 = (bf16[5632,256]{1,0:T(8,128)(2,1)}, bf16[5632,256]{1,0:T(8,128)(2,1)}, u32[]{:S(2)}, u32[]{:S(2)}) collective-permute-start(bf16[5632,256]{1,0:T(8,128)(2,1)} %get-tuple-element.132), channel_id=1, source_target_pairs={{0,4},{4,0},{1,5},{5,1},{2,6},{6,2},{3,7},{7,3}} | collective-permute-start | bytes 8650760 | tf_op jit(solution)/shard_map/ppermute | solution.py:424
  1690.5 35.5 %collective-permute-start.25 = (bf16[1280,512]{1,0:T(8,128)(2,1)}, bf16[1280,512]{1,0:T(8,128)(2,1)}, u32[]{:S(2)}, u32[]{:S(2)}) collective-permute-start(bf16[1280,512]{1,0:T(8,128)(2,1)} %get-tuple-element.136), channel_id=1, source_target_pairs={{0,3},{1,0},{2,1},{3,2},{4,7},{5,4},{6,5},{7,6}} | collective-permute-start | bytes 3932168 | tf_op jit(solution)/shard_map/ppermute | solution.py:429
  1692.9 63.6 %collective-permute-start.27 = (bf16[1280,512]{1,0:T(8,128)(2,1)}, bf16[1280,512]{1,0:T(8,128)(2,1)}, u32[]{:S(2)}, u32[]{:S(2)}) collective-permute-start(bf16[1280,512]{1,0:T(8,128)(2,1)} %get-tuple-element.138), channel_id=1, source_target_pairs={{0,2},{1,3},{2,0},{3,1},{4,6},{5,7},{6,4},{7,5}} | collective-permute-start | bytes 3932168 | tf_op jit(solution)/shard_map/ppermute | solution.py:429
  1698.5 58.0 %collective-permute-start.29 = (bf16[1280,512]{1,0:T(8,128)(2,1)}, bf16[1280,512]{1,0:T(8,128)(2,1)}, u32[]{:S(2)}, u32[]{:S(2)}) collective-permute-start(bf16[1280,512]{1,0:T(8,128)(2,1)} %get-tuple-element.140), channel_id=1, source_target_pairs={{0,1},{1,2},{2,3},{3,0},{4,5},{5,6},{6,7},{7,4}} | collective-permute-start | bytes 3932168 | tf_op jit(solution)/shard_map/ppermute | solution.py:429
  1717.4 77.5 %collective-permute-start.32 = (bf16[5632,128]{1,0:T(8,128)(2,1)}, bf16[5632,128]{1,0:T(8,128)(2,1)}, u32[]{:S(2)}, u32[]{:S(2)}) collective-permute-start(bf16[5632,128]{1,0:T(8,128)(2,1)} %get-tuple-element.149), channel_id=1, source_target_pairs={{0,4},{4,0},{1,5},{5,1},{2,6},{6,2},{3,7},{7,3}} | collective-permute-start | bytes 4325384 | tf_op jit(solution)/shard_map/ppermute | solution.py:424
  1719.1 100.9 %collective-permute-start.33 = (bf16[1280,256]{1,0:T(8,128)(2,1)}, bf16[1280,256]{1,0:T(8,128)(2,1)S(1)}, u32[]{:S(2)}, u32[]{:S(2)}) collective-permute-start(bf16[1280,256]{1,0:T(8,128)(2,1)} %get-tuple-element.152), channel_id=1, source_target_pairs={{0,3},{1,0},{2,1},{3,2},{4,7},{5,4},{6,5},{7,6}} | collective-permute-start | bytes 1966088 | tf_op jit(solution)/shard_map/ppermute | solution.py:429
  1726.0 94.2 %collective-permute-start.35 = (bf16[1280,256]{1,0:T(8,128)(2,1)}, bf16[1280,256]{1,0:T(8,128)(2,1)}, u32[]{:S(2)}, u32[]{:S(2)}) collective-permute-start(bf16[1280,256]{1,0:T(8,128)(2,1)} %get-tuple-element.154), channel_id=1, source_target_pairs={{0,2},{1,3},{2,0},{3,1},{4,6},{5,7},{6,4},{7,5}} | collective-permute-start | bytes 1966088 | tf_op jit(solution)/shard_map/ppermute | solution.py:429
  1756.5 70.0 %collective-permute-start.37 = (bf16[1280,256]{1,0:T(8,128)(2,1)}, bf16[1280,256]{1,0:T(8,128)(2,1)}, u32[]{:S(2)}, u32[]{:S(2)}) collective-permute-start(bf16[1280,256]{1,0:T(8,128)(2,1)} %get-tuple-element.156), channel_id=1, source_target_pairs={{0,1},{1,2},{2,3},{3,0},{4,5},{5,6},{6,7},{7,4}} | collective-permute-start | bytes 1966088 | tf_op jit(solution)/shard_map/ppermute | solution.py:429
  1756.5 45.4 %collective-permute-start.31 = (bf16[5632,128]{1,0:T(8,128)(2,1)}, bf16[5632,128]{1,0:T(8,128)(2,1)}, u32[]{:S(2)}, u32[]{:S(2)}) collective-permute-start(bf16[5632,128]{1,0:T(8,128)(2,1)} %get-tuple-element.146), channel_id=1, source_target_pairs={{0,4},{4,0},{1,5},{5,1},{2,6},{6,2},{3,7},{7,3}} | collective-permute-start | bytes 4325384 | tf_op jit(solution)/shard_map/ppermute | solution.py:424
  1794.9 31.6 %collective-permute-start.34 = (bf16[1280,256]{1,0:T(8,128)(2,1)}, bf16[1280,256]{1,0:T(8,128)(2,1)}, u32[]{:S(2)}, u32[]{:S(2)}) collective-permute-start(bf16[1280,256]{1,0:T(8,128)(2,1)} %get-tuple-element.153), channel_id=1, source_target_pairs={{0,3},{1,0},{2,1},{3,2},{4,7},{5,4},{6,5},{7,6}} | collective-permute-start | bytes 1966088 | tf_op jit(solution)/shard_map/ppermute | solution.py:429
  1801.9 25.1 %collective-permute-start.36 = (bf16[1280,256]{1,0:T(8,128)(2,1)}, bf16[1280,256]{1,0:T(8,128)(2,1)}, u32[]{:S(2)}, u32[]{:S(2)}) collective-permute-start(bf16[1280,256]{1,0:T(8,128)(2,1)} %get-tuple-element.155), channel_id=1, source_target_pairs={{0,2},{1,3},{2,0},{3,1},{4,6},{5,7},{6,4},{7,5}} | collective-permute-start | bytes 1966088 | tf_op jit(solution)/shard_map/ppermute | solution.py:429
  1820.1 26.2 %collective-permute-start.38 = (bf16[1280,256]{1,0:T(8,128)(2,1)}, bf16[1280,256]{1,0:T(8,128)(2,1)}, u32[]{:S(2)}, u32[]{:S(2)}) collective-permute-start(bf16[1280,256]{1,0:T(8,128)(2,1)} %get-tuple-element.157), channel_id=1, source_target_pairs={{0,1},{1,2},{2,3},{3,0},{4,5},{5,6},{6,7},{7,4}} | collective-permute-start | bytes 1966088 | tf_op jit(solution)/shard_map/ppermute | solution.py:429
  1820.9 25.6 %collective-permute-start.39 = (bf16[1280,256]{1,0:T(8,128)(2,1)}, bf16[1280,256]{1,0:T(8,128)(2,1)S(1)}, u32[]{:S(2)}, u32[]{:S(2)}) collective-permute-start(bf16[1280,256]{1,0:T(8,128)(2,1)} %get-tuple-element.160), channel_id=1, source_target_pairs={{0,3},{1,0},{2,1},{3,2},{4,7},{5,4},{6,5},{7,6}} | collective-permute-start | bytes 1966088 | tf_op jit(solution)/shard_map/ppermute | solution.py:429
  1826.5 29.5 %collective-permute-start.41 = (bf16[1280,256]{1,0:T(8,128)(2,1)}, bf16[1280,256]{1,0:T(8,128)(2,1)}, u32[]{:S(2)}, u32[]{:S(2)}) collective-permute-start(bf16[1280,256]{1,0:T(8,128)(2,1)} %get-tuple-element.162), channel_id=1, source_target_pairs={{0,2},{1,3},{2,0},{3,1},{4,6},{5,7},{6,4},{7,5}} | collective-permute-start | bytes 1966088 | tf_op jit(solution)/shard_map/ppermute | solution.py:429
  1826.5 42.2 %collective-permute-start.43 = (bf16[1280,256]{1,0:T(8,128)(2,1)}, bf16[1280,256]{1,0:T(8,128)(2,1)}, u32[]{:S(2)}, u32[]{:S(2)}) collective-permute-start(bf16[1280,256]{1,0:T(8,128)(2,1)} %get-tuple-element.164), channel_id=1, source_target_pairs={{0,1},{1,2},{2,3},{3,0},{4,5},{5,6},{6,7},{7,4}} | collective-permute-start | bytes 1966088 | tf_op jit(solution)/shard_map/ppermute | solution.py:429
  1827.0 41.7 %collective-permute-start.40 = (bf16[1280,128]{1,0:T(8,128)(2,1)}, bf16[1280,128]{1,0:T(8,128)(2,1)S(1)}, u32[]{:S(2)}, u32[]{:S(2)}) collective-permute-start(bf16[1280,128]{1,0:T(8,128)(2,1)} %get-tuple-element.161), channel_id=1, source_target_pairs={{0,3},{1,0},{2,1},{3,2},{4,7},{5,4},{6,5},{7,6}} | collective-permute-start | bytes 983048 | tf_op jit(solution)/shard_map/ppermute | solution.py:429
  1846.3 34.9 %collective-permute-start.42 = (bf16[1280,128]{1,0:T(8,128)(2,1)}, bf16[1280,128]{1,0:T(8,128)(2,1)}, u32[]{:S(2)}, u32[]{:S(2)}) collective-permute-start(bf16[1280,128]{1,0:T(8,128)(2,1)} %get-tuple-element.163), channel_id=1, source_target_pairs={{0,2},{1,3},{2,0},{3,1},{4,6},{5,7},{6,4},{7,5}} | collective-permute-start | bytes 983048 | tf_op jit(solution)/shard_map/ppermute | solution.py:429
  1846.5 36.2 %collective-permute-start.44 = (bf16[1280,128]{1,0:T(8,128)(2,1)}, bf16[1280,128]{1,0:T(8,128)(2,1)}, u32[]{:S(2)}, u32[]{:S(2)}) collective-permute-start(bf16[1280,128]{1,0:T(8,128)(2,1)} %get-tuple-element.165), channel_id=1, source_target_pairs={{0,1},{1,2},{2,3},{3,0},{4,5},{5,6},{6,7},{7,4}} | collective-permute-start | bytes 983048 | tf_op jit(solution)/shard_map/ppermute | solution.py:429
  1856.0 37.5 %collective-permute-start.45 = (bf16[1280,128]{1,0:T(8,128)(2,1)}, bf16[1280,128]{1,0:T(8,128)(2,1)}, u32[]{:S(2)}, u32[]{:S(2)}) collective-permute-start(bf16[1280,128]{1,0:T(8,128)(2,1)} %get-tuple-element.168), channel_id=1, source_target_pairs={{0,3},{1,0},{2,1},{3,2},{4,7},{5,4},{6,5},{7,6}} | collective-permute-start | bytes 983048 | tf_op jit(solution)/shard_map/ppermute | solution.py:429
  1868.7 24.8 %collective-permute-start.46 = (bf16[1280,128]{1,0:T(8,128)(2,1)}, bf16[1280,128]{1,0:T(8,128)(2,1)}, u32[]{:S(2)}, u32[]{:S(2)}) collective-permute-start(bf16[1280,128]{1,0:T(8,128)(2,1)} %get-tuple-element.169), channel_id=1, source_target_pairs={{0,2},{1,3},{2,0},{3,1},{4,6},{5,7},{6,4},{7,5}} | collective-permute-start | bytes 983048 | tf_op jit(solution)/shard_map/ppermute | solution.py:429
  1868.7 24.8 %collective-permute-start.47 = (bf16[1280,128]{1,0:T(8,128)(2,1)}, bf16[1280,128]{1,0:T(8,128)(2,1)}, u32[]{:S(2)}, u32[]{:S(2)}) collective-permute-start(bf16[1280,128]{1,0:T(8,128)(2,1)} %get-tuple-element.170), channel_id=1, source_target_pairs={{0,1},{1,2},{2,3},{3,0},{4,5},{5,6},{6,7},{7,4}} | collective-permute-start | bytes 983048 | tf_op jit(solution)/shard_map/ppermute | solution.py:429
  (9 other events, 155.8 us)

commit v3 on v2

--- a/solution.py
+++ b/solution.py
@@ -20,9 +20,20 @@
 ALIGN = 16
 REACH = 512
 DEEP = 4
+DOWN_BLOCK = 512
 SUB = 512
-WIDE_CHUNKS = (512, 1536, 1536, 2048)
-DOWN_PIECES = ((0, 0, 512), (1, 0, 512), (0, 512, 256), (1, 512, 256), (0, 768, 256), (1, 768, 128), (1, 896, 128))
+WIDE_CHUNKS = (512, 2048, 1536, 1536)
+DOWN_PIECES = (
+    (0, 0, 512, (0, 11)),
+    (1, 0, 512, (0, 11)),
+    (0, 512, 256, (0, 11)),
+    (1, 512, 256, (0, 11)),
+    (0, 768, 256, (0, 11)),
+    (1, 768, 128, (0, 11)),
+    (1, 896, 128, (0, 8)),
+    (1, 896, 128, (8, 11)),
+)
+DOWN_SHARES = 11
 
 
 def capacity_rows(tok_rows, top_k, n_exp):
@@ -148,11 +159,15 @@
         def _():
             send(i - 2).wait()
 
-        rows = rows_buf[i % 2]
-        for j in range(0, cols, SUB):
-            g = jnp.dot(rows, gate_w[:, j : j + SUB], preferred_element_type=F32)
-            u = jnp.dot(rows, up_w[:, j : j + SUB], preferred_element_type=F32)
-            h_buf[i % 2, :, j : j + SUB] = (jax.nn.silu(g) * u).astype(BF16)
+        def part(j, carry):
+            span = pl.ds(pl.multiple_of(j * SUB, SUB), SUB)
+            rows = rows_buf[i % 2]
+            g = jnp.dot(rows, gate_w[:, span], preferred_element_type=F32)
+            u = jnp.dot(rows, up_w[:, span], preferred_element_type=F32)
+            h_buf[i % 2, :, span] = (jax.nn.silu(g) * u).astype(BF16)
+            return carry
+
+        lax.fori_loop(0, cols // SUB, part, 0)
         send(i).start()
         return carry
 
@@ -195,22 +210,33 @@
     )(*args)
 
 
-def down_body(n_group, local, meta_ref, h_ref, w_ref, *refs):
-    out_refs = refs[:n_group]
-    h_buf, out_buf, w_buf, h_sems, out_sems, sem = refs[n_group:]
+def down_body(n_group, local, lo_hid, adds, partial, meta_ref, h_ref, w_ref, *refs):
+    sum_ref, refs = (refs[0], refs[1:]) if adds else (None, refs)
+    n_out = 1 if partial else n_group
+    out_refs = refs[:n_out]
+    h_buf, out_buf, w_buf, sum_buf, h_sems, out_sems, sum_sems, sem = refs[n_out:]
     n_live = meta_ref[1 + n_group]
-
-    def fetch(i):
-        return pltpu.make_async_copy(h_ref.at[tile_at(i), :], h_buf.at[i % DEEP], h_sems.at[i % DEEP])
+    hid = pl.ds(lo_hid, w_buf.shape[0])
+    block = min(w_buf.shape[1], DOWN_BLOCK)
+
+    def fetches(i):
+        copies = [pltpu.make_async_copy(h_ref.at[tile_at(i), hid], h_buf.at[i % DEEP], h_sems.at[i % DEEP])]
+        if adds:
+            copies.append(pltpu.make_async_copy(sum_ref.at[tile_at(i), :], sum_buf.at[i % DEEP], sum_sems.at[i % DEEP]))
+        return copies
 
     def sent(i):
         pltpu.make_async_copy(out_buf.at[i % 2], out_refs[0].at[tile_at(0), :], out_sems.at[i % 2]).wait()
 
+    def send(i, there, tile):
+        pltpu.make_async_copy(out_buf.at[i % 2], there.at[tile_at(tile), :], out_sems.at[i % 2]).start()
+
     for i in range(DEEP - 1):
 
         @pl.when(i < n_live)
         def _():
-            fetch(i).start()
+            for copy in fetches(i):
+                copy.start()
 
     copy = pltpu.make_async_copy(w_ref if local is None else w_ref.at[local], w_buf, sem)
     copy.start()
@@ -219,20 +245,33 @@
     def step(i, carry):
         @pl.when(i + DEEP - 1 < n_live)
         def _():
-            fetch(i + DEEP - 1).start()
-
-        fetch(i).wait()
+            for copy in fetches(i + DEEP - 1):
+                copy.start()
+
+        for copy in fetches(i):
+            copy.wait()
 
         @pl.when(i >= 2)
         def _():
             sent(i)
 
-        out_buf[i % 2] = jnp.dot(h_buf[i % DEEP], w_buf[...], preferred_element_type=F32).astype(BF16)
+        def part(j, carry):
+            span = pl.ds(pl.multiple_of(j * block, block), block)
+            total = jnp.dot(h_buf[i % DEEP], w_buf[:, span], preferred_element_type=F32)
+            if adds:
+                total += sum_buf[i % DEEP, :, span]
+            out_buf[i % 2, :, span] = total.astype(out_buf.dtype)
+            return carry
+
+        lax.fori_loop(0, w_buf.shape[1] // block, part, 0)
+        if partial:
+            send(i, out_refs[0], i)
+            return carry
         for d in range(n_group):
 
             @pl.when((i >= meta_ref[1 + d]) & (i < meta_ref[2 + d]))
             def _():
-                pltpu.make_async_copy(out_buf.at[i % 2], out_refs[d].at[tile_at(i - meta_ref[1 + d]), :], out_sems.at[i % 2]).start()
+                send(i, out_refs[d], i - meta_ref[1 + d])
 
         return carry
 
@@ -243,48 +282,57 @@
         def _():
             sent(n_live - back)
 
-    for d in range(n_group):
+    for d in range(0 if partial else n_group):
         @pl.when(meta_ref[1 + d] == meta_ref[2 + d])
         def _():
             out_buf[0] = jnp.zeros_like(out_buf[0])
-            blank = pltpu.make_async_copy(out_buf.at[0], out_refs[d].at[tile_at(0), :], out_sems.at[0])
-            blank.start()
-            blank.wait()
-
-
-def down_part(meta, hidden, weight, n_group, local=None):
+            send(0, out_refs[d], 0)
+            sent(0)
+
+
+def down_part(meta, hidden, weight, n_group, local=None, lo_hid=0, sums=None, partial=False):
     n_rows = hidden.shape[0]
-    ffn, width = weight.shape[-2:]
+    n_hid, width = weight.shape[-2:]
+    adds = sums is not None
+    out_type = F32 if partial else BF16
+    rows = n_rows if partial else n_rows // n_group
     return pl.pallas_call(
-        functools.partial(down_body, n_group, local),
-        in_specs=[smem(), any_spec(), any_spec()],
-        out_specs=[any_spec()] * n_group,
+        functools.partial(down_body, n_group, local, lo_hid, adds, partial),
+        in_specs=[smem()] + [any_spec()] * (2 + adds),
+        out_specs=[any_spec()] * (1 if partial else n_group),
         scratch_shapes=[
-            pltpu.VMEM((DEEP, TILE, ffn), BF16),
-            pltpu.VMEM((2, TILE, width), BF16),
-            pltpu.VMEM((ffn, width), BF16),
+            pltpu.VMEM((DEEP, TILE, n_hid), BF16),
+            pltpu.VMEM((2, TILE, width), out_type),
+            pltpu.VMEM((n_hid, width), BF16),
+            pltpu.VMEM((DEEP, TILE, width) if adds else (DEEP, 8, 128), F32),
             pltpu.SemaphoreType.DMA((DEEP,)),
             pltpu.SemaphoreType.DMA((2,)),
+            pltpu.SemaphoreType.DMA((DEEP,)),
             pltpu.SemaphoreType.DMA,
         ],
-        out_shape=[jax.ShapeDtypeStruct((n_rows // n_group, width), BF16)] * n_group,
+        out_shape=[jax.ShapeDtypeStruct((rows, width), out_type)] * (1 if partial else n_group),
         compiler_params=pltpu.CompilerParams(vmem_limit_bytes=VMEM_LIMIT),
-        cost_estimate=pl.CostEstimate(flops=2 * n_rows * ffn * width, bytes_accessed=n_rows * ffn * 2, transcendentals=0),
+        cost_estimate=pl.CostEstimate(flops=2 * n_rows * n_hid * width, bytes_accessed=n_rows * n_hid * 2, transcendentals=0),
         name="down_part",
-    )(meta, hidden, weight)
-
-
-def mix_body(n_exp, n_tile, subs, col_ref, chunk_ref, pos_ref, gate_ref, x_ref, *refs):
-    back_refs = refs[:n_exp]
-    y_ref, mark_ref, back_buf, near_buf, x_buf, y_buf, sems = refs[-7:]
-    width = x_buf.shape[1]
-    capacity = back_refs[0].shape[0]
-    cols = pl.ds(pl.multiple_of(col_ref[0], 128), width)
-    copies = [
-        pltpu.make_async_copy(ref.at[:, pl.ds(sub * width, width)], back_buf.at[pl.ds(e * capacity, capacity), :], sems.at[e])
-        for e, (ref, sub) in enumerate(zip(back_refs, subs))
-    ]
-    copies.append(pltpu.make_async_copy(x_ref.at[:, cols], x_buf, sems.at[n_exp]))
+    )(meta, hidden, weight, *([sums] if adds else []))
+
+
+def mix_body(n_exp, n_tile, subs, widths, col_ref, chunk_ref, pos_ref, gate_ref, x_ref, *refs):
+    n_set = len(widths)
+    back_refs = refs[: n_set * n_exp]
+    y_ref, mark_ref = refs[-3 - 4 * n_set : -1 - 4 * n_set]
+    bufs, sems = refs[-1 - 4 * n_set : -1], refs[-1]
+    sets, copies = [], []
+    for g, width in enumerate(widths):
+        back_buf, near_buf, x_buf, y_buf = bufs[4 * g : 4 * g + 4]
+        cols = pl.ds(pl.multiple_of(col_ref[g], 128), width)
+        sets.append((back_buf, near_buf, x_buf, y_buf, cols))
+        for e in range(n_exp):
+            ref, sub = back_refs[g * n_exp + e], subs[g * n_exp + e]
+            capacity = ref.shape[0]
+            here = back_buf.at[pl.ds(e * capacity, capacity), :]
+            copies.append(pltpu.make_async_copy(ref.at[:, pl.ds(sub * width, width)], here, sems.at[len(copies)]))
+        copies.append(pltpu.make_async_copy(x_ref.at[:, cols], x_buf, sems.at[len(copies)]))
     for copy in copies:
         copy.start()
     for copy in copies:
@@ -294,50 +342,55 @@
         for k in range(MIX_UNROLL):
             i = block * MIX_UNROLL + k
             tokens = pl.ds(pl.multiple_of(i * MIX_TILE, MIX_TILE), MIX_TILE)
-            for c in range(REACH // ALIGN):
-                chunk = pl.multiple_of(chunk_ref[i * (REACH // ALIGN) + c], ALIGN)
-                near_buf[k, c * ALIGN : (c + 1) * ALIGN, :] = back_buf[pl.ds(chunk, ALIGN), :]
             seat = lax.broadcasted_iota(I32, (MIX_TILE, REACH), 1)
             pick = jnp.concatenate([(seat == pos_ref[tokens, j : j + 1]).astype(F32).astype(BF16) for j in range(2)], axis=0)
-            found = jnp.dot(pick, near_buf[k], preferred_element_type=F32)
-            mixed = gate_ref[tokens, 0:1] * found[:MIX_TILE] + gate_ref[tokens, 1:2] * found[MIX_TILE:]
-            y_buf[tokens, :] = (x_buf[tokens, :].astype(F32) + mixed).astype(BF16)
+            for back_buf, near_buf, x_buf, y_buf, _ in sets:
+                for c in range(REACH // ALIGN):
+                    chunk = pl.multiple_of(chunk_ref[i * (REACH // ALIGN) + c], ALIGN)
+                    near_buf[k, c * ALIGN : (c + 1) * ALIGN, :] = back_buf[pl.ds(chunk, ALIGN), :]
+                found = jnp.dot(pick, near_buf[k], preferred_element_type=F32)
+                mixed = gate_ref[tokens, 0:1] * found[:MIX_TILE] + gate_ref[tokens, 1:2] * found[MIX_TILE:]
+                y_buf[tokens, :] = (x_buf[tokens, :].astype(F32) + mixed).astype(BF16)
         return carry
 
     lax.fori_loop(0, n_tile // MIX_UNROLL, step, 0)
-    out = pltpu.make_async_copy(y_buf, y_ref.at[:, cols], sems.at[0])
-    out.start()
-    out.wait()
+    outs = [pltpu.make_async_copy(y_buf, y_ref.at[:, cols], sems.at[g]) for g, (_, _, _, y_buf, cols) in enumerate(sets)]
+    for out in outs:
+        out.start()
+    for out in outs:
+        out.wait()
     mark_ref[0] = 0
 
 
-def mix_cols(col, y_loc, x_loc, pos, gate_loc, chunks, width, back):
+def mix_cols(col, y_loc, x_loc, pos, gate_loc, chunks, widths, back):
     tok_rows, d_model = x_loc.shape
-    n_exp = len(back)
+    n_exp = len(back) // len(widths)
     capacity = back[0][0].shape[0]
     vmem = pl.BlockSpec(memory_space=pltpu.VMEM)
     args = [col, chunks, pos, gate_loc, x_loc, *[array for array, _ in back]]
-    specs = [smem(), smem(), vmem, vmem, any_spec()] + [any_spec()] * n_exp
+    specs = [smem(), smem(), vmem, vmem, any_spec()] + [any_spec()] * len(back)
     alias = {}
     if y_loc is not None:
         alias = {len(args): 0}
         args.append(y_loc)
         specs.append(any_spec())
-    return pl.pallas_call(
-        functools.partial(mix_body, n_exp, tok_rows // MIX_TILE, tuple(sub for _, sub in back)),
-        in_specs=specs,
-        out_specs=[any_spec(), smem()],
-        scratch_shapes=[
+    bufs = []
+    for width in widths:
+        bufs += [
             pltpu.VMEM((n_exp * capacity, width), BF16),
             pltpu.VMEM((MIX_UNROLL, REACH, width), BF16),
             pltpu.VMEM((tok_rows, width), BF16),
             pltpu.VMEM((tok_rows, width), BF16),
-            pltpu.SemaphoreType.DMA((n_exp + 1,)),
-        ],
+        ]
+    return pl.pallas_call(
+        functools.partial(mix_body, n_exp, tok_rows // MIX_TILE, tuple(sub for _, sub in back), widths),
+        in_specs=specs,
+        out_specs=[any_spec(), smem()],
+        scratch_shapes=bufs + [pltpu.SemaphoreType.DMA(((n_exp + 1) * len(widths),))],
         out_shape=[jax.ShapeDtypeStruct((tok_rows, d_model), BF16), jax.ShapeDtypeStruct((1,), I32)],
         input_output_aliases=alias,
         compiler_params=pltpu.CompilerParams(vmem_limit_bytes=VMEM_LIMIT),
-        cost_estimate=pl.CostEstimate(flops=20_000_000 * width, bytes_accessed=20_000 * width, transcendentals=0),
+        cost_estimate=pl.CostEstimate(flops=20_000_000 * sum(widths), bytes_accessed=20_000 * sum(widths), transcendentals=0),
         name="mix_cols",
     )(*args)
 
@@ -359,7 +412,7 @@
     def whole_step(x_loc, idx_loc, gate_loc, wg_loc, wu_loc, wd_loc):
         tok_rows, _ = x_loc.shape
         top_k = idx_loc.shape[1]
-        n_local, half, _ = wg_loc.shape
+        n_local, half, ffn = wg_loc.shape
         n_exp = n_local * n_group
         capacity = capacity_rows(tok_rows, top_k, n_exp)
         side = lax.axis_index("data")
@@ -412,7 +465,8 @@
         parts = [jnp.stack([w[0, :, : wide_spans[0][1]] for w in (wg_loc, wu_loc)])]
         later = after((wg_loc, wu_loc), parts[0])
         parts += [jnp.stack([w[l, :, lo : lo + n] for w in later]) for l in locals_ for lo, n in wide_spans if l or lo]
-        parts += [wd_loc[l, :, lo : lo + n] for l, lo, n in DOWN_PIECES]
+        hid = [(first * ffn // DOWN_SHARES, stop * ffn // DOWN_SHARES) for *_, (first, stop) in DOWN_PIECES]
+        parts += [wd_loc[l, a:b, lo : lo + n] for (l, lo, n, _), (a, b) in zip(DOWN_PIECES, hid)]
         far = []
 
         def cross():
@@ -429,10 +483,10 @@
                 out.append(lax.ppermute(blocks[d], "expert", [(s, (s + step * d) % n_group) for s in range(n_group)]))
             return out
 
-        def mix(y_loc, col, width, back):
-            col = col.astype(I32)[None]
-            back = [(back[l][0][d], back[l][1]) for d in range(n_group) for l in locals_]
-            out = in_turn(mix_cols, col, y_loc, x_loc, pos, gate_loc, chunks, width, back)
+        def mix(y_loc, *sets):
+            col = jnp.stack([col for col, _, _ in sets]).astype(I32)
+            back = [(pair[l][0][d], pair[l][1]) for _, _, pair in sets for d in range(n_group) for l in locals_]
+            out = in_turn(mix_cols, col, y_loc, x_loc, pos, gate_loc, chunks, tuple(width for _, width, _ in sets), back)
             done[-1] = out[1][0]
             return out[0]
 
@@ -450,25 +504,28 @@
         for l in locals_:
             hidden.append(None)
             for k, (lo, n) in enumerate(wide_spans):
-                if l or k >= 2:
+                if k >= 2 or (l and k):
                     cross()
                 hidden[l] = in_turn(wide_part, meta[l], hidden[l], rows[l], wg_loc, wu_loc, far[l * n_wide + k], l, lo, n, follows=k == 0)
+            if l == 0:
+                cross()
             own.append(exchange(in_turn(down_part, meta[l], hidden[l], wd_loc, n_group, l, follows=False), -1))
 
-        def far_piece(i):
+        def far_piece(i, sums=None, partial=False):
             cross()
             l = DOWN_PIECES[i][0]
-            return exchange(in_turn(down_part, meta[l], hidden[l], far[n_local * n_wide + i], n_group), -1)
+            out = in_turn(down_part, meta[l], hidden[l], far[n_local * n_wide + i], n_group, None, hid[i][0], sums, partial)
+            return out[0] if partial else exchange(out, -1)
 
         far_col = (1 - side) * half
         ret = [far_piece(0), far_piece(1)]
-        y_loc = mix(None, side * half, half, [(own[l], 0) for l in locals_])
+        y_loc = mix(None, (side * half, half, [(own[l], 0) for l in locals_]))
         ret += [far_piece(2), far_piece(3)]
-        y_loc = mix(y_loc, far_col, 512, [(ret[0], 0), (ret[1], 0)])
-        ret += [far_piece(4), far_piece(5), far_piece(6)]
-        y_loc = mix(y_loc, far_col + 512, 256, [(ret[2], 0), (ret[3], 0)])
-        y_loc = mix(y_loc, far_col + 768, 128, [(ret[4], 0), (ret[5], 0)])
-        return mix(y_loc, far_col + 896, 128, [(ret[4], 1), (ret[6], 0)])
+        y_loc = mix(y_loc, (far_col, 512, [(ret[0], 0), (ret[1], 0)]))
+        ret += [far_piece(4), far_piece(5)]
+        ret.append(far_piece(7, far_piece(6, partial=True)))
+        y_loc = mix(y_loc, (far_col + 512, 256, [(ret[2], 0), (ret[3], 0)]), (far_col + 768, 128, [(ret[4], 0), (ret[5], 0)]))
+        return mix(y_loc, (far_col + 896, 128, [(ret[4], 1), (ret[6], 0)]))
 
     in_specs = (tok_spec, tok_spec, tok_spec, wide_spec, wide_spec, down_spec)
     return jax.shard_map(whole_step, mesh=mesh, in_specs=in_specs, out_specs=tok_spec, check_vma=False)

time: 1910 us -> 1880 us (0.984)
  waiting for transfers between devices: 803 us -> 723 us
  Pallas kernels: 824 us -> 864 us
    ppermute x15 -> x16, waiting for transfers between devices: 603 us -> 527 us  [cross(): far.append(lax.ppermute(piece, 'data', swap))]
    pallas_call x8, Pallas kernels: 406 us -> 440 us  [wide_part(): pl.pallas_call(functools.partial(wide_body, n_group, local, lo_col, cols)...]
    pallas_call x9 -> x10, Pallas kernels: 257 us -> 268 us  [down_part(): pl.pallas_call(functools.partial(down_body, n_group, local, lo_hid, adds,...]
    pallas_call x5 -> x4, Pallas kernels: 76.3 us -> 69.6 us  [mix_cols(): pl.pallas_call(functools.partial(mix_body, n_exp, tok_rows // MIX_TILE, t...]
  transfers between devices with their start and end apart: 48 -> 49, of which waited for: 15 -> 11; matrix products, arithmetic and copies ran while one was open for 5% -> 5% of each run, Pallas kernels for 41% -> 43%
where the time goes in v3:
time: 1880 us
  Pallas kernels  864 us (46%)
  waiting for transfers between devices  723 us (38%)
  starting transfers between devices  170 us (9%)
  local copies, waits for them, and re-layouts  66.6 us (4%)
  other arithmetic  47.1 us (3%)
    ppermute x16, waiting for transfers between devices, cross(): far.append(lax.ppermute(piece, 'data', swap))  527 us
    pallas_call x8, Pallas kernels, wide_part(): pl.pallas_call(functools.partial(wide_body, n_group, local, lo_col, cols)...  440 us
    pallas_call x10, Pallas kernels, down_part(): pl.pallas_call(functools.partial(down_body, n_group, local, lo_hid, adds,...  268 us
    ppermute x33, waiting for transfers between devices, exchange(): lax.ppermute(blocks[d], 'expert', [(s, (s + step * d) % n_group) for s in...  197 us
    ppermute x33, starting transfers between devices, exchange(): lax.ppermute(blocks[d], 'expert', [(s, (s + step * d) % n_group) for s in...  157 us
    pallas_call x2, Pallas kernels, pack_rows(): pl.pallas_call(functools.partial(pack_body, n_local, local, n_blk, n_grou...  85.7 us
    pallas_call x4, Pallas kernels, mix_cols(): pl.pallas_call(functools.partial(mix_body, n_exp, tok_rows // MIX_TILE, t...  69.6 us
  transfers between devices with their start and end apart: 49, of which 11 were waited for; matrix products, arithmetic and copies ran while one was open for 5% of the time, Pallas kernels for 43%

profile of v3, /device:TPU:0, one launch (start us, length us, event | category | flops | bytes accessed | tf_op | source)
XLA Modules:
  0.0 1879.6 jit_solution(4721162698129728112)
XLA Ops:
  6.4 6.7 all-reduce
  17.1 40.4 %pack_rows.2 = (bf16[1280,2048]{1,0:T(8,128)(2,1)}, bf16[1280,2048]{1,0:T(8,128)(2,1)}, bf16[1280,2048]{1,0:T(8,128)(2,1)}, bf16[1280,2048]{1,0:T(8,128)(2,1)}) custom-call(s32[136]{0:T(256)} %reshape.314.first_ref, s32[8,4096]{1,0:T(8,128)} %get-tuple-element.198.slot_ref, bf16[4096,2048]{1,0:T(8,128)(2,1)} %x_ref.11), custom_call_target="tpu_custom_call" | custom-call | flops 20000000000 | bytes 60000000 | tf_op jit(solution)/shard_map/pack_rows/pallas_call | solution.py:95
  65.8 11.3 fusion.20
  77.2 6.3 pad_maximum_fusion.1
  84.8 17.7 fusion.18
  107.1 45.3 %pack_rows.3 = (bf16[1280,2048]{1,0:T(8,128)(2,1)}, bf16[1280,2048]{1,0:T(8,128)(2,1)}, bf16[1280,2048]{1,0:T(8,128)(2,1)}, bf16[1280,2048]{1,0:T(8,128)(2,1)}) custom-call(s32[136]{0:T(256)} %reshape.314.first_ref, s32[8,4096]{1,0:T(8,128)} %get-tuple-element.198.slot_ref, bf16[4096,2048]{1,0:T(8,128)(2,1)} %x_ref.11), custom_call_target="tpu_custom_call" | custom-call | flops 20000000000 | bytes 60000000 | tf_op jit(solution)/shard_map/pack_rows/pallas_call | solution.py:95
  164.6 6.2 pad_maximum_fusion
  196.2 6.9 slice_bitcast_fusion.2
  209.0 76.1 %collective-permute-done.2.refs_3_ = bf16[1280,2048]{1,0:T(8,128)(2,1)} collective-permute-done((bf16[1280,2048]{1,0:T(8,128)(2,1)}, bf16[1280,2048]{1,0:T(8,128)(2,1)}, u32[]{:S(2)}, u32[]{:S(2)}) %collective-permute-start.2) | collective-permute-done | bytes 5242912 | tf_op jit(solution)/shard_map/ppermute | solution.py:483
  287.7 22.1 %wide_part.8.refs_7_ = bf16[5120,5632]{1,0:T(8,128)(2,1)} custom-call(s32[6]{0:T(128)} %pad_add_fusion.6.meta_ref, bf16[1280,2048]{1,0:T(8,128)(2,1)} %get-tuple-element.90.refs_0_, bf16[1280,2048]{1,0:T(8,128)(2,1)} %collective-permute-done.refs_1_, bf16[1280,2048]{1,0:T(8,128)(2,1)} %collective-permute-done.1.refs_2_, ...), custom_call_target="tpu_custom_call" | custom-call | flops 21474836480 | bytes 20971520 | tf_op jit(solution)/shard_map/wide_part/pallas_call | solution.py:192
  309.8 118.7 %collective-permute-done.11.refs_6_ = bf16[2,1024,1536]{2,1,0:T(8,128)(2,1)} collective-permute-done((bf16[2,1024,1536]{2,1,0:T(8,128)(2,1)}, bf16[2,1024,1536]{2,1,0:T(8,128)(2,1)}, u32[]{:S(2)}, u32[]{:S(2)}) %collective-permute-start.11) | collective-permute-done | bytes 6291488 | tf_op jit(solution)/shard_map/ppermute | solution.py:478
  429.3 79.2 %wide_part.9.refs_7_ = bf16[5120,5632]{1,0:T(8,128)(2,1)} custom-call(s32[6]{0:T(128)} %pad_add_fusion.6.meta_ref, bf16[1280,2048]{1,0:T(8,128)(2,1)} %get-tuple-element.90.refs_0_, bf16[1280,2048]{1,0:T(8,128)(2,1)} %collective-permute-done.refs_1_, bf16[1280,2048]{1,0:T(8,128)(2,1)} %collective-permute-done.1.refs_2_, ...), custom_call_target="tpu_custom_call", output_to_operand_aliasing={{}: (8, {})} | custom-call | flops 85899345920 | bytes 20971520 | tf_op jit(solution)/shard_map/wide_part/pallas_call | solution.py:192
  508.5 97.9 %collective-permute-done.12.refs_6_ = bf16[2,1024,512]{2,1,0:T(8,128)(2,1)} collective-permute-done((bf16[2,1024,512]{2,1,0:T(8,128)(2,1)}, bf16[2,1024,512]{2,1,0:T(8,128)(2,1)}, u32[]{:S(2)}, u32[]{:S(2)}) %collective-permute-start.12) | collective-permute-done | bytes 2097184 | tf_op jit(solution)/shard_map/ppermute | solution.py:478
  607.2 59.5 %wide_part.10.refs_7_ = bf16[5120,5632]{1,0:T(8,128)(2,1)} custom-call(s32[6]{0:T(128)} %pad_add_fusion.6.meta_ref, bf16[1280,2048]{1,0:T(8,128)(2,1)} %get-tuple-element.90.refs_0_, bf16[1280,2048]{1,0:T(8,128)(2,1)} %collective-permute-done.refs_1_, bf16[1280,2048]{1,0:T(8,128)(2,1)} %collective-permute-done.1.refs_2_, ...), custom_call_target="tpu_custom_call", output_to_operand_aliasing={{}: (8, {})} | custom-call | flops 64424509440 | bytes 20971520 | tf_op jit(solution)/shard_map/wide_part/pallas_call | solution.py:192
  666.8 59.5 %wide_part.11.h_ref = bf16[5120,5632]{1,0:T(8,128)(2,1)} custom-call(s32[6]{0:T(128)} %pad_add_fusion.6.meta_ref, bf16[1280,2048]{1,0:T(8,128)(2,1)} %get-tuple-element.90.refs_0_, bf16[1280,2048]{1,0:T(8,128)(2,1)} %collective-permute-done.refs_1_, bf16[1280,2048]{1,0:T(8,128)(2,1)} %collective-permute-done.1.refs_2_, ...), custom_call_target="tpu_custom_call", output_to_operand_aliasing={{}: (8, {})} | custom-call | flops 64424509440 | bytes 20971520 | tf_op jit(solution)/shard_map/wide_part/pallas_call | solution.py:192
  726.3 18.7 collective-permute-done.13.refs_6_
  745.9 54.9 %down_part.10 = (bf16[1280,1024]{1,0:T(8,128)(2,1)}, bf16[1280,1024]{1,0:T(8,128)(2,1)}, bf16[1280,1024]{1,0:T(8,128)(2,1)}, bf16[1280,1024]{1,0:T(8,128)(2,1)}) custom-call(s32[6]{0:T(128)} %pad_add_fusion.6.meta_ref, bf16[5120,5632]{1,0:T(8,128)(2,1)} %wide_part.11.h_ref, bf16[2,5632,1024]{2,1,0:T(8,128)(2,1)} %w_ref.3), custom_call_target="tpu_custom_call" | custom-call | flops 59055800320 | bytes 57671680 | tf_op jit(solution)/shard_map/down_part/pallas_call | solution.py:299
  800.8 46.6 %collective-permute-start.16 = (bf16[1280,1024]{1,0:T(8,128)(2,1)}, bf16[1280,1024]{1,0:T(8,128)(2,1)}, u32[]{:S(2)}, u32[]{:S(2)}) collective-permute-start(bf16[1280,1024]{1,0:T(8,128)(2,1)} %get-tuple-element.122), channel_id=1, source_target_pairs={{0,3},{1,0},{2,1},{3,2},{4,7},{5,4},{6,5},{7,6}} | collective-permute-start | bytes 7864328 | tf_op jit(solution)/shard_map/ppermute | solution.py:483
  850.1 22.0 %wide_part.12.refs_7_ = bf16[5120,5632]{1,0:T(8,128)(2,1)} custom-call(s32[6]{0:T(128)} %pad_add_fusion.4.meta_ref, bf16[1280,2048]{1,0:T(8,128)(2,1)} %get-tuple-element.96.refs_0_, bf16[1280,2048]{1,0:T(8,128)(2,1)} %collective-permute-done.3.refs_1_, bf16[1280,2048]{1,0:T(8,128)(2,1)} %collective-permute-done.4.refs_2_, ...), custom_call_target="tpu_custom_call" | custom-call | flops 21474836480 | bytes 20971520 | tf_op jit(solution)/shard_map/wide_part/pallas_call | solution.py:192
  872.1 173.5 %collective-permute-done.14.w_ref = bf16[5632,512]{1,0:T(8,128)(2,1)} collective-permute-done((bf16[5632,512]{1,0:T(8,128)(2,1)}, bf16[5632,512]{1,0:T(8,128)(2,1)}, u32[]{:S(2)}, u32[]{:S(2)}) %collective-permute-start.14) | collective-permute-done | bytes 5767200 | tf_op jit(solution)/shard_map/ppermute | solution.py:478
  1047.7 79.0 %wide_part.13.refs_7_ = bf16[5120,5632]{1,0:T(8,128)(2,1)} custom-call(s32[6]{0:T(128)} %pad_add_fusion.4.meta_ref, bf16[1280,2048]{1,0:T(8,128)(2,1)} %get-tuple-element.96.refs_0_, bf16[1280,2048]{1,0:T(8,128)(2,1)} %collective-permute-done.3.refs_1_, bf16[1280,2048]{1,0:T(8,128)(2,1)} %collective-permute-done.4.refs_2_, ...), custom_call_target="tpu_custom_call", output_to_operand_aliasing={{}: (8, {})} | custom-call | flops 85899345920 | bytes 20971520 | tf_op jit(solution)/shard_map/wide_part/pallas_call | solution.py:192
  1127.7 59.5 %wide_part.14.refs_7_ = bf16[5120,5632]{1,0:T(8,128)(2,1)} custom-call(s32[6]{0:T(128)} %pad_add_fusion.4.meta_ref, bf16[1280,2048]{1,0:T(8,128)(2,1)} %get-tuple-element.96.refs_0_, bf16[1280,2048]{1,0:T(8,128)(2,1)} %collective-permute-done.3.refs_1_, bf16[1280,2048]{1,0:T(8,128)(2,1)} %collective-permute-done.4.refs_2_, ...), custom_call_target="tpu_custom_call", output_to_operand_aliasing={{}: (8, {})} | custom-call | flops 64424509440 | bytes 20971520 | tf_op jit(solution)/shard_map/wide_part/pallas_call | solution.py:192
  1187.2 117.7 %collective-permute-done.30.w_ref = bf16[5632,256]{1,0:T(8,128)(2,1)} collective-permute-done((bf16[5632,256]{1,0:T(8,128)(2,1)}, bf16[5632,256]{1,0:T(8,128)(2,1)}, u32[]{:S(2)}, u32[]{:S(2)}) %collective-permute-start.30) | collective-permute-done | bytes 2883616 | tf_op jit(solution)/shard_map/ppermute | solution.py:478
  1305.8 59.5 %wide_part.15.h_ref = bf16[5120,5632]{1,0:T(8,128)(2,1)} custom-call(s32[6]{0:T(128)} %pad_add_fusion.4.meta_ref, bf16[1280,2048]{1,0:T(8,128)(2,1)} %get-tuple-element.96.refs_0_, bf16[1280,2048]{1,0:T(8,128)(2,1)} %collective-permute-done.3.refs_1_, bf16[1280,2048]{1,0:T(8,128)(2,1)} %collective-permute-done.4.refs_2_, ...), custom_call_target="tpu_custom_call", output_to_operand_aliasing={{}: (8, {})} | custom-call | flops 64424509440 | bytes 20971520 | tf_op jit(solution)/shard_map/wide_part/pallas_call | solution.py:192
  1365.4 54.9 %down_part.11 = (bf16[1280,1024]{1,0:T(8,128)(2,1)}, bf16[1280,1024]{1,0:T(8,128)(2,1)}, bf16[1280,1024]{1,0:T(8,128)(2,1)}, bf16[1280,1024]{1,0:T(8,128)(2,1)}) custom-call(s32[6]{0:T(128)} %pad_add_fusion.4.meta_ref, bf16[5120,5632]{1,0:T(8,128)(2,1)} %wide_part.15.h_ref, bf16[2,5632,1024]{2,1,0:T(8,128)(2,1)} %w_ref.3), custom_call_target="tpu_custom_call" | custom-call | flops 59055800320 | bytes 57671680 | tf_op jit(solution)/shard_map/down_part/pallas_call | solution.py:299
  1420.2 29.9 %down_part.12 = (bf16[1280,512]{1,0:T(8,128)(2,1)}, bf16[1280,512]{1,0:T(8,128)(2,1)}, bf16[1280,512]{1,0:T(8,128)(2,1)}, bf16[1280,512]{1,0:T(8,128)(2,1)}) custom-call(s32[6]{0:T(128)} %pad_add_fusion.6.meta_ref, bf16[5120,5632]{1,0:T(8,128)(2,1)} %wide_part.11.h_ref, bf16[5632,512]{1,0:T(8,128)(2,1)} %collective-permute-done.14.w_ref), custom_call_target="tpu_custom_call" | custom-call | flops 29527900160 | bytes 57671680 | tf_op jit(solution)/shard_map/down_part/pallas_call | solution.py:299
  1450.1 51.7 %collective-permute-start.17 = (bf16[1280,1024]{1,0:T(8,128)(2,1)}, bf16[1280,1024]{1,0:T(8,128)(2,1)}, u32[]{:S(2)}, u32[]{:S(2)}) collective-permute-start(bf16[1280,1024]{1,0:T(8,128)(2,1)} %get-tuple-element.123), channel_id=1, source_target_pairs={{0,3},{1,0},{2,1},{3,2},{4,7},{5,4},{6,5},{7,6}} | collective-permute-start | bytes 7864328 | tf_op jit(solution)/shard_map/ppermute | solution.py:483
  1502.0 29.9 %down_part.13 = (bf16[1280,512]{1,0:T(8,128)(2,1)}, bf16[1280,512]{1,0:T(8,128)(2,1)}, bf16[1280,512]{1,0:T(8,128)(2,1)}, bf16[1280,512]{1,0:T(8,128)(2,1)}) custom-call(s32[6]{0:T(128)} %pad_add_fusion.4.meta_ref, bf16[5120,5632]{1,0:T(8,128)(2,1)} %wide_part.15.h_ref, bf16[5632,512]{1,0:T(8,128)(2,1)} %collective-permute-done.15.w_ref), custom_call_target="tpu_custom_call" | custom-call | flops 29527900160 | bytes 57671680 | tf_op jit(solution)/shard_map/down_part/pallas_call | solution.py:299
  1531.9 11.6 collective-permute-start.24
  1543.5 15.9 collective-permute-done.17.refs_3_
  1559.4 56.2 %collective-permute-done.19.refs_5_ = bf16[1280,1024]{1,0:T(8,128)(2,1)} collective-permute-done((bf16[1280,1024]{1,0:T(8,128)(2,1)}, bf16[1280,1024]{1,0:T(8,128)(2,1)}, u32[]{:S(2)}, u32[]{:S(2)}) %collective-permute-start.19) | collective-permute-done | bytes 2621472 | tf_op jit(solution)/shard_map/ppermute | solution.py:483
  1617.3 27.4 %mix_cols.4 = (bf16[4096,2048]{1,0:T(8,128)(2,1)}, s32[1]{0:T(128)}) custom-call(s32[1]{0:T(128)} %bitcast.13.col_ref, s32[1024]{0:T(1024)} %mul.74.chunk_ref, s32[4096,2]{1,0:T(8,128)} %copy.34.pos_ref, f32[4096,2]{1,0:T(8,128)} %copy.35.gate_ref, bf16[4096,2048]{1,0:T(8,128)(2,1)} %x_ref.11, bf16[1280,1024]{1,0:T(8,128)(2,1)} %get-tuple-element.112.refs_0_, ...), custom_call_target="tpu_custom_call" | custom-call | flops 20480000000 | bytes 20480000 | tf_op jit(solution)/shard_map/mix_cols/pallas_call | solution.py:385
  1645.9 18.7 down_part.14
  1665.6 7.1 collective-permute-start.27
  1672.9 18.7 down_part.15
  1691.9 6.9 collective-permute-start.34
  1702.2 28.5 %collective-permute-done.27.refs_5_ = bf16[1280,512]{1,0:T(8,128)(2,1)} collective-permute-done((bf16[1280,512]{1,0:T(8,128)(2,1)}, bf16[1280,512]{1,0:T(8,128)(2,1)}, u32[]{:S(2)}, u32[]{:S(2)}) %collective-permute-start.27) | collective-permute-done | bytes 1310752 | tf_op jit(solution)/shard_map/ppermute | solution.py:483
  1731.0 16.7 mix_cols.5
  1748.8 18.7 down_part.16
  1767.5 7.0 collective-permute-start.35
  1778.2 18.1 down_part.17
  1796.4 8.2 collective-permute-done.37.refs_5_
  1806.3 11.6 collective-permute-done.40.refs_10_.refs_2_
  1820.3 14.4 down_part.18.refs_0_
  1834.7 9.8 down_part.19
  1844.5 7.1 collective-permute-start.46
  1852.4 15.4 mix_cols.6
  1869.3 10.1 mix_cols.7
  (179 shorter events, 97.8 us)
Async XLA Ops:
  57.5 151.5 %collective-permute-start = (bf16[1280,2048]{1,0:T(8,128)(2,1)}, bf16[1280,2048]{1,0:T(8,128)(2,1)}, u32[]{:S(2)}, u32[]{:S(2)}) collective-permute-start(bf16[1280,2048]{1,0:T(8,128)(2,1)} %get-tuple-element.93), channel_id=1, source_target_pairs={{0,1},{1,2},{2,3},{3,0},{4,5},{5,6},{6,7},{7,4}} | collective-permute-start | bytes 15728648 | tf_op jit(solution)/shard_map/ppermute | solution.py:483
  57.5 151.5 %collective-permute-start.1 = (bf16[1280,2048]{1,0:T(8,128)(2,1)}, bf16[1280,2048]{1,0:T(8,128)(2,1)}, u32[]{:S(2)}, u32[]{:S(2)}) collective-permute-start(bf16[1280,2048]{1,0:T(8,128)(2,1)} %get-tuple-element.94), channel_id=1, source_target_pairs={{0,2},{1,3},{2,0},{3,1},{4,6},{5,7},{6,4},{7,5}} | collective-permute-start | bytes 15728648 | tf_op jit(solution)/shard_map/ppermute | solution.py:483
  59.5 225.5 %collective-permute-start.2 = (bf16[1280,2048]{1,0:T(8,128)(2,1)}, bf16[1280,2048]{1,0:T(8,128)(2,1)}, u32[]{:S(2)}, u32[]{:S(2)}) collective-permute-start(bf16[1280,2048]{1,0:T(8,128)(2,1)} %get-tuple-element.95), channel_id=1, source_target_pairs={{0,3},{1,0},{2,1},{3,2},{4,7},{5,4},{6,5},{7,6}} | collective-permute-start | bytes 15728648 | tf_op jit(solution)/shard_map/ppermute | solution.py:483
  65.1 127.7 %collective-permute-start.10 = (bf16[2,1024,512]{2,1,0:T(8,128)(2,1)}, bf16[2,1024,512]{2,1,0:T(8,128)(2,1)}, u32[]{:S(2)}, u32[]{:S(2)}) collective-permute-start(bf16[2,1024,512]{2,1,0:T(8,128)(2,1)} %pad_maximum_fusion.6), channel_id=1, source_target_pairs={{0,4},{4,0},{1,5},{5,1},{2,6},{6,2},{3,7},{7,3}} | collective-permute-start | bytes 6291464 | tf_op jit(solution)/shard_map/ppermute | solution.py:478
  83.5 226.3 %collective-permute-start.6 = (bf16[2,1024,2048]{2,1,0:T(8,128)(2,1)}, bf16[2,1024,2048]{2,1,0:T(8,128)(2,1)}, u32[]{:S(2)}, u32[]{:S(2)}) collective-permute-start(bf16[2,1024,2048]{2,1,0:T(8,128)(2,1)} %pad_maximum_fusion.1), channel_id=1, source_target_pairs={{0,4},{4,0},{1,5},{5,1},{2,6},{6,2},{3,7},{7,3}} | collective-permute-start | bytes 25165832 | tf_op jit(solution)/shard_map/ppermute | solution.py:478
  192.8 235.7 %collective-permute-start.11 = (bf16[2,1024,1536]{2,1,0:T(8,128)(2,1)}, bf16[2,1024,1536]{2,1,0:T(8,128)(2,1)}, u32[]{:S(2)}, u32[]{:S(2)}) collective-permute-start(bf16[2,1024,1536]{2,1,0:T(8,128)(2,1)} %pad_maximum_fusion.5), channel_id=1, source_target_pairs={{0,4},{4,0},{1,5},{5,1},{2,6},{6,2},{3,7},{7,3}} | collective-permute-start | bytes 18874376 | tf_op jit(solution)/shard_map/ppermute | solution.py:478
  285.1 515.7 %collective-permute-start.3 = (bf16[1280,2048]{1,0:T(8,128)(2,1)}, bf16[1280,2048]{1,0:T(8,128)(2,1)}, u32[]{:S(2)}, u32[]{:S(2)}) collective-permute-start(bf16[1280,2048]{1,0:T(8,128)(2,1)} %get-tuple-element.98), channel_id=1, source_target_pairs={{0,1},{1,2},{2,3},{3,0},{4,5},{5,6},{6,7},{7,4}} | collective-permute-start | bytes 15728648 | tf_op jit(solution)/shard_map/ppermute | solution.py:483
  285.6 561.8 %collective-permute-start.4 = (bf16[1280,2048]{1,0:T(8,128)(2,1)}, bf16[1280,2048]{1,0:T(8,128)(2,1)}, u32[]{:S(2)}, u32[]{:S(2)}) collective-permute-start(bf16[1280,2048]{1,0:T(8,128)(2,1)} %get-tuple-element.100), channel_id=1, source_target_pairs={{0,2},{1,3},{2,0},{3,1},{4,6},{5,7},{6,4},{7,5}} | collective-permute-start | bytes 15728648 | tf_op jit(solution)/shard_map/ppermute | solution.py:483
  287.7 562.2 %collective-permute-start.5 = (bf16[1280,2048]{1,0:T(8,128)(2,1)}, bf16[1280,2048]{1,0:T(8,128)(2,1)}, u32[]{:S(2)}, u32[]{:S(2)}) collective-permute-start(bf16[1280,2048]{1,0:T(8,128)(2,1)} %get-tuple-element.102), channel_id=1, source_target_pairs={{0,3},{1,0},{2,1},{3,2},{4,7},{5,4},{6,5},{7,6}} | collective-permute-start | bytes 15728648 | tf_op jit(solution)/shard_map/ppermute | solution.py:483
  309.8 357.0 %collective-permute-start.7 = (bf16[2,1024,1536]{2,1,0:T(8,128)(2,1)}, bf16[2,1024,1536]{2,1,0:T(8,128)(2,1)}, u32[]{:S(2)}, u32[]{:S(2)}) collective-permute-start(bf16[2,1024,1536]{2,1,0:T(8,128)(2,1)} %pad_maximum_fusion.3), channel_id=1, source_target_pairs={{0,4},{4,0},{1,5},{5,1},{2,6},{6,2},{3,7},{7,3}} | collective-permute-start | bytes 18874376 | tf_op jit(solution)/shard_map/ppermute | solution.py:478
  428.5 177.8 %collective-permute-start.12 = (bf16[2,1024,512]{2,1,0:T(8,128)(2,1)}, bf16[2,1024,512]{2,1,0:T(8,128)(2,1)}, u32[]{:S(2)}, u32[]{:S(2)}) collective-permute-start(bf16[2,1024,512]{2,1,0:T(8,128)(2,1)} %pad_maximum_fusion.7), channel_id=1, source_target_pairs={{0,4},{4,0},{1,5},{5,1},{2,6},{6,2},{3,7},{7,3}} | collective-permute-start | bytes 6291464 | tf_op jit(solution)/shard_map/ppermute | solution.py:478
  606.4 138.7 %collective-permute-start.13 = (bf16[2,1024,1536]{2,1,0:T(8,128)(2,1)}, bf16[2,1024,1536]{2,1,0:T(8,128)(2,1)}, u32[]{:S(2)}, u32[]{:S(2)}) collective-permute-start(bf16[2,1024,1536]{2,1,0:T(8,128)(2,1)} %pad_maximum_fusion.4), channel_id=1, source_target_pairs={{0,4},{4,0},{1,5},{5,1},{2,6},{6,2},{3,7},{7,3}} | collective-permute-start | bytes 18874376 | tf_op jit(solution)/shard_map/ppermute | solution.py:478
  666.7 379.8 %collective-permute-start.8 = (bf16[2,1024,2048]{2,1,0:T(8,128)(2,1)}, bf16[2,1024,2048]{2,1,0:T(8,128)(2,1)}, u32[]{:S(2)}, u32[]{:S(2)}) collective-permute-start(bf16[2,1024,2048]{2,1,0:T(8,128)(2,1)} %pad_maximum_fusion), channel_id=1, source_target_pairs={{0,4},{4,0},{1,5},{5,1},{2,6},{6,2},{3,7},{7,3}} | collective-permute-start | bytes 25165832 | tf_op jit(solution)/shard_map/ppermute | solution.py:478
  745.0 300.6 %collective-permute-start.14 = (bf16[5632,512]{1,0:T(8,128)(2,1)}, bf16[5632,512]{1,0:T(8,128)(2,1)}, u32[]{:S(2)}, u32[]{:S(2)}) collective-permute-start(bf16[5632,512]{1,0:T(8,128)(2,1)} %get-tuple-element.116), channel_id=1, source_target_pairs={{0,4},{4,0},{1,5},{5,1},{2,6},{6,2},{3,7},{7,3}} | collective-permute-start | bytes 17301512 | tf_op jit(solution)/shard_map/ppermute | solution.py:478
  800.8 701.0 %collective-permute-start.16 = (bf16[1280,1024]{1,0:T(8,128)(2,1)}, bf16[1280,1024]{1,0:T(8,128)(2,1)}, u32[]{:S(2)}, u32[]{:S(2)}) collective-permute-start(bf16[1280,1024]{1,0:T(8,128)(2,1)} %get-tuple-element.122), channel_id=1, source_target_pairs={{0,3},{1,0},{2,1},{3,2},{4,7},{5,4},{6,5},{7,6}} | collective-permute-start | bytes 7864328 | tf_op jit(solution)/shard_map/ppermute | solution.py:483
  847.4 684.5 %collective-permute-start.18 = (bf16[1280,1024]{1,0:T(8,128)(2,1)}, bf16[1280,1024]{1,0:T(8,128)(2,1)}, u32[]{:S(2)}, u32[]{:S(2)}) collective-permute-start(bf16[1280,1024]{1,0:T(8,128)(2,1)} %get-tuple-element.124), channel_id=1, source_target_pairs={{0,2},{1,3},{2,0},{3,1},{4,6},{5,7},{6,4},{7,5}} | collective-permute-start | bytes 7864328 | tf_op jit(solution)/shard_map/ppermute | solution.py:483
  849.9 693.6 %collective-permute-start.20 = (bf16[1280,1024]{1,0:T(8,128)(2,1)}, bf16[1280,1024]{1,0:T(8,128)(2,1)}, u32[]{:S(2)}, u32[]{:S(2)}) collective-permute-start(bf16[1280,1024]{1,0:T(8,128)(2,1)} %get-tuple-element.126), channel_id=1, source_target_pairs={{0,1},{1,2},{2,3},{3,0},{4,5},{5,6},{6,7},{7,4}} | collective-permute-start | bytes 7864328 | tf_op jit(solution)/shard_map/ppermute | solution.py:483
  1045.6 81.1 %collective-permute-start.22 = (bf16[5632,256]{1,0:T(8,128)(2,1)}, bf16[5632,256]{1,0:T(8,128)(2,1)}, u32[]{:S(2)}, u32[]{:S(2)}) collective-permute-start(bf16[5632,256]{1,0:T(8,128)(2,1)} %get-tuple-element.129), channel_id=1, source_target_pairs={{0,4},{4,0},{1,5},{5,1},{2,6},{6,2},{3,7},{7,3}} | collective-permute-start | bytes 8650760 | tf_op jit(solution)/shard_map/ppermute | solution.py:478
  1046.6 258.3 %collective-permute-start.9 = (bf16[2,1024,1536]{2,1,0:T(8,128)(2,1)}, bf16[2,1024,1536]{2,1,0:T(8,128)(2,1)}, u32[]{:S(2)}, u32[]{:S(2)}) collective-permute-start(bf16[2,1024,1536]{2,1,0:T(8,128)(2,1)} %pad_maximum_fusion.2), channel_id=1, source_target_pairs={{0,4},{4,0},{1,5},{5,1},{2,6},{6,2},{3,7},{7,3}} | collective-permute-start | bytes 18874376 | tf_op jit(solution)/shard_map/ppermute | solution.py:478
  1126.7 178.2 %collective-permute-start.30 = (bf16[5632,256]{1,0:T(8,128)(2,1)}, bf16[5632,256]{1,0:T(8,128)(2,1)}, u32[]{:S(2)}, u32[]{:S(2)}) collective-permute-start(bf16[5632,256]{1,0:T(8,128)(2,1)} %get-tuple-element.143), channel_id=1, source_target_pairs={{0,4},{4,0},{1,5},{5,1},{2,6},{6,2},{3,7},{7,3}} | collective-permute-start | bytes 8650760 | tf_op jit(solution)/shard_map/ppermute | solution.py:478
  1304.9 196.9 %collective-permute-start.15 = (bf16[5632,512]{1,0:T(8,128)(2,1)}, bf16[5632,512]{1,0:T(8,128)(2,1)}, u32[]{:S(2)}, u32[]{:S(2)}) collective-permute-start(bf16[5632,512]{1,0:T(8,128)(2,1)} %get-tuple-element.119), channel_id=1, source_target_pairs={{0,4},{4,0},{1,5},{5,1},{2,6},{6,2},{3,7},{7,3}} | collective-permute-start | bytes 17301512 | tf_op jit(solution)/shard_map/ppermute | solution.py:478
  1450.1 109.3 %collective-permute-start.17 = (bf16[1280,1024]{1,0:T(8,128)(2,1)}, bf16[1280,1024]{1,0:T(8,128)(2,1)}, u32[]{:S(2)}, u32[]{:S(2)}) collective-permute-start(bf16[1280,1024]{1,0:T(8,128)(2,1)} %get-tuple-element.123), channel_id=1, source_target_pairs={{0,3},{1,0},{2,1},{3,2},{4,7},{5,4},{6,5},{7,6}} | collective-permute-start | bytes 7864328 | tf_op jit(solution)/shard_map/ppermute | solution.py:483
  1501.8 113.7 %collective-permute-start.19 = (bf16[1280,1024]{1,0:T(8,128)(2,1)}, bf16[1280,1024]{1,0:T(8,128)(2,1)}, u32[]{:S(2)}, u32[]{:S(2)}) collective-permute-start(bf16[1280,1024]{1,0:T(8,128)(2,1)} %get-tuple-element.125), channel_id=1, source_target_pairs={{0,2},{1,3},{2,0},{3,1},{4,6},{5,7},{6,4},{7,5}} | collective-permute-start | bytes 7864328 | tf_op jit(solution)/shard_map/ppermute | solution.py:483
  1501.8 115.5 %collective-permute-start.21 = (bf16[1280,1024]{1,0:T(8,128)(2,1)}, bf16[1280,1024]{1,0:T(8,128)(2,1)}, u32[]{:S(2)}, u32[]{:S(2)}) collective-permute-start(bf16[1280,1024]{1,0:T(8,128)(2,1)} %get-tuple-element.127), channel_id=1, source_target_pairs={{0,1},{1,2},{2,3},{3,0},{4,5},{5,6},{6,7},{7,4}} | collective-permute-start | bytes 7864328 | tf_op jit(solution)/shard_map/ppermute | solution.py:483
  1531.9 133.7 %collective-permute-start.24 = (bf16[1280,512]{1,0:T(8,128)(2,1)}, bf16[1280,512]{1,0:T(8,128)(2,1)}, u32[]{:S(2)}, u32[]{:S(2)}) collective-permute-start(bf16[1280,512]{1,0:T(8,128)(2,1)} %get-tuple-element.135), channel_id=1, source_target_pairs={{0,3},{1,0},{2,1},{3,2},{4,7},{5,4},{6,5},{7,6}} | collective-permute-start | bytes 3932168 | tf_op jit(solution)/shard_map/ppermute | solution.py:483
  1543.5 148.1 %collective-permute-start.26 = (bf16[1280,512]{1,0:T(8,128)(2,1)}, bf16[1280,512]{1,0:T(8,128)(2,1)}, u32[]{:S(2)}, u32[]{:S(2)}) collective-permute-start(bf16[1280,512]{1,0:T(8,128)(2,1)} %get-tuple-element.137), channel_id=1, source_target_pairs={{0,2},{1,3},{2,0},{3,1},{4,6},{5,7},{6,4},{7,5}} | collective-permute-start | bytes 3932168 | tf_op jit(solution)/shard_map/ppermute | solution.py:483
  1559.4 132.5 %collective-permute-start.28 = (bf16[1280,512]{1,0:T(8,128)(2,1)}, bf16[1280,512]{1,0:T(8,128)(2,1)}, u32[]{:S(2)}, u32[]{:S(2)}) collective-permute-start(bf16[1280,512]{1,0:T(8,128)(2,1)} %get-tuple-element.139), channel_id=1, source_target_pairs={{0,1},{1,2},{2,3},{3,0},{4,5},{5,6},{6,7},{7,4}} | collective-permute-start | bytes 3932168 | tf_op jit(solution)/shard_map/ppermute | solution.py:483
  1615.6 57.1 %collective-permute-start.23 = (bf16[5632,256]{1,0:T(8,128)(2,1)}, bf16[5632,256]{1,0:T(8,128)(2,1)}, u32[]{:S(2)}, u32[]{:S(2)}) collective-permute-start(bf16[5632,256]{1,0:T(8,128)(2,1)} %get-tuple-element.132), channel_id=1, source_target_pairs={{0,4},{4,0},{1,5},{5,1},{2,6},{6,2},{3,7},{7,3}} | collective-permute-start | bytes 8650760 | tf_op jit(solution)/shard_map/ppermute | solution.py:478
  1664.6 34.1 %collective-permute-start.25 = (bf16[1280,512]{1,0:T(8,128)(2,1)}, bf16[1280,512]{1,0:T(8,128)(2,1)}, u32[]{:S(2)}, u32[]{:S(2)}) collective-permute-start(bf16[1280,512]{1,0:T(8,128)(2,1)} %get-tuple-element.136), channel_id=1, source_target_pairs={{0,3},{1,0},{2,1},{3,2},{4,7},{5,4},{6,5},{7,6}} | collective-permute-start | bytes 3932168 | tf_op jit(solution)/shard_map/ppermute | solution.py:483
  1665.6 65.1 %collective-permute-start.27 = (bf16[1280,512]{1,0:T(8,128)(2,1)}, bf16[1280,512]{1,0:T(8,128)(2,1)}, u32[]{:S(2)}, u32[]{:S(2)}) collective-permute-start(bf16[1280,512]{1,0:T(8,128)(2,1)} %get-tuple-element.138), channel_id=1, source_target_pairs={{0,2},{1,3},{2,0},{3,1},{4,6},{5,7},{6,4},{7,5}} | collective-permute-start | bytes 3932168 | tf_op jit(solution)/shard_map/ppermute | solution.py:483
  1672.7 58.0 %collective-permute-start.29 = (bf16[1280,512]{1,0:T(8,128)(2,1)}, bf16[1280,512]{1,0:T(8,128)(2,1)}, u32[]{:S(2)}, u32[]{:S(2)}) collective-permute-start(bf16[1280,512]{1,0:T(8,128)(2,1)} %get-tuple-element.140), channel_id=1, source_target_pairs={{0,1},{1,2},{2,3},{3,0},{4,5},{5,6},{6,7},{7,4}} | collective-permute-start | bytes 3932168 | tf_op jit(solution)/shard_map/ppermute | solution.py:483
  1691.6 82.9 %collective-permute-start.32 = (bf16[4096,128]{1,0:T(8,128)(2,1)}, bf16[4096,128]{1,0:T(8,128)(2,1)}, u32[]{:S(2)}, u32[]{:S(2)}) collective-permute-start(bf16[4096,128]{1,0:T(8,128)(2,1)} %slice_bitcast_fusion.6), channel_id=1, source_target_pairs={{0,4},{4,0},{1,5},{5,1},{2,6},{6,2},{3,7},{7,3}} | collective-permute-start | bytes 3145736 | tf_op jit(solution)/shard_map/ppermute | solution.py:478
  1691.9 82.8 %collective-permute-start.34 = (bf16[1280,256]{1,0:T(8,128)(2,1)}, bf16[1280,256]{1,0:T(8,128)(2,1)S(1)}, u32[]{:S(2)}, u32[]{:S(2)}) collective-permute-start(bf16[1280,256]{1,0:T(8,128)(2,1)} %get-tuple-element.154), channel_id=1, source_target_pairs={{0,3},{1,0},{2,1},{3,2},{4,7},{5,4},{6,5},{7,6}} | collective-permute-start | bytes 1966088 | tf_op jit(solution)/shard_map/ppermute | solution.py:483
  1698.8 76.1 %collective-permute-start.36 = (bf16[1280,256]{1,0:T(8,128)(2,1)}, bf16[1280,256]{1,0:T(8,128)(2,1)}, u32[]{:S(2)}, u32[]{:S(2)}) collective-permute-start(bf16[1280,256]{1,0:T(8,128)(2,1)} %get-tuple-element.156), channel_id=1, source_target_pairs={{0,2},{1,3},{2,0},{3,1},{4,6},{5,7},{6,4},{7,5}} | collective-permute-start | bytes 1966088 | tf_op jit(solution)/shard_map/ppermute | solution.py:483
  1730.7 45.8 %collective-permute-start.38 = (bf16[1280,256]{1,0:T(8,128)(2,1)}, bf16[1280,256]{1,0:T(8,128)(2,1)}, u32[]{:S(2)}, u32[]{:S(2)}) collective-permute-start(bf16[1280,256]{1,0:T(8,128)(2,1)} %get-tuple-element.158), channel_id=1, source_target_pairs={{0,1},{1,2},{2,3},{3,0},{4,5},{5,6},{6,7},{7,4}} | collective-permute-start | bytes 1966088 | tf_op jit(solution)/shard_map/ppermute | solution.py:483
  1730.7 36.8 %collective-permute-start.31 = (bf16[5632,128]{1,0:T(8,128)(2,1)}, bf16[5632,128]{1,0:T(8,128)(2,1)}, u32[]{:S(2)}, u32[]{:S(2)}) collective-permute-start(bf16[5632,128]{1,0:T(8,128)(2,1)} %slice_bitcast_fusion.5), channel_id=1, source_target_pairs={{0,4},{4,0},{1,5},{5,1},{2,6},{6,2},{3,7},{7,3}} | collective-permute-start | bytes 4325384 | tf_op jit(solution)/shard_map/ppermute | solution.py:478
  1767.5 28.8 %collective-permute-start.35 = (bf16[1280,256]{1,0:T(8,128)(2,1)}, bf16[1280,256]{1,0:T(8,128)(2,1)}, u32[]{:S(2)}, u32[]{:S(2)}) collective-permute-start(bf16[1280,256]{1,0:T(8,128)(2,1)} %get-tuple-element.155), channel_id=1, source_target_pairs={{0,3},{1,0},{2,1},{3,2},{4,7},{5,4},{6,5},{7,6}} | collective-permute-start | bytes 1966088 | tf_op jit(solution)/shard_map/ppermute | solution.py:483
  1774.5 30.1 %collective-permute-start.37 = (bf16[1280,256]{1,0:T(8,128)(2,1)}, bf16[1280,256]{1,0:T(8,128)(2,1)}, u32[]{:S(2)}, u32[]{:S(2)}) collective-permute-start(bf16[1280,256]{1,0:T(8,128)(2,1)} %get-tuple-element.157), channel_id=1, source_target_pairs={{0,2},{1,3},{2,0},{3,1},{4,6},{5,7},{6,4},{7,5}} | collective-permute-start | bytes 1966088 | tf_op jit(solution)/shard_map/ppermute | solution.py:483
  1774.7 29.9 %collective-permute-start.39 = (bf16[1280,256]{1,0:T(8,128)(2,1)}, bf16[1280,256]{1,0:T(8,128)(2,1)}, u32[]{:S(2)}, u32[]{:S(2)}) collective-permute-start(bf16[1280,256]{1,0:T(8,128)(2,1)} %get-tuple-element.159), channel_id=1, source_target_pairs={{0,1},{1,2},{2,3},{3,0},{4,5},{5,6},{6,7},{7,4}} | collective-permute-start | bytes 1966088 | tf_op jit(solution)/shard_map/ppermute | solution.py:483
  1775.5 42.4 %collective-permute-start.40 = (bf16[1280,256]{1,0:T(8,128)(2,1)}, bf16[1280,256]{1,0:T(8,128)(2,1)S(1)}, u32[]{:S(2)}, u32[]{:S(2)}) collective-permute-start(bf16[1280,256]{1,0:T(8,128)(2,1)} %get-tuple-element.160), channel_id=1, source_target_pairs={{0,3},{1,0},{2,1},{3,2},{4,7},{5,4},{6,5},{7,6}} | collective-permute-start | bytes 1966088 | tf_op jit(solution)/shard_map/ppermute | solution.py:483
  1776.5 41.7 %collective-permute-start.33 = (bf16[1536,128]{1,0:T(8,128)(2,1)}, bf16[1536,128]{1,0:T(8,128)(2,1)}, u32[]{:S(2)}, u32[]{:S(2)}) collective-permute-start(bf16[1536,128]{1,0:T(8,128)(2,1)} %slice_bitcast_fusion.7), channel_id=1, source_target_pairs={{0,4},{4,0},{1,5},{5,1},{2,6},{6,2},{3,7},{7,3}} | collective-permute-start | bytes 1179656 | tf_op jit(solution)/shard_map/ppermute | solution.py:478
  1796.3 48.2 %collective-permute-start.42 = (bf16[1280,256]{1,0:T(8,128)(2,1)}, bf16[1280,256]{1,0:T(8,128)(2,1)}, u32[]{:S(2)}, u32[]{:S(2)}) collective-permute-start(bf16[1280,256]{1,0:T(8,128)(2,1)} %get-tuple-element.162), channel_id=1, source_target_pairs={{0,2},{1,3},{2,0},{3,1},{4,6},{5,7},{6,4},{7,5}} | collective-permute-start | bytes 1966088 | tf_op jit(solution)/shard_map/ppermute | solution.py:483
  1804.6 47.0 %collective-permute-start.44 = (bf16[1280,256]{1,0:T(8,128)(2,1)}, bf16[1280,256]{1,0:T(8,128)(2,1)}, u32[]{:S(2)}, u32[]{:S(2)}) collective-permute-start(bf16[1280,256]{1,0:T(8,128)(2,1)} %get-tuple-element.164), channel_id=1, source_target_pairs={{0,1},{1,2},{2,3},{3,0},{4,5},{5,6},{6,7},{7,4}} | collective-permute-start | bytes 1966088 | tf_op jit(solution)/shard_map/ppermute | solution.py:483
  1804.6 47.0 %collective-permute-start.41 = (bf16[1280,128]{1,0:T(8,128)(2,1)}, bf16[1280,128]{1,0:T(8,128)(2,1)S(1)}, u32[]{:S(2)}, u32[]{:S(2)}) collective-permute-start(bf16[1280,128]{1,0:T(8,128)(2,1)} %get-tuple-element.161), channel_id=1, source_target_pairs={{0,3},{1,0},{2,1},{3,2},{4,7},{5,4},{6,5},{7,6}} | collective-permute-start | bytes 983048 | tf_op jit(solution)/shard_map/ppermute | solution.py:483
  1818.0 33.8 %collective-permute-start.43 = (bf16[1280,128]{1,0:T(8,128)(2,1)}, bf16[1280,128]{1,0:T(8,128)(2,1)}, u32[]{:S(2)}, u32[]{:S(2)}) collective-permute-start(bf16[1280,128]{1,0:T(8,128)(2,1)} %get-tuple-element.163), channel_id=1, source_target_pairs={{0,2},{1,3},{2,0},{3,1},{4,6},{5,7},{6,4},{7,5}} | collective-permute-start | bytes 983048 | tf_op jit(solution)/shard_map/ppermute | solution.py:483
  1818.2 33.6 %collective-permute-start.45 = (bf16[1280,128]{1,0:T(8,128)(2,1)}, bf16[1280,128]{1,0:T(8,128)(2,1)}, u32[]{:S(2)}, u32[]{:S(2)}) collective-permute-start(bf16[1280,128]{1,0:T(8,128)(2,1)} %get-tuple-element.165), channel_id=1, source_target_pairs={{0,1},{1,2},{2,3},{3,0},{4,5},{5,6},{6,7},{7,4}} | collective-permute-start | bytes 983048 | tf_op jit(solution)/shard_map/ppermute | solution.py:483
  1844.5 23.9 %collective-permute-start.46 = (bf16[1280,128]{1,0:T(8,128)(2,1)}, bf16[1280,128]{1,0:T(8,128)(2,1)S(1)}, u32[]{:S(2)}, u32[]{:S(2)}) collective-permute-start(bf16[1280,128]{1,0:T(8,128)(2,1)} %get-tuple-element.168), channel_id=1, source_target_pairs={{0,3},{1,0},{2,1},{3,2},{4,7},{5,4},{6,5},{7,6}} | collective-permute-start | bytes 983048 | tf_op jit(solution)/shard_map/ppermute | solution.py:483
  1851.7 16.8 collective-permute-start.48
  (21 other events, 311.6 us)

commit v4 on v3

--- a/solution.py
+++ b/solution.py
@@ -16,10 +16,8 @@
 TILE = 256
 TOK_BLOCK = 256
 MIX_TILE = 128
-MIX_UNROLL = 4
 ALIGN = 16
 REACH = 512
-DEEP = 4
 DOWN_BLOCK = 512
 SUB = 512
 WIDE_CHUNKS = (512, 2048, 1536, 1536)
@@ -210,7 +208,7 @@
     )(*args)
 
 
-def down_body(n_group, local, lo_hid, adds, partial, meta_ref, h_ref, w_ref, *refs):
+def down_body(n_group, local, lo_hid, adds, partial, deep, pair_size, meta_ref, h_ref, w_ref, *refs):
     sum_ref, refs = (refs[0], refs[1:]) if adds else (None, refs)
     n_out = 1 if partial else n_group
     out_refs = refs[:n_out]
@@ -220,67 +218,85 @@
     block = min(w_buf.shape[1], DOWN_BLOCK)
 
     def fetches(i):
-        copies = [pltpu.make_async_copy(h_ref.at[tile_at(i), hid], h_buf.at[i % DEEP], h_sems.at[i % DEEP])]
+        copies = [pltpu.make_async_copy(h_ref.at[tile_at(i), hid], h_buf.at[i % deep], h_sems.at[i % deep])]
         if adds:
-            copies.append(pltpu.make_async_copy(sum_ref.at[tile_at(i), :], sum_buf.at[i % DEEP], sum_sems.at[i % DEEP]))
+            copies.append(pltpu.make_async_copy(sum_ref.at[tile_at(i), :], sum_buf.at[i % deep], sum_sems.at[i % deep]))
         return copies
 
     def sent(i):
-        pltpu.make_async_copy(out_buf.at[i % 2], out_refs[0].at[tile_at(0), :], out_sems.at[i % 2]).wait()
+        pltpu.make_async_copy(out_buf.at[i % deep], out_refs[0].at[tile_at(0), :], out_sems.at[i % deep]).wait()
 
     def send(i, there, tile):
-        pltpu.make_async_copy(out_buf.at[i % 2], there.at[tile_at(tile), :], out_sems.at[i % 2]).start()
-
-    for i in range(DEEP - 1):
+        pltpu.make_async_copy(out_buf.at[i % deep], there.at[tile_at(tile), :], out_sems.at[i % deep]).start()
+
+    copy = pltpu.make_async_copy(w_ref if local is None else w_ref.at[local], w_buf, sem)
+    copy.start()
+    for i in range(deep - pair_size):
 
         @pl.when(i < n_live)
         def _():
-            for copy in fetches(i):
-                copy.start()
-
-    copy = pltpu.make_async_copy(w_ref if local is None else w_ref.at[local], w_buf, sem)
-    copy.start()
+            for fetch in fetches(i):
+                fetch.start()
+
     copy.wait()
 
-    def step(i, carry):
-        @pl.when(i + DEEP - 1 < n_live)
-        def _():
-            for copy in fetches(i + DEEP - 1):
-                copy.start()
-
-        for copy in fetches(i):
-            copy.wait()
-
-        @pl.when(i >= 2)
+    def step(pair, carry):
+        for k in range(pair_size):
+            i = pair * pair_size + k
+
+            @pl.when(i + deep - pair_size < n_live)
+            def _():
+                for fetch in fetches(i + deep - pair_size):
+                    fetch.start()
+
+        for k in range(pair_size):
+            i = pair * pair_size + k
+
+            @pl.when(i < n_live)
+            def _():
+                for fetch in fetches(i):
+                    fetch.wait()
+
+            @pl.when((i >= deep) & (i - deep < n_live))
+            def _():
+                sent(i)
+
+        slots = pl.ds(pair % (deep // pair_size) * pair_size, pair_size)
+
+        def part(j, carry):
+            span = pl.ds(pl.multiple_of(j * block, block), block)
+            total = jnp.dot(h_buf[slots].reshape(pair_size * TILE, -1), w_buf[:, span], preferred_element_type=F32)
+            if adds:
+                total += sum_buf[slots, :, span].reshape(pair_size * TILE, -1)
+            out_buf[slots, :, span] = total.astype(out_buf.dtype).reshape(pair_size, TILE, -1)
+            return carry
+
+        lax.fori_loop(0, w_buf.shape[1] // block, part, 0)
+        for k in range(pair_size):
+            i = pair * pair_size + k
+            if partial:
+
+                @pl.when(i < n_live)
+                def _():
+                    send(i, out_refs[0], i)
+
+                continue
+            for d in range(n_group):
+
+                @pl.when((i >= meta_ref[1 + d]) & (i < meta_ref[2 + d]))
+                def _():
+                    send(i, out_refs[d], i - meta_ref[1 + d])
+
+        return carry
+
+    n_pair = (n_live + pair_size - 1) // pair_size
+    lax.fori_loop(0, n_pair, step, 0)
+    for back in range(deep, 0, -1):
+        i = n_pair * pair_size - back
+
+        @pl.when((i >= 0) & (i < n_live))
         def _():
             sent(i)
-
-        def part(j, carry):
-            span = pl.ds(pl.multiple_of(j * block, block), block)
-            total = jnp.dot(h_buf[i % DEEP], w_buf[:, span], preferred_element_type=F32)
-            if adds:
-                total += sum_buf[i % DEEP, :, span]
-            out_buf[i % 2, :, span] = total.astype(out_buf.dtype)
-            return carry
-
-        lax.fori_loop(0, w_buf.shape[1] // block, part, 0)
-        if partial:
-            send(i, out_refs[0], i)
-            return carry
-        for d in range(n_group):
-
-            @pl.when((i >= meta_ref[1 + d]) & (i < meta_ref[2 + d]))
-            def _():
-                send(i, out_refs[d], i - meta_ref[1 + d])
-
-        return carry
-
-    lax.fori_loop(0, n_live, step, 0)
-    for back in (2, 1):
-
-        @pl.when(n_live >= back)
-        def _():
-            sent(n_live - back)
 
     for d in range(0 if partial else n_group):
         @pl.when(meta_ref[1 + d] == meta_ref[2 + d])
@@ -294,20 +310,21 @@
     n_rows = hidden.shape[0]
     n_hid, width = weight.shape[-2:]
     adds = sums is not None
+    deep, pair_size = (6, 2) if width >= 512 else (4, 1)
     out_type = F32 if partial else BF16
     rows = n_rows if partial else n_rows // n_group
     return pl.pallas_call(
-        functools.partial(down_body, n_group, local, lo_hid, adds, partial),
+        functools.partial(down_body, n_group, local, lo_hid, adds, partial, deep, pair_size),
         in_specs=[smem()] + [any_spec()] * (2 + adds),
         out_specs=[any_spec()] * (1 if partial else n_group),
         scratch_shapes=[
-            pltpu.VMEM((DEEP, TILE, n_hid), BF16),
-            pltpu.VMEM((2, TILE, width), out_type),
+            pltpu.VMEM((deep, TILE, n_hid), BF16),
+            pltpu.VMEM((deep, TILE, width), out_type),
             pltpu.VMEM((n_hid, width), BF16),
-            pltpu.VMEM((DEEP, TILE, width) if adds else (DEEP, 8, 128), F32),
-            pltpu.SemaphoreType.DMA((DEEP,)),
-            pltpu.SemaphoreType.DMA((2,)),
-            pltpu.SemaphoreType.DMA((DEEP,)),
+            pltpu.VMEM((deep, TILE, width) if adds else (deep, 8, 128), F32),
+            pltpu.SemaphoreType.DMA((deep,)),
+            pltpu.SemaphoreType.DMA((deep,)),
+            pltpu.SemaphoreType.DMA((deep,)),
             pltpu.SemaphoreType.DMA,
         ],
         out_shape=[jax.ShapeDtypeStruct((rows, width), out_type)] * (1 if partial else n_group),
@@ -317,12 +334,13 @@
     )(meta, hidden, weight, *([sums] if adds else []))
 
 
-def mix_body(n_exp, n_tile, subs, widths, col_ref, chunk_ref, pos_ref, gate_ref, x_ref, *refs):
+def mix_body(n_exp, n_tile, subs, widths, unroll, col_ref, chunk_ref, pos_ref, gate_ref, x_ref, *refs):
     n_set = len(widths)
     back_refs = refs[: n_set * n_exp]
-    y_ref, mark_ref = refs[-3 - 4 * n_set : -1 - 4 * n_set]
-    bufs, sems = refs[-1 - 4 * n_set : -1], refs[-1]
-    sets, copies = [], []
+    y_ref, mark_ref, pos_buf, gate_buf = refs[-6 - 4 * n_set : -2 - 4 * n_set]
+    bufs, sems, y_sems = refs[-2 - 4 * n_set : -2], refs[-2], refs[-1]
+    sets = []
+    copies = [pltpu.make_async_copy(pos_ref, pos_buf, sems.at[0]), pltpu.make_async_copy(gate_ref, gate_buf, sems.at[1])]
     for g, width in enumerate(widths):
         back_buf, near_buf, x_buf, y_buf = bufs[4 * g : 4 * g + 4]
         cols = pl.ds(pl.multiple_of(col_ref[g], 128), width)
@@ -338,27 +356,32 @@
     for copy in copies:
         copy.wait()
 
+    def out(g, block):
+        _, _, _, y_buf, cols = sets[g]
+        rows = pl.ds(pl.multiple_of(block * (unroll * MIX_TILE), unroll * MIX_TILE), unroll * MIX_TILE)
+        return pltpu.make_async_copy(y_buf.at[rows, :], y_ref.at[rows, cols], y_sems.at[g, block])
+
     def step(block, carry):
-        for k in range(MIX_UNROLL):
-            i = block * MIX_UNROLL + k
+        for k in range(unroll):
+            i = block * unroll + k
             tokens = pl.ds(pl.multiple_of(i * MIX_TILE, MIX_TILE), MIX_TILE)
             seat = lax.broadcasted_iota(I32, (MIX_TILE, REACH), 1)
-            pick = jnp.concatenate([(seat == pos_ref[tokens, j : j + 1]).astype(F32).astype(BF16) for j in range(2)], axis=0)
+            pick = jnp.concatenate([(seat == pos_buf[tokens, j : j + 1]).astype(F32).astype(BF16) for j in range(2)], axis=0)
             for back_buf, near_buf, x_buf, y_buf, _ in sets:
                 for c in range(REACH // ALIGN):
                     chunk = pl.multiple_of(chunk_ref[i * (REACH // ALIGN) + c], ALIGN)
                     near_buf[k, c * ALIGN : (c + 1) * ALIGN, :] = back_buf[pl.ds(chunk, ALIGN), :]
                 found = jnp.dot(pick, near_buf[k], preferred_element_type=F32)
-                mixed = gate_ref[tokens, 0:1] * found[:MIX_TILE] + gate_ref[tokens, 1:2] * found[MIX_TILE:]
+                mixed = gate_buf[tokens, 0:1] * found[:MIX_TILE] + gate_buf[tokens, 1:2] * found[MIX_TILE:]
                 y_buf[tokens, :] = (x_buf[tokens, :].astype(F32) + mixed).astype(BF16)
+        for g in range(n_set):
+            out(g, block).start()
         return carry
 
-    lax.fori_loop(0, n_tile // MIX_UNROLL, step, 0)
-    outs = [pltpu.make_async_copy(y_buf, y_ref.at[:, cols], sems.at[g]) for g, (_, _, _, y_buf, cols) in enumerate(sets)]
-    for out in outs:
-        out.start()
-    for out in outs:
-        out.wait()
+    lax.fori_loop(0, n_tile // unroll, step, 0)
+    for block in range(n_tile // unroll):
+        for g in range(n_set):
+            out(g, block).wait()
     mark_ref[0] = 0
 
 
@@ -366,27 +389,31 @@
     tok_rows, d_model = x_loc.shape
     n_exp = len(back) // len(widths)
     capacity = back[0][0].shape[0]
-    vmem = pl.BlockSpec(memory_space=pltpu.VMEM)
+    unroll = 4 if sum(widths) < 512 else 2
     args = [col, chunks, pos, gate_loc, x_loc, *[array for array, _ in back]]
-    specs = [smem(), smem(), vmem, vmem, any_spec()] + [any_spec()] * len(back)
+    specs = [smem(), smem()] + [any_spec()] * (3 + len(back))
     alias = {}
     if y_loc is not None:
         alias = {len(args): 0}
         args.append(y_loc)
         specs.append(any_spec())
-    bufs = []
+    bufs = [pltpu.VMEM(pos.shape, I32), pltpu.VMEM(gate_loc.shape, F32)]
     for width in widths:
         bufs += [
             pltpu.VMEM((n_exp * capacity, width), BF16),
-            pltpu.VMEM((MIX_UNROLL, REACH, width), BF16),
+            pltpu.VMEM((unroll, REACH, width), BF16),
             pltpu.VMEM((tok_rows, width), BF16),
             pltpu.VMEM((tok_rows, width), BF16),
         ]
     return pl.pallas_call(
-        functools.partial(mix_body, n_exp, tok_rows // MIX_TILE, tuple(sub for _, sub in back), widths),
+        functools.partial(mix_body, n_exp, tok_rows // MIX_TILE, tuple(sub for _, sub in back), widths, unroll),
         in_specs=specs,
         out_specs=[any_spec(), smem()],
-        scratch_shapes=bufs + [pltpu.SemaphoreType.DMA(((n_exp + 1) * len(widths),))],
+        scratch_shapes=bufs
+        + [
+            pltpu.SemaphoreType.DMA((2 + (n_exp + 1) * len(widths),)),
+            pltpu.SemaphoreType.DMA((len(widths), tok_rows // MIX_TILE // unroll)),
+        ],
         out_shape=[jax.ShapeDtypeStruct((tok_rows, d_model), BF16), jax.ShapeDtypeStruct((1,), I32)],
         input_output_aliases=alias,
         compiler_params=pltpu.CompilerParams(vmem_limit_bytes=VMEM_LIMIT),

time: 1880 us -> 1870 us (level)
  transfers between devices with their start and end apart: 49 -> 49, of which waited for: 11 -> 12; matrix products, arithmetic and copies ran while one was open for 5% -> 5% of each run, Pallas kernels for 43% -> 43%
where the time goes in v4:
time: 1870 us
  Pallas kernels  847 us (45%)
  waiting for transfers between devices  735 us (39%)
  starting transfers between devices  166 us (9%)
  local copies, waits for them, and re-layouts  66.6 us (4%)
  other arithmetic  47.1 us (3%)
    ppermute x16, waiting for transfers between devices, cross(): far.append(lax.ppermute(piece, 'data', swap))  529 us
    pallas_call x8, Pallas kernels, wide_part(): pl.pallas_call(functools.partial(wide_body, n_group, local, lo_col, cols)...  440 us
    pallas_call x10, Pallas kernels, down_part(): pl.pallas_call(functools.partial(down_body, n_group, local, lo_hid, adds,...  254 us
    ppermute x33, waiting for transfers between devices, exchange(): lax.ppermute(blocks[d], 'expert', [(s, (s + step * d) % n_group) for s in...  205 us
    ppermute x33, starting transfers between devices, exchange(): lax.ppermute(blocks[d], 'expert', [(s, (s + step * d) % n_group) for s in...  152 us
    pallas_call x2, Pallas kernels, pack_rows(): pl.pallas_call(functools.partial(pack_body, n_local, local, n_blk, n_grou...  85.7 us
    pallas_call x4, Pallas kernels, mix_cols(): pl.pallas_call(functools.partial(mix_body, n_exp, tok_rows // MIX_TILE, t...  67.1 us
  transfers between devices with their start and end apart: 49, of which 12 were waited for; matrix products, arithmetic and copies ran while one was open for 5% of the time, Pallas kernels for 43%

profile of v4, /device:TPU:0, one launch (start us, length us, event | category | flops | bytes accessed | tf_op | source)
XLA Modules:
  0.0 1869.7 jit_solution(14763549686910447320)
XLA Ops:
  6.4 6.7 all-reduce
  17.1 40.4 %pack_rows.2 = (bf16[1280,2048]{1,0:T(8,128)(2,1)}, bf16[1280,2048]{1,0:T(8,128)(2,1)}, bf16[1280,2048]{1,0:T(8,128)(2,1)}, bf16[1280,2048]{1,0:T(8,128)(2,1)}) custom-call(s32[136]{0:T(256)} %reshape.314.first_ref, s32[8,4096]{1,0:T(8,128)} %get-tuple-element.198.slot_ref, bf16[4096,2048]{1,0:T(8,128)(2,1)} %x_ref.11), custom_call_target="tpu_custom_call" | custom-call | flops 20000000000 | bytes 60000000 | tf_op jit(solution)/shard_map/pack_rows/pallas_call | solution.py:93
  65.8 11.3 fusion.20
  77.2 6.3 pad_maximum_fusion.1
  84.8 17.7 fusion.18
  107.1 45.3 %pack_rows.3 = (bf16[1280,2048]{1,0:T(8,128)(2,1)}, bf16[1280,2048]{1,0:T(8,128)(2,1)}, bf16[1280,2048]{1,0:T(8,128)(2,1)}, bf16[1280,2048]{1,0:T(8,128)(2,1)}) custom-call(s32[136]{0:T(256)} %reshape.314.first_ref, s32[8,4096]{1,0:T(8,128)} %get-tuple-element.198.slot_ref, bf16[4096,2048]{1,0:T(8,128)(2,1)} %x_ref.11), custom_call_target="tpu_custom_call" | custom-call | flops 20000000000 | bytes 60000000 | tf_op jit(solution)/shard_map/pack_rows/pallas_call | solution.py:93
  164.6 6.2 pad_maximum_fusion
  196.2 6.9 slice_bitcast_fusion.2
  209.0 76.1 %collective-permute-done.2.refs_3_ = bf16[1280,2048]{1,0:T(8,128)(2,1)} collective-permute-done((bf16[1280,2048]{1,0:T(8,128)(2,1)}, bf16[1280,2048]{1,0:T(8,128)(2,1)}, u32[]{:S(2)}, u32[]{:S(2)}) %collective-permute-start.2) | collective-permute-done | bytes 5242912 | tf_op jit(solution)/shard_map/ppermute | solution.py:510
  287.7 22.1 %wide_part.8.refs_7_ = bf16[5120,5632]{1,0:T(8,128)(2,1)} custom-call(s32[6]{0:T(128)} %pad_add_fusion.6.meta_ref, bf16[1280,2048]{1,0:T(8,128)(2,1)} %get-tuple-element.90.refs_0_, bf16[1280,2048]{1,0:T(8,128)(2,1)} %collective-permute-done.refs_1_, bf16[1280,2048]{1,0:T(8,128)(2,1)} %collective-permute-done.1.refs_2_, ...), custom_call_target="tpu_custom_call" | custom-call | flops 21474836480 | bytes 20971520 | tf_op jit(solution)/shard_map/wide_part/pallas_call | solution.py:190
  309.8 118.7 %collective-permute-done.11.refs_6_ = bf16[2,1024,1536]{2,1,0:T(8,128)(2,1)} collective-permute-done((bf16[2,1024,1536]{2,1,0:T(8,128)(2,1)}, bf16[2,1024,1536]{2,1,0:T(8,128)(2,1)}, u32[]{:S(2)}, u32[]{:S(2)}) %collective-permute-start.11) | collective-permute-done | bytes 6291488 | tf_op jit(solution)/shard_map/ppermute | solution.py:505
  429.3 79.2 %wide_part.9.refs_7_ = bf16[5120,5632]{1,0:T(8,128)(2,1)} custom-call(s32[6]{0:T(128)} %pad_add_fusion.6.meta_ref, bf16[1280,2048]{1,0:T(8,128)(2,1)} %get-tuple-element.90.refs_0_, bf16[1280,2048]{1,0:T(8,128)(2,1)} %collective-permute-done.refs_1_, bf16[1280,2048]{1,0:T(8,128)(2,1)} %collective-permute-done.1.refs_2_, ...), custom_call_target="tpu_custom_call", output_to_operand_aliasing={{}: (8, {})} | custom-call | flops 85899345920 | bytes 20971520 | tf_op jit(solution)/shard_map/wide_part/pallas_call | solution.py:190
  508.5 97.9 %collective-permute-done.12.refs_6_ = bf16[2,1024,512]{2,1,0:T(8,128)(2,1)} collective-permute-done((bf16[2,1024,512]{2,1,0:T(8,128)(2,1)}, bf16[2,1024,512]{2,1,0:T(8,128)(2,1)}, u32[]{:S(2)}, u32[]{:S(2)}) %collective-permute-start.12) | collective-permute-done | bytes 2097184 | tf_op jit(solution)/shard_map/ppermute | solution.py:505
  607.2 59.5 %wide_part.10.refs_7_ = bf16[5120,5632]{1,0:T(8,128)(2,1)} custom-call(s32[6]{0:T(128)} %pad_add_fusion.6.meta_ref, bf16[1280,2048]{1,0:T(8,128)(2,1)} %get-tuple-element.90.refs_0_, bf16[1280,2048]{1,0:T(8,128)(2,1)} %collective-permute-done.refs_1_, bf16[1280,2048]{1,0:T(8,128)(2,1)} %collective-permute-done.1.refs_2_, ...), custom_call_target="tpu_custom_call", output_to_operand_aliasing={{}: (8, {})} | custom-call | flops 64424509440 | bytes 20971520 | tf_op jit(solution)/shard_map/wide_part/pallas_call | solution.py:190
  666.8 59.5 %wide_part.11.h_ref = bf16[5120,5632]{1,0:T(8,128)(2,1)} custom-call(s32[6]{0:T(128)} %pad_add_fusion.6.meta_ref, bf16[1280,2048]{1,0:T(8,128)(2,1)} %get-tuple-element.90.refs_0_, bf16[1280,2048]{1,0:T(8,128)(2,1)} %collective-permute-done.refs_1_, bf16[1280,2048]{1,0:T(8,128)(2,1)} %collective-permute-done.1.refs_2_, ...), custom_call_target="tpu_custom_call", output_to_operand_aliasing={{}: (8, {})} | custom-call | flops 64424509440 | bytes 20971520 | tf_op jit(solution)/shard_map/wide_part/pallas_call | solution.py:190
  726.3 18.7 %collective-permute-done.13.refs_6_ = bf16[2,1024,1536]{2,1,0:T(8,128)(2,1)} collective-permute-done((bf16[2,1024,1536]{2,1,0:T(8,128)(2,1)}, bf16[2,1024,1536]{2,1,0:T(8,128)(2,1)}, u32[]{:S(2)}, u32[]{:S(2)}) %collective-permute-start.13) | collective-permute-done | bytes 6291488 | tf_op jit(solution)/shard_map/ppermute | solution.py:505
  745.9 52.9 %down_part.10 = (bf16[1280,1024]{1,0:T(8,128)(2,1)}, bf16[1280,1024]{1,0:T(8,128)(2,1)}, bf16[1280,1024]{1,0:T(8,128)(2,1)}, bf16[1280,1024]{1,0:T(8,128)(2,1)}) custom-call(s32[6]{0:T(128)} %pad_add_fusion.6.meta_ref, bf16[5120,5632]{1,0:T(8,128)(2,1)} %wide_part.11.h_ref, bf16[2,5632,1024]{2,1,0:T(8,128)(2,1)} %w_ref.3), custom_call_target="tpu_custom_call" | custom-call | flops 59055800320 | bytes 57671680 | tf_op jit(solution)/shard_map/down_part/pallas_call | solution.py:316
  798.8 45.7 %collective-permute-start.16 = (bf16[1280,1024]{1,0:T(8,128)(2,1)}, bf16[1280,1024]{1,0:T(8,128)(2,1)}, u32[]{:S(2)}, u32[]{:S(2)}) collective-permute-start(bf16[1280,1024]{1,0:T(8,128)(2,1)} %get-tuple-element.122), channel_id=1, source_target_pairs={{0,3},{1,0},{2,1},{3,2},{4,7},{5,4},{6,5},{7,6}} | collective-permute-start | bytes 7864328 | tf_op jit(solution)/shard_map/ppermute | solution.py:510
  847.2 22.0 %wide_part.12.refs_7_ = bf16[5120,5632]{1,0:T(8,128)(2,1)} custom-call(s32[6]{0:T(128)} %pad_add_fusion.4.meta_ref, bf16[1280,2048]{1,0:T(8,128)(2,1)} %get-tuple-element.96.refs_0_, bf16[1280,2048]{1,0:T(8,128)(2,1)} %collective-permute-done.3.refs_1_, bf16[1280,2048]{1,0:T(8,128)(2,1)} %collective-permute-done.4.refs_2_, ...), custom_call_target="tpu_custom_call" | custom-call | flops 21474836480 | bytes 20971520 | tf_op jit(solution)/shard_map/wide_part/pallas_call | solution.py:190
  869.2 176.4 %collective-permute-done.14.w_ref = bf16[5632,512]{1,0:T(8,128)(2,1)} collective-permute-done((bf16[5632,512]{1,0:T(8,128)(2,1)}, bf16[5632,512]{1,0:T(8,128)(2,1)}, u32[]{:S(2)}, u32[]{:S(2)}) %collective-permute-start.14) | collective-permute-done | bytes 5767200 | tf_op jit(solution)/shard_map/ppermute | solution.py:505
  1047.7 79.0 %wide_part.13.refs_7_ = bf16[5120,5632]{1,0:T(8,128)(2,1)} custom-call(s32[6]{0:T(128)} %pad_add_fusion.4.meta_ref, bf16[1280,2048]{1,0:T(8,128)(2,1)} %get-tuple-element.96.refs_0_, bf16[1280,2048]{1,0:T(8,128)(2,1)} %collective-permute-done.3.refs_1_, bf16[1280,2048]{1,0:T(8,128)(2,1)} %collective-permute-done.4.refs_2_, ...), custom_call_target="tpu_custom_call", output_to_operand_aliasing={{}: (8, {})} | custom-call | flops 85899345920 | bytes 20971520 | tf_op jit(solution)/shard_map/wide_part/pallas_call | solution.py:190
  1127.7 59.5 %wide_part.14.refs_7_ = bf16[5120,5632]{1,0:T(8,128)(2,1)} custom-call(s32[6]{0:T(128)} %pad_add_fusion.4.meta_ref, bf16[1280,2048]{1,0:T(8,128)(2,1)} %get-tuple-element.96.refs_0_, bf16[1280,2048]{1,0:T(8,128)(2,1)} %collective-permute-done.3.refs_1_, bf16[1280,2048]{1,0:T(8,128)(2,1)} %collective-permute-done.4.refs_2_, ...), custom_call_target="tpu_custom_call", output_to_operand_aliasing={{}: (8, {})} | custom-call | flops 64424509440 | bytes 20971520 | tf_op jit(solution)/shard_map/wide_part/pallas_call | solution.py:190
  1187.2 117.7 %collective-permute-done.30.w_ref = bf16[5632,256]{1,0:T(8,128)(2,1)} collective-permute-done((bf16[5632,256]{1,0:T(8,128)(2,1)}, bf16[5632,256]{1,0:T(8,128)(2,1)}, u32[]{:S(2)}, u32[]{:S(2)}) %collective-permute-start.30) | collective-permute-done | bytes 2883616 | tf_op jit(solution)/shard_map/ppermute | solution.py:505
  1305.8 59.5 %wide_part.15.h_ref = bf16[5120,5632]{1,0:T(8,128)(2,1)} custom-call(s32[6]{0:T(128)} %pad_add_fusion.4.meta_ref, bf16[1280,2048]{1,0:T(8,128)(2,1)} %get-tuple-element.96.refs_0_, bf16[1280,2048]{1,0:T(8,128)(2,1)} %collective-permute-done.3.refs_1_, bf16[1280,2048]{1,0:T(8,128)(2,1)} %collective-permute-done.4.refs_2_, ...), custom_call_target="tpu_custom_call", output_to_operand_aliasing={{}: (8, {})} | custom-call | flops 64424509440 | bytes 20971520 | tf_op jit(solution)/shard_map/wide_part/pallas_call | solution.py:190
  1365.4 52.9 %down_part.11 = (bf16[1280,1024]{1,0:T(8,128)(2,1)}, bf16[1280,1024]{1,0:T(8,128)(2,1)}, bf16[1280,1024]{1,0:T(8,128)(2,1)}, bf16[1280,1024]{1,0:T(8,128)(2,1)}) custom-call(s32[6]{0:T(128)} %pad_add_fusion.4.meta_ref, bf16[5120,5632]{1,0:T(8,128)(2,1)} %wide_part.15.h_ref, bf16[2,5632,1024]{2,1,0:T(8,128)(2,1)} %w_ref.3), custom_call_target="tpu_custom_call" | custom-call | flops 59055800320 | bytes 57671680 | tf_op jit(solution)/shard_map/down_part/pallas_call | solution.py:316
  1418.3 29.0 %down_part.12 = (bf16[1280,512]{1,0:T(8,128)(2,1)}, bf16[1280,512]{1,0:T(8,128)(2,1)}, bf16[1280,512]{1,0:T(8,128)(2,1)}, bf16[1280,512]{1,0:T(8,128)(2,1)}) custom-call(s32[6]{0:T(128)} %pad_add_fusion.6.meta_ref, bf16[5120,5632]{1,0:T(8,128)(2,1)} %wide_part.11.h_ref, bf16[5632,512]{1,0:T(8,128)(2,1)} %collective-permute-done.14.w_ref), custom_call_target="tpu_custom_call" | custom-call | flops 29527900160 | bytes 57671680 | tf_op jit(solution)/shard_map/down_part/pallas_call | solution.py:316
  1447.3 50.2 %collective-permute-start.17 = (bf16[1280,1024]{1,0:T(8,128)(2,1)}, bf16[1280,1024]{1,0:T(8,128)(2,1)}, u32[]{:S(2)}, u32[]{:S(2)}) collective-permute-start(bf16[1280,1024]{1,0:T(8,128)(2,1)} %get-tuple-element.123), channel_id=1, source_target_pairs={{0,3},{1,0},{2,1},{3,2},{4,7},{5,4},{6,5},{7,6}} | collective-permute-start | bytes 7864328 | tf_op jit(solution)/shard_map/ppermute | solution.py:510
  1497.7 29.0 %down_part.13 = (bf16[1280,512]{1,0:T(8,128)(2,1)}, bf16[1280,512]{1,0:T(8,128)(2,1)}, bf16[1280,512]{1,0:T(8,128)(2,1)}, bf16[1280,512]{1,0:T(8,128)(2,1)}) custom-call(s32[6]{0:T(128)} %pad_add_fusion.4.meta_ref, bf16[5120,5632]{1,0:T(8,128)(2,1)} %wide_part.15.h_ref, bf16[5632,512]{1,0:T(8,128)(2,1)} %collective-permute-done.15.w_ref), custom_call_target="tpu_custom_call" | custom-call | flops 29527900160 | bytes 57671680 | tf_op jit(solution)/shard_map/down_part/pallas_call | solution.py:316
  1526.7 11.1 collective-permute-start.24
  1537.9 17.3 collective-permute-done.17.refs_3_
  1555.1 56.2 %collective-permute-done.19.refs_5_ = bf16[1280,1024]{1,0:T(8,128)(2,1)} collective-permute-done((bf16[1280,1024]{1,0:T(8,128)(2,1)}, bf16[1280,1024]{1,0:T(8,128)(2,1)}, u32[]{:S(2)}, u32[]{:S(2)}) %collective-permute-start.19) | collective-permute-done | bytes 2621472 | tf_op jit(solution)/shard_map/ppermute | solution.py:510
  1613.0 26.2 %mix_cols.4 = (bf16[4096,2048]{1,0:T(8,128)(2,1)}, s32[1]{0:T(128)}) custom-call(s32[1]{0:T(128)} %bitcast.13.col_ref, s32[1024]{0:T(1024)} %mul.74.chunk_ref, s32[4096,2]{1,0:T(8,128)} %copy.34.pos_ref, f32[4096,2]{1,0:T(8,128)} %copy.35.gate_ref, bf16[4096,2048]{1,0:T(8,128)(2,1)} %x_ref.11, bf16[1280,1024]{1,0:T(8,128)(2,1)} %get-tuple-element.112.refs_0_, ...), custom_call_target="tpu_custom_call" | custom-call | flops 20480000000 | bytes 20480000 | tf_op jit(solution)/shard_map/mix_cols/pallas_call | solution.py:408
  1640.5 17.0 down_part.14
  1658.3 7.1 collective-permute-start.27
  1665.6 17.0 down_part.15
  1683.1 6.8 collective-permute-start.34
  1695.6 28.1 %collective-permute-done.27.refs_5_ = bf16[1280,512]{1,0:T(8,128)(2,1)} collective-permute-done((bf16[1280,512]{1,0:T(8,128)(2,1)}, bf16[1280,512]{1,0:T(8,128)(2,1)}, u32[]{:S(2)}, u32[]{:S(2)}) %collective-permute-start.27) | collective-permute-done | bytes 1310752 | tf_op jit(solution)/shard_map/ppermute | solution.py:510
  1725.4 16.8 mix_cols.5
  1743.4 17.0 down_part.16
  1760.4 7.0 collective-permute-start.35
  1770.4 16.4 down_part.17
  1786.9 11.5 collective-permute-done.37.refs_5_
  1800.1 10.3 collective-permute-done.40.refs_10_.refs_2_
  1812.5 13.8 down_part.18.refs_0_
  1826.3 8.7 down_part.19
  1835.1 8.1 collective-permute-start.46
  1843.9 14.5 mix_cols.6
  1859.9 9.6 mix_cols.7
  (179 shorter events, 100.7 us)
Async XLA Ops:
  57.5 151.5 %collective-permute-start = (bf16[1280,2048]{1,0:T(8,128)(2,1)}, bf16[1280,2048]{1,0:T(8,128)(2,1)}, u32[]{:S(2)}, u32[]{:S(2)}) collective-permute-start(bf16[1280,2048]{1,0:T(8,128)(2,1)} %get-tuple-element.93), channel_id=1, source_target_pairs={{0,1},{1,2},{2,3},{3,0},{4,5},{5,6},{6,7},{7,4}} | collective-permute-start | bytes 15728648 | tf_op jit(solution)/shard_map/ppermute | solution.py:510
  57.5 151.5 %collective-permute-start.1 = (bf16[1280,2048]{1,0:T(8,128)(2,1)}, bf16[1280,2048]{1,0:T(8,128)(2,1)}, u32[]{:S(2)}, u32[]{:S(2)}) collective-permute-start(bf16[1280,2048]{1,0:T(8,128)(2,1)} %get-tuple-element.94), channel_id=1, source_target_pairs={{0,2},{1,3},{2,0},{3,1},{4,6},{5,7},{6,4},{7,5}} | collective-permute-start | bytes 15728648 | tf_op jit(solution)/shard_map/ppermute | solution.py:510
  59.5 225.5 %collective-permute-start.2 = (bf16[1280,2048]{1,0:T(8,128)(2,1)}, bf16[1280,2048]{1,0:T(8,128)(2,1)}, u32[]{:S(2)}, u32[]{:S(2)}) collective-permute-start(bf16[1280,2048]{1,0:T(8,128)(2,1)} %get-tuple-element.95), channel_id=1, source_target_pairs={{0,3},{1,0},{2,1},{3,2},{4,7},{5,4},{6,5},{7,6}} | collective-permute-start | bytes 15728648 | tf_op jit(solution)/shard_map/ppermute | solution.py:510
  65.1 127.7 %collective-permute-start.10 = (bf16[2,1024,512]{2,1,0:T(8,128)(2,1)}, bf16[2,1024,512]{2,1,0:T(8,128)(2,1)}, u32[]{:S(2)}, u32[]{:S(2)}) collective-permute-start(bf16[2,1024,512]{2,1,0:T(8,128)(2,1)} %pad_maximum_fusion.6), channel_id=1, source_target_pairs={{0,4},{4,0},{1,5},{5,1},{2,6},{6,2},{3,7},{7,3}} | collective-permute-start | bytes 6291464 | tf_op jit(solution)/shard_map/ppermute | solution.py:505
  83.5 226.3 %collective-permute-start.6 = (bf16[2,1024,2048]{2,1,0:T(8,128)(2,1)}, bf16[2,1024,2048]{2,1,0:T(8,128)(2,1)}, u32[]{:S(2)}, u32[]{:S(2)}) collective-permute-start(bf16[2,1024,2048]{2,1,0:T(8,128)(2,1)} %pad_maximum_fusion.1), channel_id=1, source_target_pairs={{0,4},{4,0},{1,5},{5,1},{2,6},{6,2},{3,7},{7,3}} | collective-permute-start | bytes 25165832 | tf_op jit(solution)/shard_map/ppermute | solution.py:505
  192.8 235.7 %collective-permute-start.11 = (bf16[2,1024,1536]{2,1,0:T(8,128)(2,1)}, bf16[2,1024,1536]{2,1,0:T(8,128)(2,1)}, u32[]{:S(2)}, u32[]{:S(2)}) collective-permute-start(bf16[2,1024,1536]{2,1,0:T(8,128)(2,1)} %pad_maximum_fusion.5), channel_id=1, source_target_pairs={{0,4},{4,0},{1,5},{5,1},{2,6},{6,2},{3,7},{7,3}} | collective-permute-start | bytes 18874376 | tf_op jit(solution)/shard_map/ppermute | solution.py:505
  285.1 513.8 %collective-permute-start.3 = (bf16[1280,2048]{1,0:T(8,128)(2,1)}, bf16[1280,2048]{1,0:T(8,128)(2,1)}, u32[]{:S(2)}, u32[]{:S(2)}) collective-permute-start(bf16[1280,2048]{1,0:T(8,128)(2,1)} %get-tuple-element.98), channel_id=1, source_target_pairs={{0,1},{1,2},{2,3},{3,0},{4,5},{5,6},{6,7},{7,4}} | collective-permute-start | bytes 15728648 | tf_op jit(solution)/shard_map/ppermute | solution.py:510
  285.6 558.9 %collective-permute-start.4 = (bf16[1280,2048]{1,0:T(8,128)(2,1)}, bf16[1280,2048]{1,0:T(8,128)(2,1)}, u32[]{:S(2)}, u32[]{:S(2)}) collective-permute-start(bf16[1280,2048]{1,0:T(8,128)(2,1)} %get-tuple-element.100), channel_id=1, source_target_pairs={{0,2},{1,3},{2,0},{3,1},{4,6},{5,7},{6,4},{7,5}} | collective-permute-start | bytes 15728648 | tf_op jit(solution)/shard_map/ppermute | solution.py:510
  287.7 559.4 %collective-permute-start.5 = (bf16[1280,2048]{1,0:T(8,128)(2,1)}, bf16[1280,2048]{1,0:T(8,128)(2,1)}, u32[]{:S(2)}, u32[]{:S(2)}) collective-permute-start(bf16[1280,2048]{1,0:T(8,128)(2,1)} %get-tuple-element.102), channel_id=1, source_target_pairs={{0,3},{1,0},{2,1},{3,2},{4,7},{5,4},{6,5},{7,6}} | collective-permute-start | bytes 15728648 | tf_op jit(solution)/shard_map/ppermute | solution.py:510
  309.8 357.0 %collective-permute-start.7 = (bf16[2,1024,1536]{2,1,0:T(8,128)(2,1)}, bf16[2,1024,1536]{2,1,0:T(8,128)(2,1)}, u32[]{:S(2)}, u32[]{:S(2)}) collective-permute-start(bf16[2,1024,1536]{2,1,0:T(8,128)(2,1)} %pad_maximum_fusion.3), channel_id=1, source_target_pairs={{0,4},{4,0},{1,5},{5,1},{2,6},{6,2},{3,7},{7,3}} | collective-permute-start | bytes 18874376 | tf_op jit(solution)/shard_map/ppermute | solution.py:505
  428.5 177.8 %collective-permute-start.12 = (bf16[2,1024,512]{2,1,0:T(8,128)(2,1)}, bf16[2,1024,512]{2,1,0:T(8,128)(2,1)}, u32[]{:S(2)}, u32[]{:S(2)}) collective-permute-start(bf16[2,1024,512]{2,1,0:T(8,128)(2,1)} %pad_maximum_fusion.7), channel_id=1, source_target_pairs={{0,4},{4,0},{1,5},{5,1},{2,6},{6,2},{3,7},{7,3}} | collective-permute-start | bytes 6291464 | tf_op jit(solution)/shard_map/ppermute | solution.py:505
  606.4 138.7 %collective-permute-start.13 = (bf16[2,1024,1536]{2,1,0:T(8,128)(2,1)}, bf16[2,1024,1536]{2,1,0:T(8,128)(2,1)}, u32[]{:S(2)}, u32[]{:S(2)}) collective-permute-start(bf16[2,1024,1536]{2,1,0:T(8,128)(2,1)} %pad_maximum_fusion.4), channel_id=1, source_target_pairs={{0,4},{4,0},{1,5},{5,1},{2,6},{6,2},{3,7},{7,3}} | collective-permute-start | bytes 18874376 | tf_op jit(solution)/shard_map/ppermute | solution.py:505
  666.7 379.8 %collective-permute-start.8 = (bf16[2,1024,2048]{2,1,0:T(8,128)(2,1)}, bf16[2,1024,2048]{2,1,0:T(8,128)(2,1)}, u32[]{:S(2)}, u32[]{:S(2)}) collective-permute-start(bf16[2,1024,2048]{2,1,0:T(8,128)(2,1)} %pad_maximum_fusion), channel_id=1, source_target_pairs={{0,4},{4,0},{1,5},{5,1},{2,6},{6,2},{3,7},{7,3}} | collective-permute-start | bytes 25165832 | tf_op jit(solution)/shard_map/ppermute | solution.py:505
  745.0 300.6 %collective-permute-start.14 = (bf16[5632,512]{1,0:T(8,128)(2,1)}, bf16[5632,512]{1,0:T(8,128)(2,1)}, u32[]{:S(2)}, u32[]{:S(2)}) collective-permute-start(bf16[5632,512]{1,0:T(8,128)(2,1)} %get-tuple-element.116), channel_id=1, source_target_pairs={{0,4},{4,0},{1,5},{5,1},{2,6},{6,2},{3,7},{7,3}} | collective-permute-start | bytes 17301512 | tf_op jit(solution)/shard_map/ppermute | solution.py:505
  798.8 698.7 %collective-permute-start.16 = (bf16[1280,1024]{1,0:T(8,128)(2,1)}, bf16[1280,1024]{1,0:T(8,128)(2,1)}, u32[]{:S(2)}, u32[]{:S(2)}) collective-permute-start(bf16[1280,1024]{1,0:T(8,128)(2,1)} %get-tuple-element.122), channel_id=1, source_target_pairs={{0,3},{1,0},{2,1},{3,2},{4,7},{5,4},{6,5},{7,6}} | collective-permute-start | bytes 7864328 | tf_op jit(solution)/shard_map/ppermute | solution.py:510
  844.5 682.2 %collective-permute-start.18 = (bf16[1280,1024]{1,0:T(8,128)(2,1)}, bf16[1280,1024]{1,0:T(8,128)(2,1)}, u32[]{:S(2)}, u32[]{:S(2)}) collective-permute-start(bf16[1280,1024]{1,0:T(8,128)(2,1)} %get-tuple-element.124), channel_id=1, source_target_pairs={{0,2},{1,3},{2,0},{3,1},{4,6},{5,7},{6,4},{7,5}} | collective-permute-start | bytes 7864328 | tf_op jit(solution)/shard_map/ppermute | solution.py:510
  847.0 690.8 %collective-permute-start.20 = (bf16[1280,1024]{1,0:T(8,128)(2,1)}, bf16[1280,1024]{1,0:T(8,128)(2,1)}, u32[]{:S(2)}, u32[]{:S(2)}) collective-permute-start(bf16[1280,1024]{1,0:T(8,128)(2,1)} %get-tuple-element.126), channel_id=1, source_target_pairs={{0,1},{1,2},{2,3},{3,0},{4,5},{5,6},{6,7},{7,4}} | collective-permute-start | bytes 7864328 | tf_op jit(solution)/shard_map/ppermute | solution.py:510
  1045.6 81.1 %collective-permute-start.22 = (bf16[5632,256]{1,0:T(8,128)(2,1)}, bf16[5632,256]{1,0:T(8,128)(2,1)}, u32[]{:S(2)}, u32[]{:S(2)}) collective-permute-start(bf16[5632,256]{1,0:T(8,128)(2,1)} %get-tuple-element.129), channel_id=1, source_target_pairs={{0,4},{4,0},{1,5},{5,1},{2,6},{6,2},{3,7},{7,3}} | collective-permute-start | bytes 8650760 | tf_op jit(solution)/shard_map/ppermute | solution.py:505
  1046.6 258.3 %collective-permute-start.9 = (bf16[2,1024,1536]{2,1,0:T(8,128)(2,1)}, bf16[2,1024,1536]{2,1,0:T(8,128)(2,1)}, u32[]{:S(2)}, u32[]{:S(2)}) collective-permute-start(bf16[2,1024,1536]{2,1,0:T(8,128)(2,1)} %pad_maximum_fusion.2), channel_id=1, source_target_pairs={{0,4},{4,0},{1,5},{5,1},{2,6},{6,2},{3,7},{7,3}} | collective-permute-start | bytes 18874376 | tf_op jit(solution)/shard_map/ppermute | solution.py:505
  1126.7 178.2 %collective-permute-start.30 = (bf16[5632,256]{1,0:T(8,128)(2,1)}, bf16[5632,256]{1,0:T(8,128)(2,1)}, u32[]{:S(2)}, u32[]{:S(2)}) collective-permute-start(bf16[5632,256]{1,0:T(8,128)(2,1)} %get-tuple-element.143), channel_id=1, source_target_pairs={{0,4},{4,0},{1,5},{5,1},{2,6},{6,2},{3,7},{7,3}} | collective-permute-start | bytes 8650760 | tf_op jit(solution)/shard_map/ppermute | solution.py:505
  1304.9 192.7 %collective-permute-start.15 = (bf16[5632,512]{1,0:T(8,128)(2,1)}, bf16[5632,512]{1,0:T(8,128)(2,1)}, u32[]{:S(2)}, u32[]{:S(2)}) collective-permute-start(bf16[5632,512]{1,0:T(8,128)(2,1)} %get-tuple-element.119), channel_id=1, source_target_pairs={{0,4},{4,0},{1,5},{5,1},{2,6},{6,2},{3,7},{7,3}} | collective-permute-start | bytes 17301512 | tf_op jit(solution)/shard_map/ppermute | solution.py:505
  1447.3 107.8 %collective-permute-start.17 = (bf16[1280,1024]{1,0:T(8,128)(2,1)}, bf16[1280,1024]{1,0:T(8,128)(2,1)}, u32[]{:S(2)}, u32[]{:S(2)}) collective-permute-start(bf16[1280,1024]{1,0:T(8,128)(2,1)} %get-tuple-element.123), channel_id=1, source_target_pairs={{0,3},{1,0},{2,1},{3,2},{4,7},{5,4},{6,5},{7,6}} | collective-permute-start | bytes 7864328 | tf_op jit(solution)/shard_map/ppermute | solution.py:510
  1497.5 113.7 %collective-permute-start.19 = (bf16[1280,1024]{1,0:T(8,128)(2,1)}, bf16[1280,1024]{1,0:T(8,128)(2,1)}, u32[]{:S(2)}, u32[]{:S(2)}) collective-permute-start(bf16[1280,1024]{1,0:T(8,128)(2,1)} %get-tuple-element.125), channel_id=1, source_target_pairs={{0,2},{1,3},{2,0},{3,1},{4,6},{5,7},{6,4},{7,5}} | collective-permute-start | bytes 7864328 | tf_op jit(solution)/shard_map/ppermute | solution.py:510
  1497.6 115.5 %collective-permute-start.21 = (bf16[1280,1024]{1,0:T(8,128)(2,1)}, bf16[1280,1024]{1,0:T(8,128)(2,1)}, u32[]{:S(2)}, u32[]{:S(2)}) collective-permute-start(bf16[1280,1024]{1,0:T(8,128)(2,1)} %get-tuple-element.127), channel_id=1, source_target_pairs={{0,1},{1,2},{2,3},{3,0},{4,5},{5,6},{6,7},{7,4}} | collective-permute-start | bytes 7864328 | tf_op jit(solution)/shard_map/ppermute | solution.py:510
  1526.7 131.6 %collective-permute-start.24 = (bf16[1280,512]{1,0:T(8,128)(2,1)}, bf16[1280,512]{1,0:T(8,128)(2,1)}, u32[]{:S(2)}, u32[]{:S(2)}) collective-permute-start(bf16[1280,512]{1,0:T(8,128)(2,1)} %get-tuple-element.135), channel_id=1, source_target_pairs={{0,3},{1,0},{2,1},{3,2},{4,7},{5,4},{6,5},{7,6}} | collective-permute-start | bytes 3932168 | tf_op jit(solution)/shard_map/ppermute | solution.py:510
  1537.9 144.7 %collective-permute-start.26 = (bf16[1280,512]{1,0:T(8,128)(2,1)}, bf16[1280,512]{1,0:T(8,128)(2,1)}, u32[]{:S(2)}, u32[]{:S(2)}) collective-permute-start(bf16[1280,512]{1,0:T(8,128)(2,1)} %get-tuple-element.137), channel_id=1, source_target_pairs={{0,2},{1,3},{2,0},{3,1},{4,6},{5,7},{6,4},{7,5}} | collective-permute-start | bytes 3932168 | tf_op jit(solution)/shard_map/ppermute | solution.py:510
  1555.1 127.9 %collective-permute-start.28 = (bf16[1280,512]{1,0:T(8,128)(2,1)}, bf16[1280,512]{1,0:T(8,128)(2,1)}, u32[]{:S(2)}, u32[]{:S(2)}) collective-permute-start(bf16[1280,512]{1,0:T(8,128)(2,1)} %get-tuple-element.139), channel_id=1, source_target_pairs={{0,1},{1,2},{2,3},{3,0},{4,5},{5,6},{6,7},{7,4}} | collective-permute-start | bytes 3932168 | tf_op jit(solution)/shard_map/ppermute | solution.py:510
  1611.3 54.1 %collective-permute-start.23 = (bf16[5632,256]{1,0:T(8,128)(2,1)}, bf16[5632,256]{1,0:T(8,128)(2,1)}, u32[]{:S(2)}, u32[]{:S(2)}) collective-permute-start(bf16[5632,256]{1,0:T(8,128)(2,1)} %get-tuple-element.132), channel_id=1, source_target_pairs={{0,4},{4,0},{1,5},{5,1},{2,6},{6,2},{3,7},{7,3}} | collective-permute-start | bytes 8650760 | tf_op jit(solution)/shard_map/ppermute | solution.py:505
  1657.5 38.1 %collective-permute-start.25 = (bf16[1280,512]{1,0:T(8,128)(2,1)}, bf16[1280,512]{1,0:T(8,128)(2,1)}, u32[]{:S(2)}, u32[]{:S(2)}) collective-permute-start(bf16[1280,512]{1,0:T(8,128)(2,1)} %get-tuple-element.136), channel_id=1, source_target_pairs={{0,3},{1,0},{2,1},{3,2},{4,7},{5,4},{6,5},{7,6}} | collective-permute-start | bytes 3932168 | tf_op jit(solution)/shard_map/ppermute | solution.py:510
  1658.3 65.3 %collective-permute-start.27 = (bf16[1280,512]{1,0:T(8,128)(2,1)}, bf16[1280,512]{1,0:T(8,128)(2,1)}, u32[]{:S(2)}, u32[]{:S(2)}) collective-permute-start(bf16[1280,512]{1,0:T(8,128)(2,1)} %get-tuple-element.138), channel_id=1, source_target_pairs={{0,2},{1,3},{2,0},{3,1},{4,6},{5,7},{6,4},{7,5}} | collective-permute-start | bytes 3932168 | tf_op jit(solution)/shard_map/ppermute | solution.py:510
  1665.4 58.2 %collective-permute-start.29 = (bf16[1280,512]{1,0:T(8,128)(2,1)}, bf16[1280,512]{1,0:T(8,128)(2,1)}, u32[]{:S(2)}, u32[]{:S(2)}) collective-permute-start(bf16[1280,512]{1,0:T(8,128)(2,1)} %get-tuple-element.140), channel_id=1, source_target_pairs={{0,1},{1,2},{2,3},{3,0},{4,5},{5,6},{6,7},{7,4}} | collective-permute-start | bytes 3932168 | tf_op jit(solution)/shard_map/ppermute | solution.py:510
  1682.6 84.8 %collective-permute-start.32 = (bf16[4096,128]{1,0:T(8,128)(2,1)}, bf16[4096,128]{1,0:T(8,128)(2,1)}, u32[]{:S(2)}, u32[]{:S(2)}) collective-permute-start(bf16[4096,128]{1,0:T(8,128)(2,1)} %slice_bitcast_fusion.6), channel_id=1, source_target_pairs={{0,4},{4,0},{1,5},{5,1},{2,6},{6,2},{3,7},{7,3}} | collective-permute-start | bytes 3145736 | tf_op jit(solution)/shard_map/ppermute | solution.py:505
  1683.1 85.4 %collective-permute-start.34 = (bf16[1280,256]{1,0:T(8,128)(2,1)}, bf16[1280,256]{1,0:T(8,128)(2,1)S(1)}, u32[]{:S(2)}, u32[]{:S(2)}) collective-permute-start(bf16[1280,256]{1,0:T(8,128)(2,1)} %get-tuple-element.154), channel_id=1, source_target_pairs={{0,3},{1,0},{2,1},{3,2},{4,7},{5,4},{6,5},{7,6}} | collective-permute-start | bytes 1966088 | tf_op jit(solution)/shard_map/ppermute | solution.py:510
  1695.6 73.1 %collective-permute-start.36 = (bf16[1280,256]{1,0:T(8,128)(2,1)}, bf16[1280,256]{1,0:T(8,128)(2,1)}, u32[]{:S(2)}, u32[]{:S(2)}) collective-permute-start(bf16[1280,256]{1,0:T(8,128)(2,1)} %get-tuple-element.156), channel_id=1, source_target_pairs={{0,2},{1,3},{2,0},{3,1},{4,6},{5,7},{6,4},{7,5}} | collective-permute-start | bytes 1966088 | tf_op jit(solution)/shard_map/ppermute | solution.py:510
  1723.6 46.6 %collective-permute-start.38 = (bf16[1280,256]{1,0:T(8,128)(2,1)}, bf16[1280,256]{1,0:T(8,128)(2,1)}, u32[]{:S(2)}, u32[]{:S(2)}) collective-permute-start(bf16[1280,256]{1,0:T(8,128)(2,1)} %get-tuple-element.158), channel_id=1, source_target_pairs={{0,1},{1,2},{2,3},{3,0},{4,5},{5,6},{6,7},{7,4}} | collective-permute-start | bytes 1966088 | tf_op jit(solution)/shard_map/ppermute | solution.py:510
  1723.6 36.7 %collective-permute-start.31 = (bf16[5632,128]{1,0:T(8,128)(2,1)}, bf16[5632,128]{1,0:T(8,128)(2,1)}, u32[]{:S(2)}, u32[]{:S(2)}) collective-permute-start(bf16[5632,128]{1,0:T(8,128)(2,1)} %slice_bitcast_fusion.5), channel_id=1, source_target_pairs={{0,4},{4,0},{1,5},{5,1},{2,6},{6,2},{3,7},{7,3}} | collective-permute-start | bytes 4325384 | tf_op jit(solution)/shard_map/ppermute | solution.py:505
  1760.4 26.5 %collective-permute-start.35 = (bf16[1280,256]{1,0:T(8,128)(2,1)}, bf16[1280,256]{1,0:T(8,128)(2,1)}, u32[]{:S(2)}, u32[]{:S(2)}) collective-permute-start(bf16[1280,256]{1,0:T(8,128)(2,1)} %get-tuple-element.155), channel_id=1, source_target_pairs={{0,3},{1,0},{2,1},{3,2},{4,7},{5,4},{6,5},{7,6}} | collective-permute-start | bytes 1966088 | tf_op jit(solution)/shard_map/ppermute | solution.py:510
  1767.4 31.0 %collective-permute-start.37 = (bf16[1280,256]{1,0:T(8,128)(2,1)}, bf16[1280,256]{1,0:T(8,128)(2,1)}, u32[]{:S(2)}, u32[]{:S(2)}) collective-permute-start(bf16[1280,256]{1,0:T(8,128)(2,1)} %get-tuple-element.157), channel_id=1, source_target_pairs={{0,2},{1,3},{2,0},{3,1},{4,6},{5,7},{6,4},{7,5}} | collective-permute-start | bytes 1966088 | tf_op jit(solution)/shard_map/ppermute | solution.py:510
  1768.4 29.9 %collective-permute-start.39 = (bf16[1280,256]{1,0:T(8,128)(2,1)}, bf16[1280,256]{1,0:T(8,128)(2,1)}, u32[]{:S(2)}, u32[]{:S(2)}) collective-permute-start(bf16[1280,256]{1,0:T(8,128)(2,1)} %get-tuple-element.159), channel_id=1, source_target_pairs={{0,1},{1,2},{2,3},{3,0},{4,5},{5,6},{6,7},{7,4}} | collective-permute-start | bytes 1966088 | tf_op jit(solution)/shard_map/ppermute | solution.py:510
  1769.3 41.1 %collective-permute-start.40 = (bf16[1280,256]{1,0:T(8,128)(2,1)}, bf16[1280,256]{1,0:T(8,128)(2,1)S(1)}, u32[]{:S(2)}, u32[]{:S(2)}) collective-permute-start(bf16[1280,256]{1,0:T(8,128)(2,1)} %get-tuple-element.160), channel_id=1, source_target_pairs={{0,3},{1,0},{2,1},{3,2},{4,7},{5,4},{6,5},{7,6}} | collective-permute-start | bytes 1966088 | tf_op jit(solution)/shard_map/ppermute | solution.py:510
  1770.2 41.7 %collective-permute-start.33 = (bf16[1536,128]{1,0:T(8,128)(2,1)}, bf16[1536,128]{1,0:T(8,128)(2,1)}, u32[]{:S(2)}, u32[]{:S(2)}) collective-permute-start(bf16[1536,128]{1,0:T(8,128)(2,1)} %slice_bitcast_fusion.7), channel_id=1, source_target_pairs={{0,4},{4,0},{1,5},{5,1},{2,6},{6,2},{3,7},{7,3}} | collective-permute-start | bytes 1179656 | tf_op jit(solution)/shard_map/ppermute | solution.py:505
  1786.8 48.2 %collective-permute-start.42 = (bf16[1280,256]{1,0:T(8,128)(2,1)}, bf16[1280,256]{1,0:T(8,128)(2,1)}, u32[]{:S(2)}, u32[]{:S(2)}) collective-permute-start(bf16[1280,256]{1,0:T(8,128)(2,1)} %get-tuple-element.162), channel_id=1, source_target_pairs={{0,2},{1,3},{2,0},{3,1},{4,6},{5,7},{6,4},{7,5}} | collective-permute-start | bytes 1966088 | tf_op jit(solution)/shard_map/ppermute | solution.py:510
  1798.3 44.8 %collective-permute-start.44 = (bf16[1280,256]{1,0:T(8,128)(2,1)}, bf16[1280,256]{1,0:T(8,128)(2,1)}, u32[]{:S(2)}, u32[]{:S(2)}) collective-permute-start(bf16[1280,256]{1,0:T(8,128)(2,1)} %get-tuple-element.164), channel_id=1, source_target_pairs={{0,1},{1,2},{2,3},{3,0},{4,5},{5,6},{6,7},{7,4}} | collective-permute-start | bytes 1966088 | tf_op jit(solution)/shard_map/ppermute | solution.py:510
  1798.3 44.8 %collective-permute-start.41 = (bf16[1280,128]{1,0:T(8,128)(2,1)}, bf16[1280,128]{1,0:T(8,128)(2,1)S(1)}, u32[]{:S(2)}, u32[]{:S(2)}) collective-permute-start(bf16[1280,128]{1,0:T(8,128)(2,1)} %get-tuple-element.161), channel_id=1, source_target_pairs={{0,3},{1,0},{2,1},{3,2},{4,7},{5,4},{6,5},{7,6}} | collective-permute-start | bytes 983048 | tf_op jit(solution)/shard_map/ppermute | solution.py:510
  1810.3 33.0 %collective-permute-start.43 = (bf16[1280,128]{1,0:T(8,128)(2,1)}, bf16[1280,128]{1,0:T(8,128)(2,1)}, u32[]{:S(2)}, u32[]{:S(2)}) collective-permute-start(bf16[1280,128]{1,0:T(8,128)(2,1)} %get-tuple-element.163), channel_id=1, source_target_pairs={{0,2},{1,3},{2,0},{3,1},{4,6},{5,7},{6,4},{7,5}} | collective-permute-start | bytes 983048 | tf_op jit(solution)/shard_map/ppermute | solution.py:510
  1811.9 31.4 %collective-permute-start.45 = (bf16[1280,128]{1,0:T(8,128)(2,1)}, bf16[1280,128]{1,0:T(8,128)(2,1)}, u32[]{:S(2)}, u32[]{:S(2)}) collective-permute-start(bf16[1280,128]{1,0:T(8,128)(2,1)} %get-tuple-element.165), channel_id=1, source_target_pairs={{0,1},{1,2},{2,3},{3,0},{4,5},{5,6},{6,7},{7,4}} | collective-permute-start | bytes 983048 | tf_op jit(solution)/shard_map/ppermute | solution.py:510
  1835.1 24.0 %collective-permute-start.46 = (bf16[1280,128]{1,0:T(8,128)(2,1)}, bf16[1280,128]{1,0:T(8,128)(2,1)S(1)}, u32[]{:S(2)}, u32[]{:S(2)}) collective-permute-start(bf16[1280,128]{1,0:T(8,128)(2,1)} %get-tuple-element.168), channel_id=1, source_target_pairs={{0,3},{1,0},{2,1},{3,2},{4,7},{5,4},{6,5},{7,6}} | collective-permute-start | bytes 983048 | tf_op jit(solution)/shard_map/ppermute | solution.py:510
  1843.2 15.9 collective-permute-start.48
  (21 other events, 308.8 us)
